TPU v7x, 128 devices: a whole 4x4x4 slice. The times are simulated.
128 devices in a mesh: grp: 4 (over z), wave: 32 (over x, y, core).
Axes of the slice: x: 4, y: 4, z: 4, core: 2. Of those that a mesh axis runs over, the one named last changes fastest.
Arguments:
- state: bfloat16 [275, 984320], P(None, ('grp', 'wave')), may hold values from -6 to 6
- held_orders: int32 [640], P(('grp', 'wave')), may hold values from -1 to 383, as said below
- pair_lows: int32 [384], P(('grp', 'wave')), may hold values from 0 to 383, each once
- inverses: bfloat16 [384, 2, 137, 137], P(('grp', 'wave')), may hold values from -2 to 3
- height_operator: bfloat16 [137, 137], replicated, may hold values from -0.5 to 0.5
- pressure_column: bfloat16 [137], replicated, may hold values from -5 to 5
- thermal_response_matrix: bfloat16 [137, 137], replicated, may hold values from -0.5 to 0.5
- mass_row: bfloat16 [137], replicated, may hold values from -0.5 to 0.5
Outputs:
- advanced: bfloat16 [275, 984320], P(None, ('grp', 'wave'))
Inputs may be any that keep to these rules, and one draw needn't show every extreme that they name: `held_orders`: each of 0 to 383 appears exactly once, all other entries are -1; some device has all 5 of its slots filled.
All inputs are finite; a program needn't handle non-finite values.
Results may differ from a plain program's by a relative error of at most 0.0052.
Values may be sent and summed in bfloat16 or wider, within the bound.
No kernel may reach another device: no remote copies, remote signals or barrier semaphores. Data moves between devices by JAX's collectives and lax.ppermute only.
A program may use at most 128 MiB of HBM per device.

v0:
```python
import jax
import jax.numpy as jnp
from jax import lax
from jax.sharding import Mesh
from jax.sharding import PartitionSpec as P

GRP_WAVE = ("grp", "wave_0", "wave_1", "wave_2")
WAVE = ("wave_0", "wave_1", "wave_2")


def in_order(tiles, dim):
    shape = list(tiles.shape[1:])
    shape[dim] *= tiles.shape[0]
    return jnp.moveaxis(tiles, 0, dim).reshape(shape)


def all_blocks(shard, axes, turns):
    tiles = shard[None]
    for k in turns:
        tiles = lax.all_gather(tiles, axes[k], axis=0, tiled=True)
    held = [lax.axis_size(axes[k]) for k in reversed(turns)]
    tiles = tiles.reshape(*held, *shard.shape)
    turned = sorted(range(len(turns)), key=lambda place: turns[len(turns) - 1 - place])
    return tiles.transpose(*turned, *range(len(turns), tiles.ndim)).reshape(-1, *shard.shape)


def gathered_by_axis(shard, axes, turns, dim):
    return in_order(all_blocks(shard, axes, turns), dim)


def send_out(message):
    return lax.all_to_all(message, GRP_WAVE, split_axis=1, concat_axis=1, tiled=True)


def send_home(message):
    return lax.all_to_all(message, GRP_WAVE, split_axis=1, concat_axis=1, tiled=True)


def solve_columns(inverses, right_side, low_mask, split):
    upper = jnp.einsum(
        "jkl,lajc->kajc", inverses[:, 1], right_side, preferred_element_type=jnp.float32
    )
    lower = jnp.einsum(
        "jkl,lajc->kajc",
        inverses[:, 0],
        right_side[..., :split],
        preferred_element_type=jnp.float32,
    )
    first = jnp.where(low_mask[None, :, :, :split], lower, upper[..., :split])
    return jnp.concatenate([first, upper[..., split:]], axis=-1).astype(jnp.bfloat16)


def shards(
    state,
    held_orders,
    pair_lows,
    inverses,
    height_operator,
    pressure_column,
    thermal_response_matrix,
    mass_row,
):
    layer_heights_count = height_operator.shape[0]
    pair_count = pair_lows.shape[0]
    slot_count = held_orders.shape[0]
    devices = lax.axis_size("grp") * lax.axis_size(WAVE)
    truncation = 2 * pair_count * devices - 1
    slot_width = 2 * (truncation + 2)
    denom = float(truncation * (truncation + 1))
    fill_col = slot_count * slot_width
    all_lows = gathered_by_axis(pair_lows, (("grp", "wave_0", "wave_1"), "wave_2"), (0, 1), 0)
    own_low = pair_lows.reshape(1, pair_count, 1)
    all_orders = gathered_by_axis(held_orders, GRP_WAVE, (0, 1, 2, 3), 0)
    low_grid = all_lows.reshape(devices, pair_count, 1, 1)
    orders = held_orders.reshape(1, 1, slot_count, 1)
    halves = jnp.arange(2, dtype=jnp.int32).reshape(1, 1, 1, 2)
    slot_ids = jnp.arange(slot_count, dtype=jnp.int32).reshape(1, 1, slot_count, 1)
    live = orders >= 0

    def place(position):
        spot = slot_ids * slot_width + 2 * position + halves
        return jnp.where(live, spot, fill_col).reshape(devices, pair_count, -1)

    first = place(jnp.where(orders <= low_grid, low_grid - orders, truncation + 1 - low_grid))
    second = place(truncation - low_grid - orders)
    hit = orders == low_grid
    found = jnp.any(hit, axis=2)
    slot_hit = jnp.sum(jnp.where(hit, slot_ids, 0), axis=2)
    extra = slot_hit * slot_width + 2 * (truncation + 1 - low_grid[:, :, 0]) + halves[:, :, 0]
    extra = jnp.where(found, extra, fill_col)
    column = jnp.concatenate([first, second, extra], axis=2).reshape(-1)
    source_orders = all_orders.reshape(devices, 1, slot_count, 1)
    low_first = jnp.broadcast_to(
        source_orders <= own_low[..., None], (devices, pair_count, slot_count, 2)
    ).reshape(devices, pair_count, -1)
    low_mask = jnp.concatenate(
        [low_first, jnp.zeros((devices, pair_count, 2 * slot_count + 2), jnp.bool_)], axis=2
    )
    split = 2 * slot_count
    per_pair = low_mask.shape[2]
    recv_shape = (devices, pair_count, per_pair)
    divergence = state[:layer_heights_count]
    thermal_state_array = state[layer_heights_count : 2 * layer_heights_count]
    pressure = state[2 * layer_heights_count]
    coeff_index = (jnp.arange(slot_width, dtype=jnp.int32) // 2)[None, :]
    order_col = held_orders[:, None]
    degree = jnp.where(
        coeff_index <= truncation - order_col, order_col + coeff_index, coeff_index - 1
    )
    lap_scale = ((degree * (degree + 1)).astype(jnp.float32) / denom).reshape(-1)
    height_drive_term = jnp.dot(
        height_operator, thermal_state_array, preferred_element_type=jnp.float32
    )
    height_drive_term = (
        height_drive_term
        + pressure_column.astype(jnp.float32)[:, None] * pressure.astype(jnp.float32)[None, :]
    )
    right_side = (divergence.astype(jnp.float32) + lap_scale[None, :] * height_drive_term).astype(
        jnp.bfloat16
    )
    message = jnp.take(right_side, column, axis=1, mode="fill", fill_value=0)
    arriving_arrays = send_out(message).reshape((layer_heights_count,) + recv_shape)
    div_sent = solve_columns(inverses, arriving_arrays, low_mask, split).reshape(
        layer_heights_count, -1
    )
    returned = send_home(div_sent)
    next_spreading_rate = (
        jnp.zeros((layer_heights_count, fill_col), jnp.bfloat16)
        .at[:, column]
        .set(returned, mode="drop")
    )
    next_thermal_state = (
        thermal_state_array.astype(jnp.float32)
        - jnp.dot(thermal_response_matrix, next_spreading_rate, preferred_element_type=jnp.float32)
    ).astype(jnp.bfloat16)
    surface_mass_next = (
        pressure.astype(jnp.float32)
        - jnp.dot(mass_row, next_spreading_rate, preferred_element_type=jnp.float32)
    ).astype(jnp.bfloat16)
    live_slot = jnp.repeat(held_orders >= 0, slot_width)[None, :]
    result = jnp.concatenate(
        [next_spreading_rate, next_thermal_state, surface_mass_next[None, :]], axis=0
    )
    return jnp.where(live_slot, result, jnp.zeros_like(result))


def solution(mesh):
    torus = Mesh(
        mesh.devices.reshape(mesh.shape["grp"], 4, 4, 2), ("grp", "wave_0", "wave_1", "wave_2")
    )
    placed = (
        P(None, GRP_WAVE),
        P(GRP_WAVE),
        P(GRP_WAVE),
        P(GRP_WAVE, None, None, None),
        P(),
        P(),
        P(),
        P(),
    )
    return jax.shard_map(
        shards, mesh=torus, in_specs=placed, out_specs=P(None, GRP_WAVE), check_vma=False
    )
```

profile of v0, /device:TPU:1, one launch (start us, length us, event | category | flops | bytes accessed | tf_op | source)
XLA Modules:
  0.0 343.0 jit_solution(1832600771421519429)
XLA Ops:
  0.0 1.3 dynamic-slice
  1.9 0.9 dynamic-update-slice
  2.8 20.8 %all-reduce = s32[192]{0:T(256)S(1)} all-reduce(s32[192]{0:T(256)S(1)} %dynamic-update-slice), channel_id=2, replica_groups=mesh['grp'=4,'wave_0'=4,'wave_1'=4,'wave_2'=2] {'grp','wave_0','wave_1'}, use_global_device_ids=true, to_apply=%add | all-reduce | flops 192 | bytes 1536
  23.6 0.1 reshape.256
  23.8 7.4 %all-gather.2 = s32[2,64,3]{1,2,0:T(4,128)S(1)} all-gather(s32[1,64,3]{1,2,0:T(4,128)S(1)} %copy.56), channel_id=1, replica_groups=mesh['grp'=4,'wave_0'=4,'wave_1'=4,'wave_2'=2] {'wave_2'}, dimensions={0}, use_global_device_ids=true | all-gather | bytes 2304 | tf_op jit(solution)/shard_map/all_gather | solution.py:20
  31.2 0.1 copy.57
  31.3 0.1 le.77
  31.4 0.7 broadcast_compare_fusion.1
  32.1 0.7 fusion.15
  32.8 0.7 compare_reduce_fusion
  33.6 0.7 broadcast_subtract_fusion.2
  34.3 0.7 multiply_add_fusion.1
  35.1 0.1 broadcast_in_dim.123
  35.2 0.1 add.162
  35.4 0.2 copy.59
  35.6 0.2 reshape.227
  35.8 0.1 fusion.9
  36.0 0.7 add_select_fusion
  36.7 0.1 select_n.101
  36.8 1.0 convert_reduce_fusion
  37.8 0.7 convert_element_type.37
  38.5 3.9 %fusion.4 = bf16[137,7690]{1,0:T(8,128)(2,1)S(1)} fusion(bf16[137,137]{1,0:T(8,128)(2,1)S(1)} %copy-done, f32[7690]{0:T(1024)S(1)} %convert_reduce_fusion, f32[137]{0:T(256)S(1)} %convert_element_type.37, f32[7690]{0:T(1024)S(1)} %fusion.11, bf16[275,7690]{1,0:T(8,128)(2,1)} %param.8), kind=kOutput, calls=%fused_computation.8 | convolution fusion | flops 294988448 | bytes 6704074 | tf_op jit(solution)/shard_map/dot_general | solution.py:111
  42.4 3.7 %copy.67 = bf16[137,7690]{0,1:T(8,128)(2,1)} copy(bf16[137,7690]{1,0:T(8,128)(2,1)S(1)} %fusion.4) | data formatting | bytes 4214120 | tf_op jit(solution)/shard_map/convert_element_type | solution.py:118
  46.1 22.6 %gather_fusion = bf16[8448,137]{1,0:T(8,128)(2,1)} fusion(bf16[137,7690]{0,1:T(8,128)(2,1)} %copy.67, s32[9216]{0:T(1024)S(1)} %pad_clamp_fusion), kind=kCustom, calls=%fused_computation | custom fusion | bytes 4663296 | tf_op jit(solution)/shard_map/jit(_take)/gather | solution.py:121
  68.8 4.6 %copy.68 = bf16[137,8448]{1,0:T(8,128)(2,1)S(1)} copy(bf16[137,8448]{0,1:T(8,128)(2,1)} %bitcast.62) | data formatting | bytes 4629504 | tf_op jit(solution)/shard_map/jit(_take)/gather | solution.py:121
  73.4 16.8 %gather.7 = bf16[137,128,66]{2,1,0:T(8,128)(2,1)} reshape(bf16[137,8448]{1,0:T(8,128)(2,1)S(1)} %copy.68) | data formatting | bytes 4629504 | tf_op jit(solution)/shard_map/jit(_take)/gather | solution.py:121
  90.2 0.1 copy.66
  90.3 2.6 broadcast_select_fusion
  92.9 5.0 %copy.88 = bf16[137,128,66]{2,0,1:T(8,128)(2,1)} copy(bf16[137,128,66]{2,1,0:T(8,128)(2,1)S(1)} %broadcast_select_fusion) | data formatting | bytes 4629504 | tf_op jit(solution)/shard_map/jit(_take)/select_n | solution.py:121
  97.9 17.0 %reshape.283 = bf16[128,2,4521]{2,1,0:T(2,128)(2,1)} reshape(bf16[128,137,66]{2,1,0:T(8,128)(2,1)} %bitcast.58) | data formatting | bytes 4629504
  115.0 3.9 %all-to-all-start = ((bf16[128,2,4521]{2,1,0:T(2,128)(2,1)}), bf16[128,2,4521]{2,1,0:T(2,128)(2,1)S(1)}, u32[]{:S(2)}, u32[]{:S(2)}) async-start(bf16[128,2,4521]{2,1,0:T(2,128)(2,1)} %reshape.283), calls=%async_computation | async-start | bytes 4718592 | tf_op jit(solution)/shard_map/all_to_all | solution.py:32
  118.9 0.7 dynamic-slice.1
  120.3 0.2 dynamic-update-slice.1
  120.6 13.8 %all-reduce.1 = s32[20]{0:T(128)S(1)} all-reduce(s32[20]{0:T(128)S(1)} %dynamic-update-slice.1), channel_id=3, replica_groups=mesh['grp'=4,'wave_0'=4,'wave_1'=4,'wave_2'=2] {'grp'}, use_global_device_ids=true, to_apply=%add.1 | all-reduce | flops 20 | bytes 160
  134.4 0.1 reshape.258
  134.5 15.7 %all-gather.3 = s32[4,4,5]{2,1,0:T(4,128)S(1)} all-gather(s32[1,4,5]{2,1,0:T(4,128)S(1)} %reshape.258), channel_id=1, replica_groups=mesh['grp'=4,'wave_0'=4,'wave_1'=4,'wave_2'=2] {'wave_0'}, dimensions={0}, use_global_device_ids=true | all-gather | bytes 400 | tf_op jit(solution)/shard_map/all_gather | solution.py:20
  150.2 0.1 copy.79
  150.2 16.4 %all-gather.4 = s32[4,16,5]{1,2,0:T(8,128)S(1)} all-gather(s32[1,16,5]{1,2,0:T(8,128)S(1)} %copy.79), channel_id=1, replica_groups=mesh['grp'=4,'wave_0'=4,'wave_1'=4,'wave_2'=2] {'wave_1'}, dimensions={0}, use_global_device_ids=true | all-gather | bytes 1600 | tf_op jit(solution)/shard_map/all_gather | solution.py:20
  166.6 0.1 reshape.262
  166.7 10.1 %all-gather.5 = s32[2,64,5]{1,2,0:T(8,128)S(1)} all-gather(s32[1,64,5]{1,2,0:T(8,128)S(1)} %reshape.262), channel_id=1, replica_groups=mesh['grp'=4,'wave_0'=4,'wave_1'=4,'wave_2'=2] {'wave_2'}, dimensions={0}, use_global_device_ids=true | all-gather | bytes 3840 | tf_op jit(solution)/shard_map/all_gather | solution.py:20
  176.9 0.1 reshape.228
  177.0 0.3 copy.63
  177.6 1.3 fusion.16
  178.9 10.2 %reshape.284 = bf16[128,137,66]{2,1,0:T(8,128)(2,1)} reshape(bf16[128,2,4521]{2,1,0:T(2,128)(2,1)S(1)} %all-to-all-done) | data formatting | bytes 4629504
  189.1 6.0 %copy.70 = bf16[137,128,66]{1,0,2:T(8,128)(2,1)S(1)} copy(bf16[137,128,66]{2,0,1:T(8,128)(2,1)} %bitcast.59) | data formatting | bytes 4629504 | tf_op jit(solution)/shard_map/all_to_all | solution.py:32
  195.1 0.8 convolution_bitcast_fusion.1
  195.9 0.1 slice.46
  196.0 0.1 copy-done.4
  196.1 0.4 fusion.5
  196.6 0.2 pad_maximum_fusion
  196.8 4.9 %copy.73 = bf16[137,128,66]{2,0,1:T(8,128)(2,1)} copy(bf16[137,128,66]{1,0,2:T(8,128)(2,1)S(1)} %bitcast.66) | data formatting | bytes 4629504 | tf_op jit(solution)/shard_map/convert_element_type | solution.py:50
  201.8 16.8 %reshape.285 = bf16[128,2,4521]{2,1,0:T(2,128)(2,1)} reshape(bf16[128,137,66]{2,1,0:T(8,128)(2,1)} %bitcast.60) | data formatting | bytes 4629504
  218.6 5.8 %all-to-all-start.1 = ((bf16[128,2,4521]{2,1,0:T(2,128)(2,1)}), bf16[128,2,4521]{2,1,0:T(2,128)(2,1)S(1)}, u32[]{:S(2)}, u32[]{:S(2)}) async-start(bf16[128,2,4521]{2,1,0:T(2,128)(2,1)} %reshape.285), calls=%async_computation.1 | async-start | bytes 4718592 | tf_op jit(solution)/shard_map/all_to_all | solution.py:36
  224.6 0.1 broadcast_in_dim.119
  224.7 32.9 %all-to-all-done.1 = bf16[128,2,4521]{2,1,0:T(2,128)(2,1)S(1)} async-done(((bf16[128,2,4521]{2,1,0:T(2,128)(2,1)}), bf16[128,2,4521]{2,1,0:T(2,128)(2,1)S(1)}, u32[]{:S(2)}, u32[]{:S(2)}) %all-to-all-start.1) | async-done | bytes 2314784 | tf_op jit(solution)/shard_map/all_to_all | solution.py:36
  257.6 10.2 %reshape.286 = bf16[128,137,66]{2,1,0:T(8,128)(2,1)} reshape(bf16[128,2,4521]{2,1,0:T(2,128)(2,1)S(1)} %all-to-all-done.1) | data formatting | bytes 4629504
  267.8 5.6 %copy.74 = bf16[137,128,66]{2,1,0:T(8,128)(2,1)} copy(bf16[137,128,66]{2,0,1:T(8,128)(2,1)} %bitcast.61) | data formatting | bytes 4629504 | tf_op jit(solution)/shard_map/all_to_all | solution.py:36
  273.4 7.4 %reshape.241 = bf16[137,8448]{1,0:T(8,128)(2,1)S(1)} reshape(bf16[137,128,66]{2,1,0:T(8,128)(2,1)} %copy.74) | data formatting | bytes 4629504 | tf_op jit(solution)/shard_map/all_to_all | solution.py:36
  280.8 3.8 %copy.75 = bf16[8448,137]{1,0:T(8,128)(2,1)} copy(bf16[8448,137]{0,1:T(8,128)(2,1)S(1)} %bitcast.65) | data formatting | bytes 4629504 | tf_op jit(solution)/shard_map/all_to_all | solution.py:36
  284.6 44.6 %scatter_custom_fusion = bf16[137,7690]{0,1:T(8,128)(2,1)} fusion(s32[8448]{0:T(1024)S(1)} %fusion.9, bf16[8448,137]{1,0:T(8,128)(2,1)} %copy.75, bf16[]{:T(256)} %constant.21.clone.1), kind=kCustom, calls=%fused_computation.17 | custom fusion | bytes 2107572 | tf_op jit(solution)/shard_map/scatter | solution.py:130
  329.2 4.5 %copy.76 = bf16[137,7690]{1,0:T(8,128)(2,1)S(1)} copy(bf16[137,7690]{0,1:T(8,128)(2,1)} %scatter_custom_fusion) | data formatting | bytes 4214120 | tf_op jit(solution)/shard_map/scatter | solution.py:130
  333.8 4.5 %fusion.3 = bf16[137,7690]{1,0:T(8,128)(2,1)S(1)} fusion(bf16[137,7690]{0,1:T(8,128)(2,1)} %scatter_custom_fusion, bf16[137,137]{1,0:T(8,128)(2,1)S(1)} %copy-done.7, bf16[275,7690]{1,0:T(8,128)(2,1)} %param.8), kind=kOutput, calls=%fused_computation.7 | convolution fusion | flops 291827840 | bytes 6358718 | tf_op jit(solution)/shard_map/dot_general | solution.py:134
  338.3 1.1 convolution_reduce_fusion
  339.5 3.3 maximum_select_fusion
  (49 shorter events, 0.7 us)
Async XLA Ops:
  0.0 38.5 %copy-start = (bf16[137,137]{1,0:T(8,128)(2,1)S(1)}, bf16[137,137]{1,0:T(8,128)(2,1)}, u32[]{:S(2)}) copy-start(bf16[137,137]{1,0:T(8,128)(2,1)} %param.12) | copy-start | bytes 112618
  115.0 4.0 %copy-start.9 = (u32[128]{0:T(128)S(1)}, u32[128]{0:T(128)}, u32[]{:S(2)}) copy-start(u32[128]{0:T(128)} %constant.72) | copy-start | bytes 1540
  115.0 5.3 %copy-start.5 = (s32[5]{0:T(128)S(1)}, s32[5]{0:T(128)}, u32[]{:S(2)}) copy-start(s32[5]{0:T(128)} %param.9) | copy-start | bytes 64
  115.0 62.4 %copy-start.6 = (s32[3]{0:T(128)S(1)}, s32[3]{0:T(128)}, u32[]{:S(2)}) copy-start(s32[3]{0:T(128)} %param.10) | copy-start | bytes 40
  115.0 62.6 %copy-start.3 = (bf16[3,2,137,137]{3,1,2,0:T(2,128)(2,1)S(1)}, bf16[3,2,137,137]{3,1,2,0:T(2,128)(2,1)}, u32[]{:S(2)}) copy-start(bf16[3,2,137,137]{3,1,2,0:T(2,128)(2,1)} %param.11) | copy-start | bytes 675688
  115.0 63.9 %all-to-all-start = ((bf16[128,2,4521]{2,1,0:T(2,128)(2,1)}), bf16[128,2,4521]{2,1,0:T(2,128)(2,1)S(1)}, u32[]{:S(2)}, u32[]{:S(2)}) async-start(bf16[128,2,4521]{2,1,0:T(2,128)(2,1)} %reshape.283), calls=%async_computation | async-start | bytes 4718592 | tf_op jit(solution)/shard_map/all_to_all | solution.py:32
  195.1 1.0 copy-start.4
  218.6 5.9 %copy-start.8 = (bf16[137]{0:T(256)(128)(2,1)S(1)}, bf16[137]{0:T(256)(128)(2,1)}, u32[]{:S(2)}) copy-start(bf16[137]{0:T(256)(128)(2,1)} %param.15) | copy-start | bytes 826
  218.6 39.0 %all-to-all-start.1 = ((bf16[128,2,4521]{2,1,0:T(2,128)(2,1)}), bf16[128,2,4521]{2,1,0:T(2,128)(2,1)S(1)}, u32[]{:S(2)}, u32[]{:S(2)}) async-start(bf16[128,2,4521]{2,1,0:T(2,128)(2,1)} %reshape.285), calls=%async_computation.1 | async-start | bytes 4718592 | tf_op jit(solution)/shard_map/all_to_all | solution.py:36
  329.2 4.5 %copy-start.7 = (bf16[137,137]{1,0:T(8,128)(2,1)S(1)}, bf16[137,137]{1,0:T(8,128)(2,1)}, u32[]{:S(2)}) copy-start(bf16[137,137]{1,0:T(8,128)(2,1)} %param.14) | copy-start | bytes 112618
  333.8 4.5 %copy-start.2 = (bf16[137,7690]{0,1:T(8,128)(2,1)S(1)}, bf16[137,7690]{0,1:T(8,128)(2,1)}, u32[]{:S(2)}) copy-start(bf16[137,7690]{0,1:T(8,128)(2,1)} %scatter_custom_fusion) | copy-start | bytes 6321184
  339.5 3.4 copy-start.1
where the time goes:
time: 348 us; the launch traced here: 343 us
  local copies, waits for them, and re-layouts  191 us (55%)
  blocking collectives  84.2 us (24%)
  waiting for transfers between devices  32.9 us (9%)
  other arithmetic  12.4 us (4%)
  matrix products  10.8 us (3%)
  starting transfers between devices  9.79 us (3%)
    unnamed x36, local copies, waits for them, and re-layouts  57.9 us
    all_gather x4, blocking collectives, all_blocks(): tiles = lax.all_gather(tiles, axes[k], axis=0, tiled=True)  49.6 us
    scatter x2, local copies, waits for them, and re-layouts, shards(): next_spreading_rate = jnp.zeros((layer_heights_count, fill_col), jnp.bflo...  49.1 us
    gather x3, local copies, waits for them, and re-layouts, shards(): message = jnp.take(right_side, column, axis=1, mode='fill', fill_value=0)  44 us
    unnamed x2, blocking collectives  34.6 us
    all_to_all x1, waiting for transfers between devices, send_home(): lax.all_to_all(message, GRP_WAVE, split_axis=1, concat_axis=1, tiled=True)  32.9 us
    all_to_all x3, local copies, waits for them, and re-layouts, send_home(): lax.all_to_all(message, GRP_WAVE, split_axis=1, concat_axis=1, tiled=True)  16.8 us
  transfers between devices with their start and end apart: 2, of which 1 were waited for; matrix products, arithmetic and copies ran while one was open for 1% of the time, Pallas kernels for 0%

commit v1 on v0

v1 whole, which is shorter than its diff:
```python
import functools

import jax
import jax.numpy as jnp
import numpy as np
from jax import lax
from jax.experimental import pallas as pl
from jax.experimental.pallas import tpu as pltpu
from jax.sharding import Mesh
from jax.sharding import PartitionSpec as P

GRP_WAVE = ("grp", "wave_0", "wave_1", "wave_2")

LANES = 128
ROWS = 24
FRONT = 768
TILE = 1024
BIG = 1 << 20


def edge_masks(slot_count, edge, shape, row_dim):
    rows = lax.broadcasted_iota(jnp.int32, shape, row_dim)
    lanes = lax.broadcasted_iota(jnp.int32, shape, len(shape) - 1)
    group = rows // 2
    return (lanes >= edge * group) & (lanes < edge * (group + 1)) & (rows < 4 * slot_count + 2)


def parity_fold(parts, axis):
    total = parts[0]
    for part in parts[1:]:
        total = total + part
    total = total + pltpu.roll(total, 2, axis)
    return total + pltpu.roll(total, 4, axis)


def slot_lines(columns, orders_ref, slot_count, slot_width):
    order = jnp.full(columns.shape, -1, jnp.int32)
    place = columns
    for s in range(slot_count):
        inside = (columns >= s * slot_width) & (columns < (s + 1) * slot_width)
        order = jnp.where(inside, orders_ref[s], order)
        place = jnp.where(inside, columns - s * slot_width, place)
    return order, place // 2


def rhs_kernel(
    sizes, orders_ref, state_ref, drive_ref, spread_ref, eye_ref, out_ref, xm, xe, lm, le, um, ue
):
    levels, slot_count, slot_width, truncation = sizes
    half = (truncation + 1) // 2
    step = pl.program_id(0)
    padded = spread_ref.shape[1]
    columns = step * TILE + lax.broadcasted_iota(jnp.int32, (1, TILE), 1)
    order, coeff = slot_lines(columns, orders_ref, slot_count, slot_width)
    degree = jnp.where(coeff <= truncation - order, order + coeff, coeff - 1)
    lap = (degree * (degree + 1)).astype(jnp.float32) / float(truncation * (truncation + 1))
    drive = jnp.dot(drive_ref[...], state_ref[...], preferred_element_type=jnp.float32)
    right = state_ref[:padded, :].astype(jnp.float32) + lap * drive
    right = jnp.where(columns < slot_count * slot_width, right, 0.0).astype(jnp.bfloat16)
    spread = jnp.dot(spread_ref[...], right, preferred_element_type=jnp.float32)
    spread = spread.astype(jnp.bfloat16)
    for k in range(TILE // 256):
        lines = lax.dot_general(
            eye_ref[...],
            spread[:, 256 * k : 256 * (k + 1)],
            (((1,), (1,)), ((), ())),
            preferred_element_type=jnp.float32,
        )
        start = pl.multiple_of(FRONT + step * TILE + 256 * k, 256)
        xm[pl.ds(start, 256), :] = lines[:, :LANES]
        xe[pl.ds(start, 256), :] = lines[:, LANES:]

    @pl.when(step == pl.num_programs(0) - 1)
    def _():
        def regroup(s, carry):
            order = jnp.maximum(orders_ref[s], 0)
            base = FRONT + s * slot_width
            for p in range(2):
                for x, low, up in ((xm, lm, um), (xe, le, ue)):
                    up[pl.ds(2 * s + p, half, stride=ROWS), :] = x[
                        pl.ds(base + 2 * (half + 1) + p, half, stride=2), :
                    ]
                    low[pl.ds(2 * s + p, half, stride=16), :] = x[
                        pl.ds(base - 2 * order + p, half, stride=2), :
                    ]
                    up[pl.ds(2 * (slot_count + s) + p, half, stride=ROWS), :] = x[
                        pl.ds(base + 2 * (half - order) + p, half, stride=2), :
                    ]

                    @pl.when(orders_ref[s] >= 0)
                    def _(x=x, up=up, p=p):
                        third = ROWS * (half - 1 - order) + 4 * slot_count + p
                        up[pl.ds(third, 1), :] = x[
                            pl.ds(base + 2 * (truncation + 1 - order) + p, 1), :
                        ]

            return carry

        lax.fori_loop(0, slot_count, regroup, 0)
        row = lax.broadcasted_iota(jnp.int32, (16, LANES), 0)
        order_rows = jnp.full((16, LANES), BIG, jnp.int32)
        for s in range(slot_count):
            order_rows = jnp.where(row // 2 == s, jnp.maximum(orders_ref[s], 0), order_rows)
        mask = edge_masks(slot_count, levels - LANES, (ROWS, LANES), 0)
        tail = lax.broadcasted_iota(jnp.int32, (8, LANES), 0) >= 6

        def assemble(n, carry):
            start = pl.multiple_of(ROWS * (half - 1 - n), 8)
            low = pl.multiple_of(16 * n, 16)
            body = um[pl.ds(start, ROWS), :]
            edge = ue[pl.ds(start, ROWS), :]
            own = order_rows <= n
            top = jnp.where(own, lm[pl.ds(low, 16), :], body[:16])
            top_edge = jnp.where(own, le[pl.ds(low, 16), :], edge[:16])
            folded = parity_fold(
                [
                    jnp.where(mask[:8], top_edge[:8], 0.0),
                    jnp.where(mask[8:16], top_edge[8:], 0.0),
                    jnp.where(mask[16:], edge[16:], 0.0),
                ],
                0,
            )
            block = jnp.concatenate([top, jnp.where(tail, folded, body[16:])], axis=0)
            out_ref[n] = block.astype(jnp.bfloat16)
            return carry

        lax.fori_loop(0, half, assemble, 0, unroll=4)


def permute_kernel(pair_count, index_ref, blocks_ref, out_ref):
    def body(d, carry):
        for j in range(pair_count):
            out_ref[d * pair_count + j] = blocks_ref[index_ref[d, j]]
        return carry

    lax.fori_loop(0, out_ref.shape[0] // pair_count, body, 0, unroll=4)


def solve_kernel(sizes, lows_ref, blocks_ref, weights_ref, orders_ref, out_ref):
    levels, slot_count = sizes
    count, pair_count = blocks_ref.shape[0], blocks_ref.shape[1]
    shape = (count, ROWS, LANES)
    mask = edge_masks(slot_count, levels - LANES, shape, 1)
    row = lax.broadcasted_iota(jnp.int32, shape, 1)
    for j in range(pair_count):
        body = blocks_ref[:, j].astype(jnp.float32)
        edge = jnp.where(row % 2 == 0, body[:, ROWS - 2 : ROWS - 1], body[:, ROWS - 1 :])
        edge = jnp.where(mask, edge, 0.0)
        lines = jnp.concatenate([body, edge], axis=-1).reshape(count * ROWS, 2 * LANES)
        lines = lines.astype(jnp.bfloat16)
        upper = jnp.dot(lines, weights_ref[j, 1], preferred_element_type=jnp.float32)
        lower = jnp.dot(lines, weights_ref[j, 0], preferred_element_type=jnp.float32)
        own = orders_ref[...] <= lows_ref[j]
        main = jnp.where(own, lower[:, :LANES], upper[:, :LANES]).reshape(shape)
        edge = jnp.where(own, lower[:, LANES:], upper[:, LANES:]).reshape(shape)
        edge = jnp.where(mask, edge, 0.0)
        folded = parity_fold([edge[:, :8], edge[:, 8:16], edge[:, 16:]], 1)
        folded = jnp.concatenate([folded, folded, folded], axis=1)
        out_ref[:, j] = jnp.where(row >= ROWS - 2, folded, main).astype(jnp.bfloat16)


def final_kernel(
    sizes, index_ref, orders_ref, blocks_ref, state_ref, weights_ref, out_ref, xm, xe, lm, le, um, ue
):
    levels, slot_count, slot_width, truncation, pair_count = sizes
    half = (truncation + 1) // 2
    step = pl.program_id(0)

    @pl.when(step == 0)
    def _():
        mask = edge_masks(slot_count, levels - LANES, (ROWS, LANES), 0)
        even = lax.broadcasted_iota(jnp.int32, (ROWS, LANES), 0) % 2 == 0

        def unfold(d, carry):
            for j in range(pair_count):
                n = index_ref[d, j]
                body = blocks_ref[d * pair_count + j].astype(jnp.float32)
                edge = jnp.where(even, body[ROWS - 2 : ROWS - 1], body[ROWS - 1 :])
                edge = jnp.where(mask, edge, 0.0)
                start = pl.multiple_of(ROWS * (half - 1 - n), 8)
                low = pl.multiple_of(16 * n, 16)
                um[pl.ds(start, ROWS), :] = body
                ue[pl.ds(start, ROWS), :] = edge
                lm[pl.ds(low, 16), :] = body[:16]
                le[pl.ds(low, 16), :] = edge[:16]
            return carry

        lax.fori_loop(0, half // pair_count, unfold, 0, unroll=2)

        def regroup(k, carry):
            s = slot_count - 1 - k
            order = jnp.maximum(orders_ref[s], 0)
            base = FRONT + s * slot_width
            for p in range(2):
                for x, low, up in ((xm, lm, um), (xe, le, ue)):
                    x[pl.ds(base + 2 * (half + 1) + p, half, stride=2), :] = up[
                        pl.ds(2 * s + p, half, stride=ROWS), :
                    ]
                    x[pl.ds(base - 2 * order + p, half, stride=2), :] = low[
                        pl.ds(2 * s + p, half, stride=16), :
                    ]
                    x[pl.ds(base + 2 * (half - order) + p, half, stride=2), :] = up[
                        pl.ds(2 * (slot_count + s) + p, half, stride=ROWS), :
                    ]
                third = ROWS * (half - 1 - order) + 4 * slot_count + p
                place = base + 2 * (truncation + 1 - order) + p
                xm[pl.ds(place, 1), :] = um[pl.ds(third, 1), :]
                xe[pl.ds(place, 1), :] = ue[pl.ds(third, 1), :]
            return carry

        lax.fori_loop(0, slot_count, regroup, 0)

    start = pl.multiple_of(FRONT + step * TILE, 256)
    lines = jnp.concatenate([xm[pl.ds(start, TILE), :], xe[pl.ds(start, TILE), :]], axis=1)
    moved = lax.dot_general(
        weights_ref[...],
        lines.astype(jnp.bfloat16),
        (((1,), (1,)), ((), ())),
        preferred_element_type=jnp.float32,
    )
    columns = step * TILE + lax.broadcasted_iota(jnp.int32, (1, TILE), 1)
    order, _ = slot_lines(columns, orders_ref, slot_count, slot_width)
    kept = lax.broadcasted_iota(jnp.int32, (state_ref.shape[0], 1), 0) >= levels
    base = jnp.where(kept, state_ref[...].astype(jnp.float32), 0.0)
    out_ref[...] = jnp.where(order >= 0, base + moved, 0.0).astype(jnp.bfloat16)


def level_of_lane(levels, slot_count):
    edge = levels - LANES
    table = np.zeros((2 * LANES, levels), np.float32)
    table[np.arange(LANES), np.arange(LANES)] = 1.0
    folded = np.arange(edge * (2 * slot_count + 1))
    table[LANES + folded, LANES + folded % edge] = 1.0
    return table


def shards(
    state,
    held_orders,
    pair_lows,
    inverses,
    height_operator,
    pressure_column,
    thermal_response_matrix,
    mass_row,
):
    levels = height_operator.shape[0]
    pair_count = pair_lows.shape[0]
    slot_count = held_orders.shape[0]
    devices = lax.axis_size(GRP_WAVE)
    half = pair_count * devices
    truncation = 2 * half - 1
    slot_width = 2 * (truncation + 2)
    width = slot_count * slot_width
    rows = state.shape[0]
    steps = -(-width // TILE)
    bf16, f32 = jnp.bfloat16, jnp.float32
    vmem = pl.BlockSpec(memory_space=pltpu.VMEM)
    smem = pl.BlockSpec(memory_space=pltpu.SMEM)
    params = functools.partial(pltpu.CompilerParams, vmem_limit_bytes=56 * 1024 * 1024)
    scratch = [
        pltpu.VMEM((FRONT + steps * TILE, LANES), f32),
        pltpu.VMEM((FRONT + steps * TILE, LANES), f32),
        pltpu.VMEM((16 * half, LANES), f32),
        pltpu.VMEM((16 * half, LANES), f32),
        pltpu.VMEM((ROWS * half, LANES), f32),
        pltpu.VMEM((ROWS * half, LANES), f32),
    ]

    own = jnp.concatenate([pair_lows, held_orders])
    own = jnp.pad(own, (0, LANES - own.shape[0]))
    index = lax.all_to_all(
        jnp.broadcast_to(own[None, None], (devices, 1, LANES)), GRP_WAVE, 0, 0, tiled=True
    ).reshape(devices, LANES)

    table = jnp.asarray(level_of_lane(levels, slot_count), bf16)
    padded = -(-levels // 16) * 16
    drive = jnp.concatenate(
        [jnp.zeros((levels, levels), bf16), height_operator, pressure_column[:, None]], axis=1
    )
    drive = jnp.pad(drive, ((0, padded - levels), (0, 0)))
    spread = jnp.pad(table, ((0, 0), (0, padded - levels)))
    eye = jnp.eye(256, dtype=bf16)

    blocks = pl.pallas_call(
        functools.partial(rhs_kernel, (levels, slot_count, slot_width, truncation)),
        grid=(steps,),
        in_specs=[
            smem,
            pl.BlockSpec((rows, TILE), lambda i: (0, i)),
            vmem,
            vmem,
            vmem,
        ],
        out_specs=pl.BlockSpec((half, ROWS, LANES), lambda i: (0, 0, 0)),
        out_shape=jax.ShapeDtypeStruct((half, ROWS, LANES), bf16),
        scratch_shapes=scratch,
        compiler_params=params(),
        cost_estimate=pl.CostEstimate(
            flops=4_000_000_000, bytes_accessed=7_000_000, transcendentals=0
        ),
        name="right_side",
    )(held_orders, state, drive, spread, eye)

    message = pl.pallas_call(
        functools.partial(permute_kernel, pair_count),
        in_specs=[smem, vmem],
        out_specs=vmem,
        out_shape=jax.ShapeDtypeStruct((half, ROWS, LANES), bf16),
        compiler_params=params(),
        name="by_owner",
    )(index, blocks)

    arrived = lax.all_to_all(
        message.reshape(devices, pair_count * ROWS, LANES), GRP_WAVE, 0, 0, tiled=True
    ).reshape(devices, pair_count, ROWS, LANES)

    weights = jnp.einsum("al,jtkl->jtak", table, inverses, preferred_element_type=f32)
    weights = jnp.einsum("jtak,bk->jtab", weights.astype(bf16), table, preferred_element_type=f32)
    weights = weights.astype(bf16)
    all_orders = index[:, pair_count : pair_count + slot_count]
    order_rows = jnp.pad(
        jnp.repeat(all_orders, 2, axis=1),
        ((0, 0), (0, ROWS - 2 * slot_count)),
        constant_values=BIG,
    ).reshape(devices * ROWS, 1)
    order_rows = jnp.broadcast_to(order_rows, (devices * ROWS, LANES))
    chunk = 16
    solved = pl.pallas_call(
        functools.partial(solve_kernel, (levels, slot_count)),
        grid=(devices // chunk,),
        in_specs=[
            smem,
            pl.BlockSpec((chunk, pair_count, ROWS, LANES), lambda i: (i, 0, 0, 0)),
            vmem,
            pl.BlockSpec((chunk * ROWS, LANES), lambda i: (i, 0)),
        ],
        out_specs=pl.BlockSpec((chunk, pair_count, ROWS, LANES), lambda i: (i, 0, 0, 0)),
        out_shape=jax.ShapeDtypeStruct((devices, pair_count, ROWS, LANES), bf16),
        compiler_params=params(),
        name="solve",
    )(pair_lows, arrived, weights, order_rows)

    returned = lax.all_to_all(
        solved.reshape(devices, pair_count * ROWS, LANES), GRP_WAVE, 0, 0, tiled=True
    ).reshape(half, ROWS, LANES)

    response = jnp.concatenate(
        [jnp.eye(levels, dtype=bf16), -thermal_response_matrix, -mass_row[None, :]], axis=0
    )
    response = jnp.dot(response, table.T, preferred_element_type=f32).astype(bf16)
    return pl.pallas_call(
        functools.partial(final_kernel, (levels, slot_count, slot_width, truncation, pair_count)),
        grid=(steps,),
        in_specs=[
            smem,
            smem,
            vmem,
            pl.BlockSpec((rows, TILE), lambda i: (0, i)),
            vmem,
        ],
        out_specs=pl.BlockSpec((rows, TILE), lambda i: (0, i)),
        out_shape=jax.ShapeDtypeStruct((rows, width), bf16),
        scratch_shapes=scratch,
        compiler_params=params(),
        name="final",
    )(index, held_orders, returned, state, response)


def solution(mesh):
    torus = Mesh(
        mesh.devices.reshape(mesh.shape["grp"], 4, 4, 2), ("grp", "wave_0", "wave_1", "wave_2")
    )
    placed = (
        P(None, GRP_WAVE),
        P(GRP_WAVE),
        P(GRP_WAVE),
        P(GRP_WAVE, None, None, None),
        P(),
        P(),
        P(),
        P(),
    )
    return jax.shard_map(
        shards, mesh=torus, in_specs=placed, out_specs=P(None, GRP_WAVE), check_vma=False
    )
```

time: 348 us -> 144 us (0.41); the launches traced: 343 us -> 143 us
  local copies, waits for them, and re-layouts: 191 us -> 6.74 us
  blocking collectives: 84.2 us -> 0 us
  Pallas kernels: 0 us -> 42 us
  waiting for transfers between devices: 32.9 us -> 62.8 us
  starting transfers between devices: 9.79 us -> 26.1 us
  other arithmetic: 12.4 us -> 2.49 us
  matrix products: 10.8 us -> 2.61 us
    unnamed x36 -> x19, local copies, waits for them, and re-layouts: 57.9 us -> 2.19 us
    all_gather x4 -> x0, blocking collectives: 49.6 us -> none  [all_blocks(): tiles = lax.all_gather(tiles, axes[k], axis=0, tiled=True)]
    scatter x2 -> x0, local copies, waits for them, and re-layouts: 49.1 us -> none  [shards(): next_spreading_rate = jnp.zeros((layer_heights_count, fill_col), jnp.bflo...]
    gather x3 -> x0, local copies, waits for them, and re-layouts: 44 us -> none  [shards(): message = jnp.take(right_side, column, axis=1, mode='fill', fill_value=0)]
    pallas_call x0 -> x4, Pallas kernels: none -> 42 us  [the longest x1 16 us: shards(): pl.pallas_call(functools.partial(rhs_kernel, (levels, slot_count, slot_wi...]
    unnamed x2 -> x0, blocking collectives: 34.6 us -> none
    all_to_all x2 -> x3, waiting for transfers between devices: 32.9 us -> 62.8 us  [the longest x1 32.1 us: shards(): lax.all_to_all(solved.reshape(devices, pair_count * ROWS, LANES), GRP_WAV...]
    all_to_all x4 -> x0, local copies, waits for them, and re-layouts: 22.8 us -> none  [the longest x3 16.8 us: send_home(): lax.all_to_all(message, GRP_WAVE, split_axis=1, concat_axis=1, tiled=True)]
  transfers between devices with their start and end apart: 2 -> 3, of which waited for: 1 -> 2; matrix products, arithmetic and copies ran while one was open for 1% -> 4% of each run, Pallas kernels for 0% -> 11%
where the time goes in v1:
time: 144 us; the launch traced here: 143 us
  waiting for transfers between devices  62.8 us (44%)
  Pallas kernels  42 us (29%)
  starting transfers between devices  26.1 us (18%)
  local copies, waits for them, and re-layouts  6.74 us (5%)
  matrix products  2.61 us (2%)
  other arithmetic  2.49 us (2%)
    all_to_all x1, waiting for transfers between devices, shards(): lax.all_to_all(solved.reshape(devices, pair_count * ROWS, LANES), GRP_WAV...  32.1 us
    all_to_all x1, waiting for transfers between devices, shards(): lax.all_to_all(message.reshape(devices, pair_count * ROWS, LANES), GRP_WA...  30.7 us
    pallas_call x1, Pallas kernels, shards(): pl.pallas_call(functools.partial(rhs_kernel, (levels, slot_count, slot_wi...  16 us
    pallas_call x1, Pallas kernels, shards(): pl.pallas_call(functools.partial(final_kernel, (levels, slot_count, slot_...  14 us
    all_to_all x1, starting transfers between devices, shards(): lax.all_to_all(jnp.broadcast_to(own[None, None], (devices, 1, LANES)), GR...  11.5 us
    all_to_all x1, starting transfers between devices, shards(): lax.all_to_all(message.reshape(devices, pair_count * ROWS, LANES), GRP_WA...  9.78 us
    pallas_call x1, Pallas kernels, shards(): pl.pallas_call(functools.partial(solve_kernel, (levels, slot_count)), gri...  8.12 us
    all_to_all x1, starting transfers between devices, shards(): lax.all_to_all(solved.reshape(devices, pair_count * ROWS, LANES), GRP_WAV...  4.89 us
  transfers between devices with their start and end apart: 3, of which 2 were waited for; matrix products, arithmetic and copies ran while one was open for 4% of the time, Pallas kernels for 11%

profile of v1, /device:TPU:1, one launch (start us, length us, event | category | flops | bytes accessed | tf_op | source)
XLA Modules:
  0.0 143.0 jit_solution(17705792862933289354)
XLA Ops:
  0.0 0.0 copy-start
  0.0 0.8 pad_add_fusion
  0.8 0.7 broadcast_in_dim.23
  1.5 11.5 %all-to-all-start = ((s32[128,1,128]{2,1,0:T(1,128)}), s32[128,1,128]{2,1,0:T(1,128)S(1)}, u32[]{:S(2)}, u32[]{:S(2)}) async-start(s32[128,1,128]{2,1,0:T(1,128)} %broadcast_in_dim.23), calls=%async_computation | async-start | bytes 131072 | tf_op jit(solution)/shard_map/all_to_all | solution.py:272
  13.0 0.7 fusion.3.eye_ref
  13.6 0.7 broadcast_in_dim.29
  14.4 1.0 pad_maximum_fusion
  15.4 0.7 pad.17.drive_ref
  16.0 16.0 %right_side.1.blocks_ref = bf16[384,24,128]{2,1,0:T(8,128)(2,1)} custom-call(s32[5]{0:T(128)} %orders_ref.3, bf16[275,7690]{1,0:T(8,128)(2,1)} %state_ref.3, bf16[144,275]{1,0:T(8,128)(2,1)} %pad.17.drive_ref, bf16[256,144]{1,0:T(8,128)(2,1)} %constant.22.spread_ref, bf16[256,256]{1,0:T(8,128)(2,1)} %fusion.3.eye_ref), custom_call_target="tpu_custom_call" | custom-call | flops 4000000000 | bytes 7000000 | tf_op jit(solution)/shard_map/right_side/pallas_call | solution.py:285
  32.1 0.0 all-to-all-done
  32.1 0.0 copy-start.3
  32.1 0.6 copy-done.3
  32.7 3.8 %by_owner.1 = bf16[384,24,128]{2,1,0:T(8,128)(2,1)} custom-call(s32[128,128]{1,0:T(8,128)} %bitcast.21, bf16[384,24,128]{2,1,0:T(8,128)(2,1)} %right_side.1.blocks_ref), custom_call_target="tpu_custom_call" | custom-call | tf_op jit(solution)/shard_map/by_owner/pallas_call | solution.py:305
  36.5 0.0 copy-start.8
  36.5 0.0 copy-start.4
  36.5 9.8 %all-to-all-start.1 = ((bf16[128,72,128]{2,1,0:T(8,128)(2,1)}), bf16[128,72,128]{2,1,0:T(8,128)(2,1)S(1)}, u32[]{:S(2)}, u32[]{:S(2)}) async-start(bf16[128,72,128]{2,1,0:T(8,128)(2,1)} %bitcast.20), calls=%async_computation.1 | async-start | bytes 4718592 | tf_op jit(solution)/shard_map/all_to_all | solution.py:314
  46.3 0.0 copy-done
  46.3 0.0 copy-done.8
  46.3 1.8 %convolution_convert_fusion.weights_ref = bf16[3,2,256,256]{3,2,1,0:T(8,128)(2,1)} fusion(bf16[256,137,1,1]{0,1,3,2:T(8,128)(2,1)S(1)} %copy-done.8, bf16[3,2,137,137]{3,1,2,0:T(2,128)(2,1)S(1)} %copy-done), kind=kOutput, calls=%fused_computation | convolution fusion | flops 166003200 | bytes 1081804 | tf_op jit(solution)/shard_map/jtak,bk->jtab/dot_general | solution.py:319
  48.1 0.0 copy-done.4
  48.1 0.1 slice.4
  48.1 0.1 copy.15
  48.2 0.1 copy.18
  48.4 0.1 broadcast_in_dim.27
  48.5 30.7 %all-to-all-done.1 = bf16[128,72,128]{2,1,0:T(8,128)(2,1)S(1)} async-done(((bf16[128,72,128]{2,1,0:T(8,128)(2,1)}), bf16[128,72,128]{2,1,0:T(8,128)(2,1)S(1)}, u32[]{:S(2)}, u32[]{:S(2)}) %all-to-all-start.1) | async-done | bytes 2359328 | tf_op jit(solution)/shard_map/all_to_all | solution.py:314
  79.2 0.0 copy-start.1
  79.2 2.2 %broadcast_in_dim.28.orders_ref = s32[3072,128]{1,0:T(8,128)} broadcast(s32[3072]{0:T(1024)S(1)} %broadcast_in_dim.27), dimensions={0} | broadcast | bytes 1585152 | tf_op jit(solution)/shard_map/broadcast_in_dim | solution.py:327
  81.4 0.0 copy-done.1
  81.4 8.1 %solve.1 = bf16[128,3,24,128]{3,2,1,0:T(8,128)(2,1)} custom-call(s32[3]{0:T(128)} %lows_ref.1, bf16[128,3,24,128]{3,2,1,0:T(8,128)(2,1)} %bitcast.17, bf16[3,2,256,256]{3,2,1,0:T(8,128)(2,1)} %convolution_convert_fusion.weights_ref, s32[3072,128]{1,0:T(8,128)} %broadcast_in_dim.28.orders_ref), custom_call_target="tpu_custom_call" | custom-call | tf_op jit(solution)/shard_map/solve/pallas_call | solution.py:329
  89.5 0.0 copy-start.5
  89.5 0.0 copy-start.6
  89.5 0.0 copy-start.7
  89.6 4.9 %all-to-all-start.2 = ((bf16[128,72,128]{2,1,0:T(8,128)(2,1)}), bf16[128,72,128]{2,1,0:T(8,128)(2,1)S(1)}, u32[]{:S(2)}, u32[]{:S(2)}) async-start(bf16[128,72,128]{2,1,0:T(8,128)(2,1)} %bitcast.19), calls=%async_computation.2 | async-start | bytes 4718592 | tf_op jit(solution)/shard_map/all_to_all | solution.py:344
  94.5 0.0 copy-done.5
  94.5 0.0 copy-done.6
  94.5 0.0 copy-done.7
  94.6 0.8 convolution_convert_fusion.2.weights_ref
  95.4 32.1 %all-to-all-done.2 = bf16[128,72,128]{2,1,0:T(8,128)(2,1)S(1)} async-done(((bf16[128,72,128]{2,1,0:T(8,128)(2,1)}), bf16[128,72,128]{2,1,0:T(8,128)(2,1)S(1)}, u32[]{:S(2)}, u32[]{:S(2)}) %all-to-all-start.2) | async-done | bytes 2359328 | tf_op jit(solution)/shard_map/all_to_all | solution.py:344
  127.5 0.0 copy-start.2
  127.5 1.4 copy-done.2
  128.9 14.0 %final.1 = bf16[275,7690]{1,0:T(8,128)(2,1)} custom-call(s32[128,128]{1,0:T(8,128)} %bitcast.22, s32[5]{0:T(128)} %orders_ref.3, bf16[384,24,128]{2,1,0:T(8,128)(2,1)} %bitcast.18, bf16[275,7690]{1,0:T(8,128)(2,1)} %state_ref.3, bf16[275,256]{1,0:T(8,128)(2,1)} %convolution_convert_fusion.2.weights_ref), custom_call_target="tpu_custom_call" | custom-call | tf_op jit(solution)/shard_map/final/pallas_call | solution.py:352
  (10 shorter events, 0.1 us)
Async XLA Ops:
  0.0 46.3 %copy-start = (bf16[3,2,137,137]{3,1,2,0:T(2,128)(2,1)S(1)}, bf16[3,2,137,137]{3,1,2,0:T(2,128)(2,1)}, u32[]{:S(2)}) copy-start(bf16[3,2,137,137]{3,1,2,0:T(2,128)(2,1)} %param.12) | copy-start | bytes 675688
  1.5 30.6 %all-to-all-start = ((s32[128,1,128]{2,1,0:T(1,128)}), s32[128,1,128]{2,1,0:T(1,128)S(1)}, u32[]{:S(2)}, u32[]{:S(2)}) async-start(s32[128,1,128]{2,1,0:T(1,128)} %broadcast_in_dim.23), calls=%async_computation | async-start | bytes 131072 | tf_op jit(solution)/shard_map/all_to_all | solution.py:272
  32.1 0.6 copy-start.3
  36.5 9.8 %copy-start.8 = (bf16[256,137,1,1]{0,1,3,2:T(8,128)(2,1)S(1)}, bf16[256,137,1,1]{0,1,3,2:T(8,128)(2,1)}, u32[]{:S(2)}) copy-start(bf16[256,137,1,1]{0,1,3,2:T(8,128)(2,1)} %constant.23) | copy-start | bytes 210436
  36.5 11.6 %copy-start.4 = (s32[128,1,128]{2,1,0:T(1,128)S(1)}, s32[128,1,128]{2,1,0:T(1,128)}, u32[]{:S(2)}) copy-start(s32[128,1,128]{2,1,0:T(1,128)} %copy-done.3) | copy-start | bytes 196612
  36.5 42.7 %all-to-all-start.1 = ((bf16[128,72,128]{2,1,0:T(8,128)(2,1)}), bf16[128,72,128]{2,1,0:T(8,128)(2,1)S(1)}, u32[]{:S(2)}, u32[]{:S(2)}) async-start(bf16[128,72,128]{2,1,0:T(8,128)(2,1)} %bitcast.20), calls=%async_computation.1 | async-start | bytes 4718592 | tf_op jit(solution)/shard_map/all_to_all | solution.py:314
  79.2 2.2 %copy-start.1 = (bf16[128,72,128]{2,1,0:T(8,128)(2,1)}, bf16[128,72,128]{2,1,0:T(8,128)(2,1)S(1)}, u32[]{:S(2)}) copy-start(bf16[128,72,128]{2,1,0:T(8,128)(2,1)S(1)} %all-to-all-done.1) | copy-start | bytes 7077892
  89.5 4.9 %copy-start.5 = (bf16[137,137]{1,0:T(8,128)(2,1)S(1)}, bf16[137,137]{1,0:T(8,128)(2,1)}, u32[]{:S(2)}) copy-start(bf16[137,137]{1,0:T(8,128)(2,1)} %param.15) | copy-start | bytes 112618
  89.5 4.9 %copy-start.6 = (bf16[137]{0:T(256)(128)(2,1)S(1)}, bf16[137]{0:T(256)(128)(2,1)}, u32[]{:S(2)}) copy-start(bf16[137]{0:T(256)(128)(2,1)} %param.16) | copy-start | bytes 826
  89.5 5.0 %copy-start.7 = (bf16[256,137]{0,1:T(8,128)(2,1)S(1)}, bf16[256,137]{0,1:T(8,128)(2,1)}, u32[]{:S(2)}) copy-start(bf16[256,137]{0,1:T(8,128)(2,1)} %constant.9.clone) | copy-start | bytes 210436
  89.6 38.0 %all-to-all-start.2 = ((bf16[128,72,128]{2,1,0:T(8,128)(2,1)}), bf16[128,72,128]{2,1,0:T(8,128)(2,1)S(1)}, u32[]{:S(2)}, u32[]{:S(2)}) async-start(bf16[128,72,128]{2,1,0:T(8,128)(2,1)} %bitcast.19), calls=%async_computation.2 | async-start | bytes 4718592 | tf_op jit(solution)/shard_map/all_to_all | solution.py:344
  127.5 1.4 %copy-start.2 = (bf16[128,72,128]{2,1,0:T(8,128)(2,1)}, bf16[128,72,128]{2,1,0:T(8,128)(2,1)S(1)}, u32[]{:S(2)}) copy-start(bf16[128,72,128]{2,1,0:T(8,128)(2,1)S(1)} %all-to-all-done.2) | copy-start | bytes 7077892

commit v2 on v1

--- a/solution.py
+++ b/solution.py
@@ -16,6 +16,8 @@
 FRONT = 768
 TILE = 1024
 BIG = 1 << 20
+LOW = 17
+UP = 25
 
 
 def edge_masks(slot_count, edge, shape, row_dim):
@@ -44,18 +46,48 @@
 
 
 def rhs_kernel(
-    sizes, orders_ref, state_ref, drive_ref, spread_ref, eye_ref, out_ref, xm, xe, lm, le, um, ue
+    sizes,
+    index_ref,
+    orders_ref,
+    state_ref,
+    height_ref,
+    pressure_ref,
+    place_ref,
+    spread_ref,
+    eye_ref,
+    out_ref,
+    drive,
+    xm,
+    xe,
+    lm,
+    le,
+    um,
+    ue,
 ):
-    levels, slot_count, slot_width, truncation = sizes
+    levels, slot_count, slot_width, truncation, pair_count = sizes
     half = (truncation + 1) // 2
     step = pl.program_id(0)
     padded = spread_ref.shape[1]
+
+    @pl.when(step == 0)
+    def _():
+        moved = jnp.dot(height_ref[...], place_ref[...], preferred_element_type=jnp.float32)
+        row = jnp.broadcast_to(pressure_ref[...].reshape(1, levels), (LANES, levels))
+        column = lax.dot_general(
+            eye_ref[:levels, :levels], row, (((1,), (1,)), ((), ())),
+            preferred_element_type=jnp.float32,
+        )
+        last = lax.broadcasted_iota(jnp.int32, moved.shape, 1) == 2 * levels
+        moved = jnp.where(last, column[:, :1], moved).astype(jnp.bfloat16)
+        drive[...] = jnp.zeros_like(drive)
+        drive[:levels, :] = moved
+
     columns = step * TILE + lax.broadcasted_iota(jnp.int32, (1, TILE), 1)
     order, coeff = slot_lines(columns, orders_ref, slot_count, slot_width)
     degree = jnp.where(coeff <= truncation - order, order + coeff, coeff - 1)
     lap = (degree * (degree + 1)).astype(jnp.float32) / float(truncation * (truncation + 1))
-    drive = jnp.dot(drive_ref[...], state_ref[...], preferred_element_type=jnp.float32)
-    right = state_ref[:padded, :].astype(jnp.float32) + lap * drive
+    pull = jnp.dot(drive[...], state_ref[...], preferred_element_type=jnp.float32)
+    right = state_ref[:padded, :].astype(jnp.float32) + lap * pull
     right = jnp.where(columns < slot_count * slot_width, right, 0.0).astype(jnp.bfloat16)
     spread = jnp.dot(spread_ref[...], right, preferred_element_type=jnp.float32)
     spread = spread.astype(jnp.bfloat16)
@@ -77,19 +109,19 @@
             base = FRONT + s * slot_width
             for p in range(2):
                 for x, low, up in ((xm, lm, um), (xe, le, ue)):
-                    up[pl.ds(2 * s + p, half, stride=ROWS), :] = x[
+                    up[pl.ds(2 * s + p, half, stride=UP), :] = x[
                         pl.ds(base + 2 * (half + 1) + p, half, stride=2), :
                     ]
-                    low[pl.ds(2 * s + p, half, stride=16), :] = x[
+                    low[pl.ds(2 * s + p, half, stride=LOW), :] = x[
                         pl.ds(base - 2 * order + p, half, stride=2), :
                     ]
-                    up[pl.ds(2 * (slot_count + s) + p, half, stride=ROWS), :] = x[
+                    up[pl.ds(2 * (slot_count + s) + p, half, stride=UP), :] = x[
                         pl.ds(base + 2 * (half - order) + p, half, stride=2), :
                     ]
 
                     @pl.when(orders_ref[s] >= 0)
                     def _(x=x, up=up, p=p):
-                        third = ROWS * (half - 1 - order) + 4 * slot_count + p
+                        third = UP * (half - 1 - order) + 4 * slot_count + p
                         up[pl.ds(third, 1), :] = x[
                             pl.ds(base + 2 * (truncation + 1 - order) + p, 1), :
                         ]
@@ -104,9 +136,10 @@
         mask = edge_masks(slot_count, levels - LANES, (ROWS, LANES), 0)
         tail = lax.broadcasted_iota(jnp.int32, (8, LANES), 0) >= 6
 
-        def assemble(n, carry):
-            start = pl.multiple_of(ROWS * (half - 1 - n), 8)
-            low = pl.multiple_of(16 * n, 16)
+        def assemble(d, j):
+            n = index_ref[d, j]
+            start = UP * (half - 1 - n)
+            low = LOW * n
             body = um[pl.ds(start, ROWS), :]
             edge = ue[pl.ds(start, ROWS), :]
             own = order_rows <= n
@@ -121,27 +154,31 @@
                 0,
             )
             block = jnp.concatenate([top, jnp.where(tail, folded, body[16:])], axis=0)
-            out_ref[n] = block.astype(jnp.bfloat16)
+            out_ref[d * pair_count + j] = block.astype(jnp.bfloat16)
+
+        def assemble_all(d, carry):
+            for j in range(pair_count):
+                assemble(d, j)
             return carry
 
-        lax.fori_loop(0, half, assemble, 0, unroll=4)
-
-
-def permute_kernel(pair_count, index_ref, blocks_ref, out_ref):
-    def body(d, carry):
-        for j in range(pair_count):
-            out_ref[d * pair_count + j] = blocks_ref[index_ref[d, j]]
-        return carry
-
-    lax.fori_loop(0, out_ref.shape[0] // pair_count, body, 0, unroll=4)
-
-
-def solve_kernel(sizes, lows_ref, blocks_ref, weights_ref, orders_ref, out_ref):
+        lax.fori_loop(0, half // pair_count, assemble_all, 0, unroll=2)
+
+
+def solve_kernel(sizes, lows_ref, index_ref, blocks_ref, weights_ref, out_ref):
     levels, slot_count = sizes
     count, pair_count = blocks_ref.shape[0], blocks_ref.shape[1]
     shape = (count, ROWS, LANES)
     mask = edge_masks(slot_count, levels - LANES, shape, 1)
     row = lax.broadcasted_iota(jnp.int32, shape, 1)
+    slot = lax.broadcasted_iota(jnp.int32, (ROWS, LANES), 0) // 2
+    orders = []
+    for k in range(count):
+        lines = jnp.full((ROWS, LANES), BIG, jnp.int32)
+        for s in range(slot_count):
+            order = index_ref[pl.program_id(0) * count + k, pair_count + s]
+            lines = jnp.where(slot == s, order, lines)
+        orders.append(lines)
+    orders = jnp.concatenate(orders, axis=0)
     for j in range(pair_count):
         body = blocks_ref[:, j].astype(jnp.float32)
         edge = jnp.where(row % 2 == 0, body[:, ROWS - 2 : ROWS - 1], body[:, ROWS - 1 :])
@@ -150,7 +187,7 @@
         lines = lines.astype(jnp.bfloat16)
         upper = jnp.dot(lines, weights_ref[j, 1], preferred_element_type=jnp.float32)
         lower = jnp.dot(lines, weights_ref[j, 0], preferred_element_type=jnp.float32)
-        own = orders_ref[...] <= lows_ref[j]
+        own = orders <= lows_ref[j]
         main = jnp.where(own, lower[:, :LANES], upper[:, :LANES]).reshape(shape)
         edge = jnp.where(own, lower[:, LANES:], upper[:, LANES:]).reshape(shape)
         edge = jnp.where(mask, edge, 0.0)
@@ -177,8 +214,8 @@
                 body = blocks_ref[d * pair_count + j].astype(jnp.float32)
                 edge = jnp.where(even, body[ROWS - 2 : ROWS - 1], body[ROWS - 1 :])
                 edge = jnp.where(mask, edge, 0.0)
-                start = pl.multiple_of(ROWS * (half - 1 - n), 8)
-                low = pl.multiple_of(16 * n, 16)
+                start = UP * (half - 1 - n)
+                low = LOW * n
                 um[pl.ds(start, ROWS), :] = body
                 ue[pl.ds(start, ROWS), :] = edge
                 lm[pl.ds(low, 16), :] = body[:16]
@@ -194,15 +231,15 @@
             for p in range(2):
                 for x, low, up in ((xm, lm, um), (xe, le, ue)):
                     x[pl.ds(base + 2 * (half + 1) + p, half, stride=2), :] = up[
-                        pl.ds(2 * s + p, half, stride=ROWS), :
+                        pl.ds(2 * s + p, half, stride=UP), :
                     ]
                     x[pl.ds(base - 2 * order + p, half, stride=2), :] = low[
-                        pl.ds(2 * s + p, half, stride=16), :
+                        pl.ds(2 * s + p, half, stride=LOW), :
                     ]
                     x[pl.ds(base + 2 * (half - order) + p, half, stride=2), :] = up[
-                        pl.ds(2 * (slot_count + s) + p, half, stride=ROWS), :
-                    ]
-                third = ROWS * (half - 1 - order) + 4 * slot_count + p
+                        pl.ds(2 * (slot_count + s) + p, half, stride=UP), :
+                    ]
+                third = UP * (half - 1 - order) + 4 * slot_count + p
                 place = base + 2 * (truncation + 1 - order) + p
                 xm[pl.ds(place, 1), :] = um[pl.ds(third, 1), :]
                 xe[pl.ds(place, 1), :] = ue[pl.ds(third, 1), :]
@@ -257,14 +294,17 @@
     bf16, f32 = jnp.bfloat16, jnp.float32
     vmem = pl.BlockSpec(memory_space=pltpu.VMEM)
     smem = pl.BlockSpec(memory_space=pltpu.SMEM)
-    params = functools.partial(pltpu.CompilerParams, vmem_limit_bytes=56 * 1024 * 1024)
+
+    def params(mib):
+        return pltpu.CompilerParams(vmem_limit_bytes=mib * 1024 * 1024)
+
     scratch = [
         pltpu.VMEM((FRONT + steps * TILE, LANES), f32),
         pltpu.VMEM((FRONT + steps * TILE, LANES), f32),
-        pltpu.VMEM((16 * half, LANES), f32),
-        pltpu.VMEM((16 * half, LANES), f32),
-        pltpu.VMEM((ROWS * half, LANES), f32),
-        pltpu.VMEM((ROWS * half, LANES), f32),
+        pltpu.VMEM((LOW * half, LANES), f32),
+        pltpu.VMEM((LOW * half, LANES), f32),
+        pltpu.VMEM((UP * half, LANES), f32),
+        pltpu.VMEM((UP * half, LANES), f32),
     ]
 
     own = jnp.concatenate([pair_lows, held_orders])
@@ -273,43 +313,34 @@
         jnp.broadcast_to(own[None, None], (devices, 1, LANES)), GRP_WAVE, 0, 0, tiled=True
     ).reshape(devices, LANES)
 
-    table = jnp.asarray(level_of_lane(levels, slot_count), bf16)
+    table = level_of_lane(levels, slot_count)
     padded = -(-levels // 16) * 16
-    drive = jnp.concatenate(
-        [jnp.zeros((levels, levels), bf16), height_operator, pressure_column[:, None]], axis=1
-    )
-    drive = jnp.pad(drive, ((0, padded - levels), (0, 0)))
-    spread = jnp.pad(table, ((0, 0), (0, padded - levels)))
-    eye = jnp.eye(256, dtype=bf16)
-
-    blocks = pl.pallas_call(
-        functools.partial(rhs_kernel, (levels, slot_count, slot_width, truncation)),
+    spread = np.zeros((2 * LANES, padded), np.float32)
+    spread[:, :levels] = table
+    place = np.zeros((levels, rows), np.float32)
+    place[:, levels : 2 * levels] = np.eye(levels)
+    table, spread, place = (jnp.asarray(x, bf16) for x in (table, spread, place))
+    eye = jnp.asarray(np.eye(256), bf16)
+
+    message = pl.pallas_call(
+        functools.partial(rhs_kernel, (levels, slot_count, slot_width, truncation, pair_count)),
         grid=(steps,),
         in_specs=[
             smem,
+            smem,
             pl.BlockSpec((rows, TILE), lambda i: (0, i)),
+            vmem,
+            vmem,
             vmem,
             vmem,
             vmem,
         ],
         out_specs=pl.BlockSpec((half, ROWS, LANES), lambda i: (0, 0, 0)),
         out_shape=jax.ShapeDtypeStruct((half, ROWS, LANES), bf16),
-        scratch_shapes=scratch,
-        compiler_params=params(),
-        cost_estimate=pl.CostEstimate(
-            flops=4_000_000_000, bytes_accessed=7_000_000, transcendentals=0
-        ),
+        scratch_shapes=[pltpu.VMEM((padded, rows), bf16)] + scratch,
+        compiler_params=params(56),
         name="right_side",
-    )(held_orders, state, drive, spread, eye)
-
-    message = pl.pallas_call(
-        functools.partial(permute_kernel, pair_count),
-        in_specs=[smem, vmem],
-        out_specs=vmem,
-        out_shape=jax.ShapeDtypeStruct((half, ROWS, LANES), bf16),
-        compiler_params=params(),
-        name="by_owner",
-    )(index, blocks)
+    )(index, held_orders, state, height_operator, pressure_column, place, spread, eye)
 
     arrived = lax.all_to_all(
         message.reshape(devices, pair_count * ROWS, LANES), GRP_WAVE, 0, 0, tiled=True
@@ -318,28 +349,21 @@
     weights = jnp.einsum("al,jtkl->jtak", table, inverses, preferred_element_type=f32)
     weights = jnp.einsum("jtak,bk->jtab", weights.astype(bf16), table, preferred_element_type=f32)
     weights = weights.astype(bf16)
-    all_orders = index[:, pair_count : pair_count + slot_count]
-    order_rows = jnp.pad(
-        jnp.repeat(all_orders, 2, axis=1),
-        ((0, 0), (0, ROWS - 2 * slot_count)),
-        constant_values=BIG,
-    ).reshape(devices * ROWS, 1)
-    order_rows = jnp.broadcast_to(order_rows, (devices * ROWS, LANES))
     chunk = 16
     solved = pl.pallas_call(
         functools.partial(solve_kernel, (levels, slot_count)),
         grid=(devices // chunk,),
         in_specs=[
             smem,
+            smem,
             pl.BlockSpec((chunk, pair_count, ROWS, LANES), lambda i: (i, 0, 0, 0)),
             vmem,
-            pl.BlockSpec((chunk * ROWS, LANES), lambda i: (i, 0)),
         ],
         out_specs=pl.BlockSpec((chunk, pair_count, ROWS, LANES), lambda i: (i, 0, 0, 0)),
         out_shape=jax.ShapeDtypeStruct((devices, pair_count, ROWS, LANES), bf16),
-        compiler_params=params(),
+        compiler_params=params(54),
         name="solve",
-    )(pair_lows, arrived, weights, order_rows)
+    )(pair_lows, index, arrived, weights)
 
     returned = lax.all_to_all(
         solved.reshape(devices, pair_count * ROWS, LANES), GRP_WAVE, 0, 0, tiled=True
@@ -362,7 +386,7 @@
         out_specs=pl.BlockSpec((rows, TILE), lambda i: (0, i)),
         out_shape=jax.ShapeDtypeStruct((rows, width), bf16),
         scratch_shapes=scratch,
-        compiler_params=params(),
+        compiler_params=params(48),
         name="final",
     )(index, held_orders, returned, state, response)
 

time: 144 us -> 133 us (0.924)
  blocking collectives: 0 us -> 21.3 us
  starting transfers between devices: 26.1 us -> 9.4 us
  Pallas kernels: 42 us -> 33.1 us
  local copies, waits for them, and re-layouts: 6.74 us -> 1.48 us
  other arithmetic: 2.49 us -> 0.84 us
    all_to_all x0 -> x1, blocking collectives: none -> 21.3 us  [shards(): lax.all_to_all(jnp.broadcast_to(own[None, None], (devices, 1, LANES)), GR...]
    all_to_all x1 -> x0, starting transfers between devices: 11.5 us -> none  [shards(): lax.all_to_all(jnp.broadcast_to(own[None, None], (devices, 1, LANES)), GR...]
    all_to_all x1, starting transfers between devices: 9.78 us -> 4.51 us  [shards(): lax.all_to_all(message.reshape(devices, pair_count * ROWS, LANES), GRP_WA...]
    pallas_call x1 -> x0, Pallas kernels: 3.79 us -> none  [shards(): pl.pallas_call(functools.partial(permute_kernel, pair_count), in_specs=[s...]
    pallas_call x1, Pallas kernels: 14 us -> 10.9 us  [shards(): pl.pallas_call(functools.partial(final_kernel, (levels, slot_count, slot_...]
    broadcast_in_dim x5 -> x0, local copies, waits for them, and re-layouts: 3.06 us -> none  [the longest x2 2.32 us: shards(): order_rows = jnp.broadcast_to(order_rows, (devices * ROWS, LANES))]
    pallas_call x1, Pallas kernels: 16 us -> 13.7 us  [shards(): pl.pallas_call(functools.partial(rhs_kernel, (levels, slot_count, slot_wi...]
  transfers between devices with their start and end apart: 3 -> 2, of which waited for: 2 -> 2; matrix products, arithmetic and copies ran while one was open for 4% -> 2% of each run, Pallas kernels for 11% -> 0%
where the time goes in v2:
time: 133 us; the launch traced here: 132 us
  waiting for transfers between devices  64 us (48%)
  Pallas kernels  33.1 us (25%)
  blocking collectives  21.3 us (16%)
  starting transfers between devices  9.4 us (7%)
  matrix products  1.96 us (1%)
  local copies, waits for them, and re-layouts  1.48 us (1%)
    all_to_all x1, waiting for transfers between devices, shards(): lax.all_to_all(solved.reshape(devices, pair_count * ROWS, LANES), GRP_WAV...  32.8 us
    all_to_all x1, waiting for transfers between devices, shards(): lax.all_to_all(message.reshape(devices, pair_count * ROWS, LANES), GRP_WA...  31.2 us
    all_to_all x1, blocking collectives, shards(): lax.all_to_all(jnp.broadcast_to(own[None, None], (devices, 1, LANES)), GR...  21.3 us
    pallas_call x1, Pallas kernels, shards(): pl.pallas_call(functools.partial(rhs_kernel, (levels, slot_count, slot_wi...  13.7 us
    pallas_call x1, Pallas kernels, shards(): pl.pallas_call(functools.partial(final_kernel, (levels, slot_count, slot_...  10.9 us
    pallas_call x1, Pallas kernels, shards(): pl.pallas_call(functools.partial(solve_kernel, (levels, slot_count)), gri...  8.44 us
    all_to_all x1, starting transfers between devices, shards(): lax.all_to_all(solved.reshape(devices, pair_count * ROWS, LANES), GRP_WAV...  4.89 us
    all_to_all x1, starting transfers between devices, shards(): lax.all_to_all(message.reshape(devices, pair_count * ROWS, LANES), GRP_WA...  4.51 us
  transfers between devices with their start and end apart: 2, of which 2 were waited for; matrix products, arithmetic and copies ran while one was open for 2% of the time, Pallas kernels for 0%

profile of v2, /device:TPU:1, one launch (start us, length us, event | category | flops | bytes accessed | tf_op | source)
XLA Modules:
  0.0 132.1 jit_solution(11362759669977081275)
XLA Ops:
  0.0 0.0 copy-start
  0.0 0.8 pad_add_fusion
  0.8 21.3 %all_to_all.15 = s32[128,1,128]{2,1,0:T(1,128)} all-to-all(s32[128,1,128]{2,1,0:T(1,128)S(1)} %broadcast_in_dim.2), channel_id=1, replica_groups=mesh['grp'=4,'wave_0'=4,'wave_1'=4,'wave_2'=2] {'grp','wave_0','wave_1',..., dimensions={0} | all-to-all | bytes 131072 | tf_op jit(solution)/shard_map/all_to_all | solution.py:312
  22.1 13.7 %right_side.1 = bf16[384,24,128]{2,1,0:T(8,128)(2,1)} custom-call(s32[128,128]{1,0:T(8,128)} %bitcast.16, s32[5]{0:T(128)} %orders_ref.3, bf16[275,7690]{1,0:T(8,128)(2,1)} %state_ref.3, bf16[137,137]{1,0:T(8,128)(2,1)} %height_ref.1, bf16[137]{0:T(256)(128)(2,1)} %pressure_ref.1, bf16[137,275]{1,0:T(8,128)(2,1)} %constant.12.clone.place_ref, ...), custom_call_target="tpu_custom_call" | custom-call | tf_op jit(solution)/shard_map/right_side/pallas_call | solution.py:325
  35.8 0.0 copy-start.7
  35.8 4.5 %all-to-all-start.1 = ((bf16[128,72,128]{2,1,0:T(8,128)(2,1)}), bf16[128,72,128]{2,1,0:T(8,128)(2,1)S(1)}, u32[]{:S(2)}, u32[]{:S(2)}) async-start(bf16[128,72,128]{2,1,0:T(8,128)(2,1)} %bitcast.21), calls=%async_computation.1 | async-start | bytes 4718592 | tf_op jit(solution)/shard_map/all_to_all | solution.py:345
  40.4 0.0 copy-done
  40.4 0.0 copy-done.7
  40.4 1.8 %convolution_convert_fusion.weights_ref = bf16[3,2,256,256]{3,2,1,0:T(8,128)(2,1)} fusion(bf16[256,137,1,1]{0,1,3,2:T(8,128)(2,1)S(1)} %copy-done.7, bf16[3,2,137,137]{3,1,2,0:T(2,128)(2,1)S(1)} %copy-done), kind=kOutput, calls=%fused_computation | convolution fusion | flops 166003200 | bytes 1081804 | tf_op jit(solution)/shard_map/jtak,bk->jtab/dot_general | solution.py:350
  42.2 31.2 %all-to-all-done.1 = bf16[128,72,128]{2,1,0:T(8,128)(2,1)S(1)} async-done(((bf16[128,72,128]{2,1,0:T(8,128)(2,1)}), bf16[128,72,128]{2,1,0:T(8,128)(2,1)S(1)}, u32[]{:S(2)}, u32[]{:S(2)}) %all-to-all-start.1) | async-done | bytes 2359328 | tf_op jit(solution)/shard_map/all_to_all | solution.py:345
  73.3 0.0 copy-start.3
  73.3 1.4 %copy-done.3 = bf16[128,72,128]{2,1,0:T(8,128)(2,1)} copy-done((bf16[128,72,128]{2,1,0:T(8,128)(2,1)}, bf16[128,72,128]{2,1,0:T(8,128)(2,1)S(1)}, u32[]{:S(2)}) %copy-start.3) | copy-done | bytes 2359320
  74.7 8.4 %solve.1 = bf16[128,3,24,128]{3,2,1,0:T(8,128)(2,1)} custom-call(s32[3]{0:T(128)} %lows_ref.1, s32[128,128]{1,0:T(8,128)} %bitcast.17, bf16[128,3,24,128]{3,2,1,0:T(8,128)(2,1)} %bitcast.20, bf16[3,2,256,256]{3,2,1,0:T(8,128)(2,1)} %convolution_convert_fusion.weights_ref), custom_call_target="tpu_custom_call" | custom-call | tf_op jit(solution)/shard_map/solve/pallas_call | solution.py:353
  83.2 0.0 copy-start.5
  83.2 0.0 copy-start.4
  83.2 0.0 copy-start.6
  83.2 0.0 copy-start.1
  83.2 0.0 copy-start.2
  83.2 4.9 %all-to-all-start.2 = ((bf16[128,72,128]{2,1,0:T(8,128)(2,1)}), bf16[128,72,128]{2,1,0:T(8,128)(2,1)S(1)}, u32[]{:S(2)}, u32[]{:S(2)}) async-start(bf16[128,72,128]{2,1,0:T(8,128)(2,1)} %bitcast.19), calls=%async_computation.2 | async-start | bytes 4718592 | tf_op jit(solution)/shard_map/all_to_all | solution.py:368
  88.1 0.0 copy-done.5
  88.1 0.0 copy-done.4
  88.2 0.0 copy-done.6
  88.2 0.2 convolution_convert_fusion.2.weights_ref
  88.4 32.8 %all-to-all-done.2 = bf16[128,72,128]{2,1,0:T(8,128)(2,1)S(1)} async-done(((bf16[128,72,128]{2,1,0:T(8,128)(2,1)}), bf16[128,72,128]{2,1,0:T(8,128)(2,1)S(1)}, u32[]{:S(2)}, u32[]{:S(2)}) %all-to-all-start.2) | async-done | bytes 2359328 | tf_op jit(solution)/shard_map/all_to_all | solution.py:368
  121.2 0.0 copy-done.1
  121.2 0.0 copy-done.2
  121.2 10.9 %final.1 = bf16[275,7690]{1,0:T(8,128)(2,1)} custom-call(s32[128,128]{1,0:T(8,128)S(1)} %bitcast.18, s32[5]{0:T(128)S(1)} %copy-done.2, bf16[384,24,128]{2,1,0:T(8,128)(2,1)S(1)} %bitcast.15, bf16[275,7690]{1,0:T(8,128)(2,1)} %state_ref.3, bf16[275,256]{1,0:T(8,128)(2,1)S(1)} %convolution_convert_fusion.2.weights_ref), custom_call_target="tpu_custom_call" | custom-call | tf_op jit(solution)/shard_map/final/pallas_call | solution.py:376
  (6 shorter events, 0.1 us)
Async XLA Ops:
  0.0 40.4 %copy-start = (bf16[3,2,137,137]{3,1,2,0:T(2,128)(2,1)S(1)}, bf16[3,2,137,137]{3,1,2,0:T(2,128)(2,1)}, u32[]{:S(2)}) copy-start(bf16[3,2,137,137]{3,1,2,0:T(2,128)(2,1)} %param.15) | copy-start | bytes 675688
  35.8 4.5 %copy-start.7 = (bf16[256,137,1,1]{0,1,3,2:T(8,128)(2,1)S(1)}, bf16[256,137,1,1]{0,1,3,2:T(8,128)(2,1)}, u32[]{:S(2)}) copy-start(bf16[256,137,1,1]{0,1,3,2:T(8,128)(2,1)} %constant.20) | copy-start | bytes 210436
  35.8 37.5 %all-to-all-start.1 = ((bf16[128,72,128]{2,1,0:T(8,128)(2,1)}), bf16[128,72,128]{2,1,0:T(8,128)(2,1)S(1)}, u32[]{:S(2)}, u32[]{:S(2)}) async-start(bf16[128,72,128]{2,1,0:T(8,128)(2,1)} %bitcast.21), calls=%async_computation.1 | async-start | bytes 4718592 | tf_op jit(solution)/shard_map/all_to_all | solution.py:345
  73.3 1.4 %copy-start.3 = (bf16[128,72,128]{2,1,0:T(8,128)(2,1)}, bf16[128,72,128]{2,1,0:T(8,128)(2,1)S(1)}, u32[]{:S(2)}) copy-start(bf16[128,72,128]{2,1,0:T(8,128)(2,1)S(1)} %all-to-all-done.1) | copy-start | bytes 7077892
  83.2 4.9 %copy-start.5 = (bf16[137]{0:T(256)(128)(2,1)S(1)}, bf16[137]{0:T(256)(128)(2,1)}, u32[]{:S(2)}) copy-start(bf16[137]{0:T(256)(128)(2,1)} %param.19) | copy-start | bytes 826
  83.2 5.0 %copy-start.4 = (bf16[137,137]{1,0:T(8,128)(2,1)S(1)}, bf16[137,137]{1,0:T(8,128)(2,1)}, u32[]{:S(2)}) copy-start(bf16[137,137]{1,0:T(8,128)(2,1)} %param.18) | copy-start | bytes 112618
  83.2 5.0 %copy-start.6 = (bf16[256,137]{0,1:T(8,128)(2,1)S(1)}, bf16[256,137]{0,1:T(8,128)(2,1)}, u32[]{:S(2)}) copy-start(bf16[256,137]{0,1:T(8,128)(2,1)} %constant.10.clone) | copy-start | bytes 210436
  83.2 38.0 %copy-start.1 = (s32[128,1,128]{2,1,0:T(1,128)S(1)}, s32[128,1,128]{2,1,0:T(1,128)}, u32[]{:S(2)}) copy-start(s32[128,1,128]{2,1,0:T(1,128)} %all_to_all.15) | copy-start | bytes 196612
  83.2 38.0 %copy-start.2 = (s32[5]{0:T(128)S(1)}, s32[5]{0:T(128)}, u32[]{:S(2)}) copy-start(s32[5]{0:T(128)} %orders_ref.3) | copy-start | bytes 64
  83.2 38.0 %all-to-all-start.2 = ((bf16[128,72,128]{2,1,0:T(8,128)(2,1)}), bf16[128,72,128]{2,1,0:T(8,128)(2,1)S(1)}, u32[]{:S(2)}, u32[]{:S(2)}) async-start(bf16[128,72,128]{2,1,0:T(8,128)(2,1)} %bitcast.19), calls=%async_computation.2 | async-start | bytes 4718592 | tf_op jit(solution)/shard_map/all_to_all | solution.py:368

commit v3 on v2

--- a/solution.py
+++ b/solution.py
@@ -64,45 +64,41 @@
     um,
     ue,
 ):
-    levels, slot_count, slot_width, truncation, pair_count = sizes
+    levels, slot_count, slot_width, truncation, pair_count, streams = sizes
     half = (truncation + 1) // 2
     step = pl.program_id(0)
-    padded = spread_ref.shape[1]
 
     @pl.when(step == 0)
     def _():
         moved = jnp.dot(height_ref[...], place_ref[...], preferred_element_type=jnp.float32)
         row = jnp.broadcast_to(pressure_ref[...].reshape(1, levels), (LANES, levels))
         column = lax.dot_general(
-            eye_ref[:levels, :levels], row, (((1,), (1,)), ((), ())),
+            eye_ref[:levels, :levels],
+            row,
+            (((1,), (1,)), ((), ())),
             preferred_element_type=jnp.float32,
         )
-        last = lax.broadcasted_iota(jnp.int32, moved.shape, 1) == 2 * levels
+        last = lax.broadcasted_iota(jnp.int32, moved.shape, 1) == moved.shape[1] - 1
         moved = jnp.where(last, column[:, :1], moved).astype(jnp.bfloat16)
         drive[...] = jnp.zeros_like(drive)
         drive[:levels, :] = moved
 
-    columns = step * TILE + lax.broadcasted_iota(jnp.int32, (1, TILE), 1)
-    order, coeff = slot_lines(columns, orders_ref, slot_count, slot_width)
-    degree = jnp.where(coeff <= truncation - order, order + coeff, coeff - 1)
-    lap = (degree * (degree + 1)).astype(jnp.float32) / float(truncation * (truncation + 1))
-    pull = jnp.dot(drive[...], state_ref[...], preferred_element_type=jnp.float32)
-    right = state_ref[:padded, :].astype(jnp.float32) + lap * pull
-    right = jnp.where(columns < slot_count * slot_width, right, 0.0).astype(jnp.bfloat16)
-    spread = jnp.dot(spread_ref[...], right, preferred_element_type=jnp.float32)
-    spread = spread.astype(jnp.bfloat16)
-    for k in range(TILE // 256):
-        lines = lax.dot_general(
-            eye_ref[...],
-            spread[:, 256 * k : 256 * (k + 1)],
-            (((1,), (1,)), ((), ())),
-            preferred_element_type=jnp.float32,
-        )
-        start = pl.multiple_of(FRONT + step * TILE + 256 * k, 256)
-        xm[pl.ds(start, 256), :] = lines[:, :LANES]
-        xe[pl.ds(start, 256), :] = lines[:, LANES:]
-
-    @pl.when(step == pl.num_programs(0) - 1)
+    @pl.when(step < streams)
+    def _():
+        columns = step * TILE + lax.broadcasted_iota(jnp.int32, (1, TILE), 1)
+        order, coeff = slot_lines(columns, orders_ref, slot_count, slot_width)
+        degree = jnp.where(coeff <= truncation - order, order + coeff, coeff - 1)
+        lap = (degree * (degree + 1)).astype(jnp.float32) / float(truncation * (truncation + 1))
+        padded = drive.shape[0]
+        pull = jnp.dot(drive[...], state_ref[LANES:, :], preferred_element_type=jnp.float32)
+        right = state_ref[:padded, :].astype(jnp.float32) + lap * pull
+        right = right.astype(jnp.bfloat16)
+        edge = jnp.dot(spread_ref[...], right[LANES:], preferred_element_type=jnp.float32)
+        start = pl.multiple_of(FRONT + step * TILE, 256)
+        xm[pl.ds(start, TILE), :] = jnp.transpose(right[:LANES].astype(jnp.float32))
+        xe[pl.ds(start, TILE), :] = jnp.transpose(edge)
+
+    @pl.when(step == streams)
     def _():
         def regroup(s, carry):
             order = jnp.maximum(orders_ref[s], 0)
@@ -129,15 +125,20 @@
             return carry
 
         lax.fori_loop(0, slot_count, regroup, 0)
+
+    @pl.when(step >= streams)
+    def _():
         row = lax.broadcasted_iota(jnp.int32, (16, LANES), 0)
         order_rows = jnp.full((16, LANES), BIG, jnp.int32)
         for s in range(slot_count):
             order_rows = jnp.where(row // 2 == s, jnp.maximum(orders_ref[s], 0), order_rows)
         mask = edge_masks(slot_count, levels - LANES, (ROWS, LANES), 0)
         tail = lax.broadcasted_iota(jnp.int32, (8, LANES), 0) >= 6
+        count = out_ref.shape[0] // pair_count
+        first = (step - streams) * count
 
         def assemble(d, j):
-            n = index_ref[d, j]
+            n = index_ref[first + d, j]
             start = UP * (half - 1 - n)
             low = LOW * n
             body = um[pl.ds(start, ROWS), :]
@@ -161,7 +162,7 @@
                 assemble(d, j)
             return carry
 
-        lax.fori_loop(0, half // pair_count, assemble_all, 0, unroll=2)
+        lax.fori_loop(0, count, assemble_all, 0, unroll=2)
 
 
 def solve_kernel(sizes, lows_ref, index_ref, blocks_ref, weights_ref, out_ref):
@@ -170,47 +171,66 @@
     shape = (count, ROWS, LANES)
     mask = edge_masks(slot_count, levels - LANES, shape, 1)
     row = lax.broadcasted_iota(jnp.int32, shape, 1)
-    slot = lax.broadcasted_iota(jnp.int32, (ROWS, LANES), 0) // 2
+    slot = lax.broadcasted_iota(jnp.int32, (16, LANES), 0) // 2
     orders = []
     for k in range(count):
-        lines = jnp.full((ROWS, LANES), BIG, jnp.int32)
+        lines = jnp.full((16, LANES), BIG, jnp.int32)
         for s in range(slot_count):
             order = index_ref[pl.program_id(0) * count + k, pair_count + s]
             lines = jnp.where(slot == s, order, lines)
         orders.append(lines)
-    orders = jnp.concatenate(orders, axis=0)
+    orders = jnp.stack(orders)
     for j in range(pair_count):
         body = blocks_ref[:, j].astype(jnp.float32)
         edge = jnp.where(row % 2 == 0, body[:, ROWS - 2 : ROWS - 1], body[:, ROWS - 1 :])
         edge = jnp.where(mask, edge, 0.0)
-        lines = jnp.concatenate([body, edge], axis=-1).reshape(count * ROWS, 2 * LANES)
-        lines = lines.astype(jnp.bfloat16)
+        lines = jnp.concatenate([body, edge], axis=-1)
+        top = lines[:, :16].reshape(count * 16, 2 * LANES).astype(jnp.bfloat16)
+        lines = lines.reshape(count * ROWS, 2 * LANES).astype(jnp.bfloat16)
         upper = jnp.dot(lines, weights_ref[j, 1], preferred_element_type=jnp.float32)
-        lower = jnp.dot(lines, weights_ref[j, 0], preferred_element_type=jnp.float32)
+        upper = upper.reshape(count, ROWS, 2 * LANES)
+        lower = jnp.dot(top, weights_ref[j, 0], preferred_element_type=jnp.float32)
+        lower = lower.reshape(count, 16, 2 * LANES)
         own = orders <= lows_ref[j]
-        main = jnp.where(own, lower[:, :LANES], upper[:, :LANES]).reshape(shape)
-        edge = jnp.where(own, lower[:, LANES:], upper[:, LANES:]).reshape(shape)
-        edge = jnp.where(mask, edge, 0.0)
-        folded = parity_fold([edge[:, :8], edge[:, 8:16], edge[:, 16:]], 1)
-        folded = jnp.concatenate([folded, folded, folded], axis=1)
-        out_ref[:, j] = jnp.where(row >= ROWS - 2, folded, main).astype(jnp.bfloat16)
+        main = jnp.where(own, lower[..., :LANES], upper[:, :16, :LANES])
+        edge = jnp.where(own, lower[..., LANES:], upper[:, :16, LANES:])
+        edge = jnp.where(mask[:, :16], edge, 0.0)
+        rest = jnp.where(mask[:, 16:], upper[:, 16:, LANES:], 0.0)
+        folded = parity_fold([edge[:, :8], edge[:, 8:], rest], 1)
+        rest = jnp.where(row[:, 16:] >= ROWS - 2, folded, upper[:, 16:, :LANES])
+        out_ref[:, j] = jnp.concatenate([main, rest], axis=1).astype(jnp.bfloat16)
 
 
 def final_kernel(
-    sizes, index_ref, orders_ref, blocks_ref, state_ref, weights_ref, out_ref, xm, xe, lm, le, um, ue
+    sizes,
+    index_ref,
+    orders_ref,
+    blocks_ref,
+    state_ref,
+    last_ref,
+    weights_ref,
+    out_ref,
+    xm,
+    xe,
+    lm,
+    le,
+    um,
+    ue,
 ):
-    levels, slot_count, slot_width, truncation, pair_count = sizes
+    levels, slot_count, slot_width, truncation, pair_count, streams = sizes
     half = (truncation + 1) // 2
     step = pl.program_id(0)
 
-    @pl.when(step == 0)
+    @pl.when(step < streams)
     def _():
         mask = edge_masks(slot_count, levels - LANES, (ROWS, LANES), 0)
         even = lax.broadcasted_iota(jnp.int32, (ROWS, LANES), 0) % 2 == 0
+        count = blocks_ref.shape[0] // pair_count
+        first = step * count
 
         def unfold(d, carry):
             for j in range(pair_count):
-                n = index_ref[d, j]
+                n = index_ref[first + d, j]
                 body = blocks_ref[d * pair_count + j].astype(jnp.float32)
                 edge = jnp.where(even, body[ROWS - 2 : ROWS - 1], body[ROWS - 1 :])
                 edge = jnp.where(mask, edge, 0.0)
@@ -222,8 +242,10 @@
                 le[pl.ds(low, 16), :] = edge[:16]
             return carry
 
-        lax.fori_loop(0, half // pair_count, unfold, 0, unroll=2)
-
+        lax.fori_loop(0, count, unfold, 0, unroll=2)
+
+    @pl.when(step == streams)
+    def _():
         def regroup(k, carry):
             s = slot_count - 1 - k
             order = jnp.maximum(orders_ref[s], 0)
@@ -247,19 +269,30 @@
 
         lax.fori_loop(0, slot_count, regroup, 0)
 
-    start = pl.multiple_of(FRONT + step * TILE, 256)
-    lines = jnp.concatenate([xm[pl.ds(start, TILE), :], xe[pl.ds(start, TILE), :]], axis=1)
-    moved = lax.dot_general(
-        weights_ref[...],
-        lines.astype(jnp.bfloat16),
-        (((1,), (1,)), ((), ())),
-        preferred_element_type=jnp.float32,
-    )
-    columns = step * TILE + lax.broadcasted_iota(jnp.int32, (1, TILE), 1)
-    order, _ = slot_lines(columns, orders_ref, slot_count, slot_width)
-    kept = lax.broadcasted_iota(jnp.int32, (state_ref.shape[0], 1), 0) >= levels
-    base = jnp.where(kept, state_ref[...].astype(jnp.float32), 0.0)
-    out_ref[...] = jnp.where(order >= 0, base + moved, 0.0).astype(jnp.bfloat16)
+    @pl.when(step >= streams)
+    def _():
+        tile = step - streams
+        start = pl.multiple_of(FRONT + tile * TILE, 256)
+        lines = jnp.concatenate([xm[pl.ds(start, TILE), :], xe[pl.ds(start, TILE), :]], axis=1)
+        moved = lax.dot_general(
+            weights_ref[...],
+            lines.astype(jnp.bfloat16),
+            (((1,), (1,)), ((), ())),
+            preferred_element_type=jnp.float32,
+        )
+        columns = tile * TILE + lax.broadcasted_iota(jnp.int32, (1, TILE), 1)
+        order, _ = slot_lines(columns, orders_ref, slot_count, slot_width)
+        moved = jnp.where(order >= 0, moved, 0.0)
+        head = state_ref.shape[0]
+        split = 2 * head
+        held = lax.broadcasted_iota(jnp.int32, (head, 1), 0) >= levels - head
+        held = held & (order >= 0)
+        kept = jnp.where(held, state_ref[...].astype(jnp.float32), 0.0)
+        out_ref[:head, :] = moved[:head].astype(jnp.bfloat16)
+        out_ref[head:split, :] = (kept + moved[head:split]).astype(jnp.bfloat16)
+        rest = out_ref.shape[0] - split
+        kept = jnp.where(order >= 0, last_ref[:rest, :].astype(jnp.float32), 0.0)
+        out_ref[split:, :] = (kept + moved[split:]).astype(jnp.bfloat16)
 
 
 def level_of_lane(levels, slot_count):
@@ -315,29 +348,31 @@
 
     table = level_of_lane(levels, slot_count)
     padded = -(-levels // 16) * 16
-    spread = np.zeros((2 * LANES, padded), np.float32)
-    spread[:, :levels] = table
-    place = np.zeros((levels, rows), np.float32)
-    place[:, levels : 2 * levels] = np.eye(levels)
+    spread = np.zeros((LANES, padded - LANES), np.float32)
+    spread[:, : levels - LANES] = table[LANES:, LANES:]
+    place = np.zeros((levels, rows - LANES), np.float32)
+    place[:, levels - LANES : 2 * levels - LANES] = np.eye(levels)
     table, spread, place = (jnp.asarray(x, bf16) for x in (table, spread, place))
     eye = jnp.asarray(np.eye(256), bf16)
 
     message = pl.pallas_call(
-        functools.partial(rhs_kernel, (levels, slot_count, slot_width, truncation, pair_count)),
-        grid=(steps,),
+        functools.partial(rhs_kernel, (levels, slot_count, slot_width, truncation, pair_count, steps)),
+        grid=(2 * steps,),
         in_specs=[
             smem,
             smem,
-            pl.BlockSpec((rows, TILE), lambda i: (0, i)),
+            pl.BlockSpec((rows, TILE), lambda i: (0, jnp.minimum(i, steps - 1))),
             vmem,
             vmem,
             vmem,
             vmem,
             vmem,
         ],
-        out_specs=pl.BlockSpec((half, ROWS, LANES), lambda i: (0, 0, 0)),
+        out_specs=pl.BlockSpec(
+            (half // steps, ROWS, LANES), lambda i: (jnp.maximum(i - steps, 0), 0, 0)
+        ),
         out_shape=jax.ShapeDtypeStruct((half, ROWS, LANES), bf16),
-        scratch_shapes=[pltpu.VMEM((padded, rows), bf16)] + scratch,
+        scratch_shapes=[pltpu.VMEM((padded, rows - LANES), bf16)] + scratch,
         compiler_params=params(56),
         name="right_side",
     )(index, held_orders, state, height_operator, pressure_column, place, spread, eye)
@@ -361,7 +396,7 @@
         ],
         out_specs=pl.BlockSpec((chunk, pair_count, ROWS, LANES), lambda i: (i, 0, 0, 0)),
         out_shape=jax.ShapeDtypeStruct((devices, pair_count, ROWS, LANES), bf16),
-        compiler_params=params(54),
+        compiler_params=params(52),
         name="solve",
     )(pair_lows, index, arrived, weights)
 
@@ -369,26 +404,28 @@
         solved.reshape(devices, pair_count * ROWS, LANES), GRP_WAVE, 0, 0, tiled=True
     ).reshape(half, ROWS, LANES)
 
+    head = levels // 8 * 8
     response = jnp.concatenate(
         [jnp.eye(levels, dtype=bf16), -thermal_response_matrix, -mass_row[None, :]], axis=0
     )
     response = jnp.dot(response, table.T, preferred_element_type=f32).astype(bf16)
     return pl.pallas_call(
-        functools.partial(final_kernel, (levels, slot_count, slot_width, truncation, pair_count)),
-        grid=(steps,),
+        functools.partial(final_kernel, (levels, slot_count, slot_width, truncation, pair_count, steps)),
+        grid=(2 * steps,),
         in_specs=[
             smem,
             smem,
-            vmem,
-            pl.BlockSpec((rows, TILE), lambda i: (0, i)),
+            pl.BlockSpec((half // steps, ROWS, LANES), lambda i: (jnp.minimum(i, steps - 1), 0, 0)),
+            pl.BlockSpec((head, TILE), lambda i: (1, jnp.maximum(i - steps, 0))),
+            pl.BlockSpec((8, TILE), lambda i: (2 * head // 8, jnp.maximum(i - steps, 0))),
             vmem,
         ],
-        out_specs=pl.BlockSpec((rows, TILE), lambda i: (0, i)),
+        out_specs=pl.BlockSpec((rows, TILE), lambda i: (0, jnp.maximum(i - steps, 0))),
         out_shape=jax.ShapeDtypeStruct((rows, width), bf16),
         scratch_shapes=scratch,
         compiler_params=params(48),
         name="final",
-    )(index, held_orders, returned, state, response)
+    )(index, held_orders, returned, state, state, response)
 
 
 def solution(mesh):

time: 133 us -> 132 us (level)
  local copies, waits for them, and re-layouts: 1.48 us -> 0.08 us
    unnamed x16, local copies, waits for them, and re-layouts: 1.43 us -> 0.04 us
  transfers between devices with their start and end apart: 2 -> 2, of which waited for: 2 -> 2; matrix products, arithmetic and copies ran while one was open for 2% -> 1% of each run, Pallas kernels for 0% -> 0%
where the time goes in v3:
time: 132 us
  waiting for transfers between devices  64.6 us (49%)
  Pallas kernels  33.1 us (25%)
  blocking collectives  21.3 us (16%)
  starting transfers between devices  10.3 us (8%)
    all_to_all x1, waiting for transfers between devices, shards(): lax.all_to_all(solved.reshape(devices, pair_count * ROWS, LANES), GRP_WAV...  32.8 us
    all_to_all x1, waiting for transfers between devices, shards(): lax.all_to_all(message.reshape(devices, pair_count * ROWS, LANES), GRP_WA...  31.9 us
    all_to_all x1, blocking collectives, shards(): lax.all_to_all(jnp.broadcast_to(own[None, None], (devices, 1, LANES)), GR...  21.3 us
    pallas_call x1, Pallas kernels, shards(): pl.pallas_call(functools.partial(rhs_kernel, (levels, slot_count, slot_wi...  13.8 us
    pallas_call x1, Pallas kernels, shards(): pl.pallas_call(functools.partial(final_kernel, (levels, slot_count, slot_...  11.3 us
    pallas_call x1, Pallas kernels, shards(): pl.pallas_call(functools.partial(solve_kernel, (levels, slot_count)), gri...  8.07 us
    all_to_all x1, starting transfers between devices, shards(): lax.all_to_all(message.reshape(devices, pair_count * ROWS, LANES), GRP_WA...  5.44 us
    all_to_all x1, starting transfers between devices, shards(): lax.all_to_all(solved.reshape(devices, pair_count * ROWS, LANES), GRP_WAV...  4.89 us
  transfers between devices with their start and end apart: 2, of which 2 were waited for; matrix products, arithmetic and copies ran while one was open for 1% of the time, Pallas kernels for 0%

profile of v3, /device:TPU:1, one launch (start us, length us, event | category | flops | bytes accessed | tf_op | source)
XLA Modules:
  0.0 131.5 jit_solution(10727562679892212149)
XLA Ops:
  0.0 0.0 copy-start
  0.0 0.8 pad_add_fusion
  0.8 21.3 %all_to_all.15 = s32[128,1,128]{2,1,0:T(1,128)} all-to-all(s32[128,1,128]{2,1,0:T(1,128)S(1)} %broadcast_in_dim.2), channel_id=1, replica_groups=mesh['grp'=4,'wave_0'=4,'wave_1'=4,'wave_2'=2] {'grp','wave_0','wave_1',..., dimensions={0} | all-to-all | bytes 131072 | tf_op jit(solution)/shard_map/all_to_all | solution.py:345
  22.1 13.8 %right_side.1 = bf16[384,24,128]{2,1,0:T(8,128)(2,1)} custom-call(s32[128,128]{1,0:T(8,128)} %bitcast.16, s32[5]{0:T(128)} %orders_ref.3, bf16[275,7690]{1,0:T(8,128)(2,1)} %last_ref.1, bf16[137,137]{1,0:T(8,128)(2,1)} %height_ref.1, bf16[137]{0:T(256)(128)(2,1)} %pressure_ref.1, bf16[137,147]{1,0:T(8,128)(2,1)} %constant.12.clone.place_ref, ...), custom_call_target="tpu_custom_call" | custom-call | tf_op jit(solution)/shard_map/right_side/pallas_call | solution.py:358
  36.0 0.0 copy-start.7
  36.0 0.0 copy-start.1
  36.0 0.0 copy-start.3
  36.0 5.4 %all-to-all-start.1 = ((bf16[128,72,128]{2,1,0:T(8,128)(2,1)}), bf16[128,72,128]{2,1,0:T(8,128)(2,1)}, u32[]{:S(2)}, u32[]{:S(2)}) async-start(bf16[128,72,128]{2,1,0:T(8,128)(2,1)} %bitcast.19), calls=%async_computation.1 | async-start | bytes 4718592 | tf_op jit(solution)/shard_map/all_to_all | solution.py:380
  41.4 0.0 copy-done
  41.4 0.0 copy-done.7
  41.5 0.9 convolution_convert_fusion.weights_ref
  42.3 31.9 %all-to-all-done.1 = bf16[128,72,128]{2,1,0:T(8,128)(2,1)} async-done(((bf16[128,72,128]{2,1,0:T(8,128)(2,1)}), bf16[128,72,128]{2,1,0:T(8,128)(2,1)}, u32[]{:S(2)}, u32[]{:S(2)}) %all-to-all-start.1) | async-done | bytes 2359328 | tf_op jit(solution)/shard_map/all_to_all | solution.py:380
  74.2 0.0 copy-done.1
  74.2 0.0 copy-done.3
  74.2 8.1 %solve.1 = bf16[128,3,24,128]{3,2,1,0:T(8,128)(2,1)} custom-call(s32[3]{0:T(128)S(1)} %copy-done.3, s32[128,128]{1,0:T(8,128)S(1)} %bitcast.17, bf16[128,3,24,128]{3,2,1,0:T(8,128)(2,1)} %bitcast.2.blocks_ref, bf16[3,2,256,256]{3,2,1,0:T(8,128)(2,1)S(1)} %convolution_convert_fusion.weights_ref), custom_call_target="tpu_custom_call" | custom-call | tf_op jit(solution)/shard_map/solve/pallas_call | solution.py:388
  82.3 0.0 copy-start.5
  82.3 0.0 copy-start.4
  82.3 0.0 copy-start.6
  82.3 0.0 copy-start.2
  82.3 4.9 %all-to-all-start.2 = ((bf16[128,72,128]{2,1,0:T(8,128)(2,1)}), bf16[128,72,128]{2,1,0:T(8,128)(2,1)S(1)}, u32[]{:S(2)}, u32[]{:S(2)}) async-start(bf16[128,72,128]{2,1,0:T(8,128)(2,1)} %bitcast.20), calls=%async_computation.2 | async-start | bytes 4718592 | tf_op jit(solution)/shard_map/all_to_all | solution.py:403
  87.2 0.0 copy-done.5
  87.2 0.0 copy-done.4
  87.3 0.0 copy-done.6
  87.3 0.2 convolution_convert_fusion.2.weights_ref
  87.5 32.8 %all-to-all-done.2 = bf16[128,72,128]{2,1,0:T(8,128)(2,1)S(1)} async-done(((bf16[128,72,128]{2,1,0:T(8,128)(2,1)}), bf16[128,72,128]{2,1,0:T(8,128)(2,1)S(1)}, u32[]{:S(2)}, u32[]{:S(2)}) %all-to-all-start.2) | async-done | bytes 2359328 | tf_op jit(solution)/shard_map/all_to_all | solution.py:403
  120.2 0.0 copy-done.2
  120.2 11.3 %final.1 = bf16[275,7690]{1,0:T(8,128)(2,1)} custom-call(s32[128,128]{1,0:T(8,128)S(1)} %bitcast.18, s32[5]{0:T(128)S(1)} %copy-done.2, bf16[384,24,128]{2,1,0:T(8,128)(2,1)S(1)} %bitcast.15, bf16[275,7690]{1,0:T(8,128)(2,1)} %last_ref.1, bf16[275,7690]{1,0:T(8,128)(2,1)} %last_ref.1, bf16[275,256]{1,0:T(8,128)(2,1)S(1)} %convolution_convert_fusion.2.weights_ref), custom_call_target="tpu_custom_call" | custom-call | tf_op jit(solution)/shard_map/final/pallas_call | solution.py:412
  (6 shorter events, 0.1 us)
Async XLA Ops:
  0.0 41.4 %copy-start = (bf16[3,2,137,137]{3,1,2,0:T(2,128)(2,1)S(1)}, bf16[3,2,137,137]{3,1,2,0:T(2,128)(2,1)}, u32[]{:S(2)}) copy-start(bf16[3,2,137,137]{3,1,2,0:T(2,128)(2,1)} %param.15) | copy-start | bytes 675688
  36.0 5.5 %copy-start.7 = (bf16[256,137,1,1]{0,1,3,2:T(8,128)(2,1)S(1)}, bf16[256,137,1,1]{0,1,3,2:T(8,128)(2,1)}, u32[]{:S(2)}) copy-start(bf16[256,137,1,1]{0,1,3,2:T(8,128)(2,1)} %constant.20) | copy-start | bytes 210436
  36.0 38.2 %copy-start.1 = (s32[128,1,128]{2,1,0:T(1,128)S(1)}, s32[128,1,128]{2,1,0:T(1,128)}, u32[]{:S(2)}) copy-start(s32[128,1,128]{2,1,0:T(1,128)} %all_to_all.15) | copy-start | bytes 196612
  36.0 38.2 %copy-start.3 = (s32[3]{0:T(128)S(1)}, s32[3]{0:T(128)}, u32[]{:S(2)}) copy-start(s32[3]{0:T(128)} %lows_ref.1) | copy-start | bytes 40
  36.0 38.2 %all-to-all-start.1 = ((bf16[128,72,128]{2,1,0:T(8,128)(2,1)}), bf16[128,72,128]{2,1,0:T(8,128)(2,1)}, u32[]{:S(2)}, u32[]{:S(2)}) async-start(bf16[128,72,128]{2,1,0:T(8,128)(2,1)} %bitcast.19), calls=%async_computation.1 | async-start | bytes 4718592 | tf_op jit(solution)/shard_map/all_to_all | solution.py:380
  82.3 4.9 %copy-start.5 = (bf16[137]{0:T(256)(128)(2,1)S(1)}, bf16[137]{0:T(256)(128)(2,1)}, u32[]{:S(2)}) copy-start(bf16[137]{0:T(256)(128)(2,1)} %param.19) | copy-start | bytes 826
  82.3 5.0 %copy-start.4 = (bf16[137,137]{1,0:T(8,128)(2,1)S(1)}, bf16[137,137]{1,0:T(8,128)(2,1)}, u32[]{:S(2)}) copy-start(bf16[137,137]{1,0:T(8,128)(2,1)} %param.18) | copy-start | bytes 112618
  82.3 5.0 %copy-start.6 = (bf16[256,137]{0,1:T(8,128)(2,1)S(1)}, bf16[256,137]{0,1:T(8,128)(2,1)}, u32[]{:S(2)}) copy-start(bf16[256,137]{0,1:T(8,128)(2,1)} %constant.10.clone) | copy-start | bytes 210436
  82.3 38.0 %copy-start.2 = (s32[5]{0:T(128)S(1)}, s32[5]{0:T(128)}, u32[]{:S(2)}) copy-start(s32[5]{0:T(128)} %orders_ref.3) | copy-start | bytes 64
  82.3 38.0 %all-to-all-start.2 = ((bf16[128,72,128]{2,1,0:T(8,128)(2,1)}), bf16[128,72,128]{2,1,0:T(8,128)(2,1)S(1)}, u32[]{:S(2)}, u32[]{:S(2)}) async-start(bf16[128,72,128]{2,1,0:T(8,128)(2,1)} %bitcast.20), calls=%async_computation.2 | async-start | bytes 4718592 | tf_op jit(solution)/shard_map/all_to_all | solution.py:403

commit v4 on v3

--- a/solution.py
+++ b/solution.py
@@ -14,7 +14,8 @@
 LANES = 128
 ROWS = 24
 FRONT = 768
-TILE = 1024
+WORDS = 8
+TILE = 3968
 BIG = 1 << 20
 LOW = 17
 UP = 25
@@ -56,6 +57,8 @@
     spread_ref,
     eye_ref,
     out_ref,
+    near,
+    index_sem,
     drive,
     xm,
     xe,
@@ -67,9 +70,11 @@
     levels, slot_count, slot_width, truncation, pair_count, streams = sizes
     half = (truncation + 1) // 2
     step = pl.program_id(0)
+    fetch = pltpu.make_async_copy(index_ref, near, index_sem)
 
     @pl.when(step == 0)
     def _():
+        fetch.start()
         moved = jnp.dot(height_ref[...], place_ref[...], preferred_element_type=jnp.float32)
         row = jnp.broadcast_to(pressure_ref[...].reshape(1, levels), (LANES, levels))
         column = lax.dot_general(
@@ -100,6 +105,8 @@
 
     @pl.when(step == streams)
     def _():
+        fetch.wait()
+
         def regroup(s, carry):
             order = jnp.maximum(orders_ref[s], 0)
             base = FRONT + s * slot_width
@@ -138,7 +145,7 @@
         first = (step - streams) * count
 
         def assemble(d, j):
-            n = index_ref[first + d, j]
+            n = near[first + d, j]
             start = UP * (half - 1 - n)
             low = LOW * n
             body = um[pl.ds(start, ROWS), :]
@@ -176,7 +183,7 @@
     for k in range(count):
         lines = jnp.full((16, LANES), BIG, jnp.int32)
         for s in range(slot_count):
-            order = index_ref[pl.program_id(0) * count + k, pair_count + s]
+            order = index_ref[(pl.program_id(0) * count + k) * WORDS + pair_count + s]
             lines = jnp.where(slot == s, order, lines)
         orders.append(lines)
     orders = jnp.stack(orders)
@@ -230,7 +237,7 @@
 
         def unfold(d, carry):
             for j in range(pair_count):
-                n = index_ref[first + d, j]
+                n = index_ref[(first + d) * WORDS + j]
                 body = blocks_ref[d * pair_count + j].astype(jnp.float32)
                 edge = jnp.where(even, body[ROWS - 2 : ROWS - 1], body[ROWS - 1 :])
                 edge = jnp.where(mask, edge, 0.0)
@@ -359,7 +366,7 @@
         functools.partial(rhs_kernel, (levels, slot_count, slot_width, truncation, pair_count, steps)),
         grid=(2 * steps,),
         in_specs=[
-            smem,
+            pl.BlockSpec(memory_space=pl.ANY),
             smem,
             pl.BlockSpec((rows, TILE), lambda i: (0, jnp.minimum(i, steps - 1))),
             vmem,
@@ -372,7 +379,12 @@
             (half // steps, ROWS, LANES), lambda i: (jnp.maximum(i - steps, 0), 0, 0)
         ),
         out_shape=jax.ShapeDtypeStruct((half, ROWS, LANES), bf16),
-        scratch_shapes=[pltpu.VMEM((padded, rows - LANES), bf16)] + scratch,
+        scratch_shapes=[
+            pltpu.SMEM((devices, LANES), jnp.int32),
+            pltpu.SemaphoreType.DMA,
+            pltpu.VMEM((padded, rows - LANES), bf16),
+        ]
+        + scratch,
         compiler_params=params(56),
         name="right_side",
     )(index, held_orders, state, height_operator, pressure_column, place, spread, eye)
@@ -384,7 +396,8 @@
     weights = jnp.einsum("al,jtkl->jtak", table, inverses, preferred_element_type=f32)
     weights = jnp.einsum("jtak,bk->jtab", weights.astype(bf16), table, preferred_element_type=f32)
     weights = weights.astype(bf16)
-    chunk = 16
+    words = index[:, :WORDS].reshape(-1)
+    chunk = 64
     solved = pl.pallas_call(
         functools.partial(solve_kernel, (levels, slot_count)),
         grid=(devices // chunk,),
@@ -398,7 +411,7 @@
         out_shape=jax.ShapeDtypeStruct((devices, pair_count, ROWS, LANES), bf16),
         compiler_params=params(52),
         name="solve",
-    )(pair_lows, index, arrived, weights)
+    )(pair_lows, words, arrived, weights)
 
     returned = lax.all_to_all(
         solved.reshape(devices, pair_count * ROWS, LANES), GRP_WAVE, 0, 0, tiled=True
@@ -425,7 +438,7 @@
         scratch_shapes=scratch,
         compiler_params=params(48),
         name="final",
-    )(index, held_orders, returned, state, state, response)
+    )(words, held_orders, returned, state, state, response)
 
 
 def solution(mesh):

time: 132 us -> 120 us (0.909)
  Pallas kernels: 33.1 us -> 21.2 us
    pallas_call x1, Pallas kernels: 13.8 us -> 8.98 us  [shards(): pl.pallas_call(functools.partial(rhs_kernel, (levels, slot_count, slot_wi...]
    pallas_call x1, Pallas kernels: 11.3 us -> 7.33 us  [shards(): pl.pallas_call(functools.partial(final_kernel, (levels, slot_count, slot_...]
    pallas_call x1, Pallas kernels: 8.07 us -> 4.87 us  [shards(): pl.pallas_call(functools.partial(solve_kernel, (levels, slot_count)), gri...]
where the time goes in v4:
time: 120 us
  waiting for transfers between devices  64.5 us (54%)
  blocking collectives  21.3 us (18%)
  Pallas kernels  21.2 us (18%)
  starting transfers between devices  10.3 us (9%)
    all_to_all x1, waiting for transfers between devices, shards(): lax.all_to_all(solved.reshape(devices, pair_count * ROWS, LANES), GRP_WAV...  32.8 us
    all_to_all x1, waiting for transfers between devices, shards(): lax.all_to_all(message.reshape(devices, pair_count * ROWS, LANES), GRP_WA...  31.8 us
    all_to_all x1, blocking collectives, shards(): lax.all_to_all(jnp.broadcast_to(own[None, None], (devices, 1, LANES)), GR...  21.3 us
    pallas_call x1, Pallas kernels, shards(): pl.pallas_call(functools.partial(rhs_kernel, (levels, slot_count, slot_wi...  8.98 us
    pallas_call x1, Pallas kernels, shards(): pl.pallas_call(functools.partial(final_kernel, (levels, slot_count, slot_...  7.33 us
    all_to_all x1, starting transfers between devices, shards(): lax.all_to_all(message.reshape(devices, pair_count * ROWS, LANES), GRP_WA...  5.45 us
    all_to_all x1, starting transfers between devices, shards(): lax.all_to_all(solved.reshape(devices, pair_count * ROWS, LANES), GRP_WAV...  4.89 us
    pallas_call x1, Pallas kernels, shards(): pl.pallas_call(functools.partial(solve_kernel, (levels, slot_count)), gri...  4.87 us
  transfers between devices with their start and end apart: 2, of which 2 were waited for; matrix products, arithmetic and copies ran while one was open for 1% of the time, Pallas kernels for 0%

profile of v4, /device:TPU:1, one launch (start us, length us, event | category | flops | bytes accessed | tf_op | source)
XLA Modules:
  0.0 119.6 jit_solution(482410048194603558)
XLA Ops:
  0.0 0.0 copy-start
  0.0 0.8 pad_add_fusion
  0.8 21.3 %all_to_all.15 = s32[128,1,128]{2,1,0:T(1,128)} all-to-all(s32[128,1,128]{2,1,0:T(1,128)S(1)} %broadcast_in_dim.2), channel_id=1, replica_groups=mesh['grp'=4,'wave_0'=4,'wave_1'=4,'wave_2'=2] {'grp','wave_0','wave_1',..., dimensions={0} | all-to-all | bytes 131072 | tf_op jit(solution)/shard_map/all_to_all | solution.py:352
  22.1 9.0 %right_side.1 = bf16[384,24,128]{2,1,0:T(8,128)(2,1)} custom-call(s32[128,128]{1,0:T(8,128)} %bitcast.19, s32[5]{0:T(128)} %orders_ref.3, bf16[275,7690]{1,0:T(8,128)(2,1)} %last_ref.1, bf16[137,137]{1,0:T(8,128)(2,1)} %height_ref.1, bf16[137]{0:T(256)(128)(2,1)} %pressure_ref.1, bf16[137,147]{1,0:T(8,128)(2,1)} %constant.12.clone.place_ref, ...), custom_call_target="tpu_custom_call" | custom-call | tf_op jit(solution)/shard_map/right_side/pallas_call | solution.py:365
  31.1 0.0 copy-start.7
  31.2 0.0 copy-start.3
  31.2 0.0 copy-start.2
  31.2 5.4 %all-to-all-start.1 = ((bf16[128,72,128]{2,1,0:T(8,128)(2,1)}), bf16[128,72,128]{2,1,0:T(8,128)(2,1)}, u32[]{:S(2)}, u32[]{:S(2)}) async-start(bf16[128,72,128]{2,1,0:T(8,128)(2,1)} %bitcast.17), calls=%async_computation.1 | async-start | bytes 4718592 | tf_op jit(solution)/shard_map/all_to_all | solution.py:392
  36.6 0.0 copy-done
  36.6 0.0 copy-done.7
  36.7 0.9 convolution_convert_fusion.weights_ref
  37.5 0.0 copy-done.3
  37.5 0.1 reshape.23.index_ref
  37.6 31.8 %all-to-all-done.1 = bf16[128,72,128]{2,1,0:T(8,128)(2,1)} async-done(((bf16[128,72,128]{2,1,0:T(8,128)(2,1)}), bf16[128,72,128]{2,1,0:T(8,128)(2,1)}, u32[]{:S(2)}, u32[]{:S(2)}) %all-to-all-start.1) | async-done | bytes 2359328 | tf_op jit(solution)/shard_map/all_to_all | solution.py:392
  69.4 0.0 copy-done.2
  69.4 4.9 %solve.1 = bf16[128,3,24,128]{3,2,1,0:T(8,128)(2,1)} custom-call(s32[3]{0:T(128)S(1)} %copy-done.2, s32[1024]{0:T(1024)S(1)} %reshape.23.index_ref, bf16[128,3,24,128]{3,2,1,0:T(8,128)(2,1)} %bitcast.2.blocks_ref, bf16[3,2,256,256]{3,2,1,0:T(8,128)(2,1)S(1)} %convolution_convert_fusion.weights_ref), custom_call_target="tpu_custom_call" | custom-call | tf_op jit(solution)/shard_map/solve/pallas_call | solution.py:401
  74.3 0.0 copy-start.5
  74.3 0.0 copy-start.4
  74.3 0.0 copy-start.6
  74.3 0.0 copy-start.1
  74.3 4.9 %all-to-all-start.2 = ((bf16[128,72,128]{2,1,0:T(8,128)(2,1)}), bf16[128,72,128]{2,1,0:T(8,128)(2,1)S(1)}, u32[]{:S(2)}, u32[]{:S(2)}) async-start(bf16[128,72,128]{2,1,0:T(8,128)(2,1)} %bitcast.18), calls=%async_computation.2 | async-start | bytes 4718592 | tf_op jit(solution)/shard_map/all_to_all | solution.py:416
  79.2 0.0 copy-done.5
  79.2 0.0 copy-done.4
  79.3 0.0 copy-done.6
  79.3 0.2 convolution_convert_fusion.2.weights_ref
  79.5 32.8 %all-to-all-done.2 = bf16[128,72,128]{2,1,0:T(8,128)(2,1)S(1)} async-done(((bf16[128,72,128]{2,1,0:T(8,128)(2,1)}), bf16[128,72,128]{2,1,0:T(8,128)(2,1)S(1)}, u32[]{:S(2)}, u32[]{:S(2)}) %all-to-all-start.2) | async-done | bytes 2359328 | tf_op jit(solution)/shard_map/all_to_all | solution.py:416
  112.2 0.0 copy-done.1
  112.2 7.3 %final.1 = bf16[275,7690]{1,0:T(8,128)(2,1)} custom-call(s32[1024]{0:T(1024)S(1)} %reshape.23.index_ref, s32[5]{0:T(128)S(1)} %copy-done.1, bf16[384,24,128]{2,1,0:T(8,128)(2,1)S(1)} %bitcast.16, bf16[275,7690]{1,0:T(8,128)(2,1)} %last_ref.1, bf16[275,7690]{1,0:T(8,128)(2,1)} %last_ref.1, bf16[275,256]{1,0:T(8,128)(2,1)S(1)} %convolution_convert_fusion.2.weights_ref), custom_call_target="tpu_custom_call" | custom-call | tf_op jit(solution)/shard_map/final/pallas_call | solution.py:425
  (6 shorter events, 0.1 us)
Async XLA Ops:
  0.0 36.6 %copy-start = (bf16[3,2,137,137]{3,1,2,0:T(2,128)(2,1)S(1)}, bf16[3,2,137,137]{3,1,2,0:T(2,128)(2,1)}, u32[]{:S(2)}) copy-start(bf16[3,2,137,137]{3,1,2,0:T(2,128)(2,1)} %param.15) | copy-start | bytes 675688
  31.1 5.5 %copy-start.7 = (bf16[256,137,1,1]{0,1,3,2:T(8,128)(2,1)S(1)}, bf16[256,137,1,1]{0,1,3,2:T(8,128)(2,1)}, u32[]{:S(2)}) copy-start(bf16[256,137,1,1]{0,1,3,2:T(8,128)(2,1)} %constant.20) | copy-start | bytes 210436
  31.2 6.4 %copy-start.3 = (s32[128,1,128]{2,1,0:T(1,128)S(1)}, s32[128,1,128]{2,1,0:T(1,128)}, u32[]{:S(2)}) copy-start(s32[128,1,128]{2,1,0:T(1,128)} %all_to_all.15) | copy-start | bytes 196612
  31.2 38.2 %copy-start.2 = (s32[3]{0:T(128)S(1)}, s32[3]{0:T(128)}, u32[]{:S(2)}) copy-start(s32[3]{0:T(128)} %lows_ref.1) | copy-start | bytes 40
  31.2 38.2 %all-to-all-start.1 = ((bf16[128,72,128]{2,1,0:T(8,128)(2,1)}), bf16[128,72,128]{2,1,0:T(8,128)(2,1)}, u32[]{:S(2)}, u32[]{:S(2)}) async-start(bf16[128,72,128]{2,1,0:T(8,128)(2,1)} %bitcast.17), calls=%async_computation.1 | async-start | bytes 4718592 | tf_op jit(solution)/shard_map/all_to_all | solution.py:392
  74.3 4.9 %copy-start.5 = (bf16[137]{0:T(256)(128)(2,1)S(1)}, bf16[137]{0:T(256)(128)(2,1)}, u32[]{:S(2)}) copy-start(bf16[137]{0:T(256)(128)(2,1)} %param.19) | copy-start | bytes 826
  74.3 5.0 %copy-start.4 = (bf16[137,137]{1,0:T(8,128)(2,1)S(1)}, bf16[137,137]{1,0:T(8,128)(2,1)}, u32[]{:S(2)}) copy-start(bf16[137,137]{1,0:T(8,128)(2,1)} %param.18) | copy-start | bytes 112618
  74.3 5.0 %copy-start.6 = (bf16[256,137]{0,1:T(8,128)(2,1)S(1)}, bf16[256,137]{0,1:T(8,128)(2,1)}, u32[]{:S(2)}) copy-start(bf16[256,137]{0,1:T(8,128)(2,1)} %constant.10.clone) | copy-start | bytes 210436
  74.3 38.0 %copy-start.1 = (s32[5]{0:T(128)S(1)}, s32[5]{0:T(128)}, u32[]{:S(2)}) copy-start(s32[5]{0:T(128)} %orders_ref.3) | copy-start | bytes 64
  74.3 38.0 %all-to-all-start.2 = ((bf16[128,72,128]{2,1,0:T(8,128)(2,1)}), bf16[128,72,128]{2,1,0:T(8,128)(2,1)S(1)}, u32[]{:S(2)}, u32[]{:S(2)}) async-start(bf16[128,72,128]{2,1,0:T(8,128)(2,1)} %bitcast.18), calls=%async_computation.2 | async-start | bytes 4718592 | tf_op jit(solution)/shard_map/all_to_all | solution.py:416

commit v5 on v4

v5 whole, which is shorter than its diff:
```python
import functools

import jax
import jax.numpy as jnp
import numpy as np
from jax import lax
from jax.experimental import pallas as pl
from jax.experimental.pallas import tpu as pltpu
from jax.sharding import Mesh
from jax.sharding import PartitionSpec as P

GRP_WAVE = ("grp", "wave_0", "wave_1", "wave_2")

LANES = 128
ROWS = 24
FRONT = 768
WORDS = 8
TILE = 3840
PARTS = 4
BIG = 1 << 20
LOW = 17
UP = 25


def edge_masks(slot_count, edge, shape, row_dim):
    rows = lax.broadcasted_iota(jnp.int32, shape, row_dim)
    lanes = lax.broadcasted_iota(jnp.int32, shape, len(shape) - 1)
    group = rows // 2
    return (lanes >= edge * group) & (lanes < edge * (group + 1)) & (rows < 4 * slot_count + 2)


def parity_fold(parts, axis):
    total = parts[0]
    for part in parts[1:]:
        total = total + part
    total = total + pltpu.roll(total, 2, axis)
    return total + pltpu.roll(total, 4, axis)


def slot_lines(columns, orders_ref, slot_count, slot_width):
    order = jnp.full(columns.shape, -1, jnp.int32)
    place = columns
    for s in range(slot_count):
        inside = (columns >= s * slot_width) & (columns < (s + 1) * slot_width)
        order = jnp.where(inside, orders_ref[s], order)
        place = jnp.where(inside, columns - s * slot_width, place)
    return order, place // 2


def column_parts(width):
    starts = list(range(0, width - TILE // 2, TILE))
    return [(a, b - a) for a, b in zip(starts, starts[1:] + [width])]


def state_copies(state_ref, first, body, tail, sems):
    copies = []
    parts = column_parts(state_ref.shape[1])
    for k, (start, size) in enumerate(parts):
        source = state_ref.at[pl.ds(first, body.shape[0]), pl.ds(start, size)]
        target = tail if k == len(parts) - 1 else body.at[:, pl.ds(start, size)]
        copies.append(pltpu.make_async_copy(source, target, sems.at[k]))
    return copies


def rhs_kernel(
    sizes,
    index_ref,
    orders_ref,
    state_ref,
    height_ref,
    pressure_ref,
    out_ref,
    near,
    index_sem,
    height,
    height_sem,
    drive,
    body,
    tail,
    state_sems,
    stage,
    out_sems,
    xm,
    xe,
    lm,
    le,
    um,
    ue,
):
    levels, slot_count, slot_width, truncation, pair_count = sizes
    half = (truncation + 1) // 2
    parts = column_parts(state_ref.shape[1])
    bring = pltpu.make_async_copy(height_ref, height, height_sem)
    bring.start()
    copies = state_copies(state_ref, 0, body, tail, state_sems)
    for copy in copies:
        copy.start()
    fetch = pltpu.make_async_copy(index_ref, near, index_sem)
    fetch.start()

    edge_count = levels - LANES
    lane = lax.broadcasted_iota(jnp.int32, (LANES, drive.shape[0] - LANES), 0)
    group = jnp.zeros_like(lane)
    for g in range(1, 2 * slot_count + 2):
        group = group + jnp.where(lane >= edge_count * g, 1, 0)
    wanted = lax.broadcasted_iota(jnp.int32, lane.shape, 1) == lane - edge_count * group
    spread = jnp.where(wanted & (group <= 2 * slot_count), 1.0, 0.0).astype(jnp.bfloat16)
    column = jnp.broadcast_to(pressure_ref[...].reshape(1, levels).astype(jnp.float32), (8, levels))
    column = jnp.transpose(column)[:, :1]
    drive[...] = jnp.zeros_like(drive)
    last = drive.shape[1] - 1
    drive[:levels, last:] = column.astype(jnp.bfloat16)
    bring.wait()
    drive[:levels, last - levels : last] = height[...]
    padded = drive.shape[0]

    for k, (start, size) in enumerate(parts):
        copies[k].wait()
        if k == len(parts) - 1:
            upper, lower = tail[:padded, :], tail[LANES:, :]
        else:
            upper = body[:padded, start : start + size]
            lower = body[LANES:, start : start + size]
        columns = start + lax.broadcasted_iota(jnp.int32, (1, size), 1)
        order, coeff = slot_lines(columns, orders_ref, slot_count, slot_width)
        degree = jnp.where(coeff <= truncation - order, order + coeff, coeff - 1)
        lap = (degree * (degree + 1)).astype(jnp.float32) / float(truncation * (truncation + 1))
        pull = jnp.dot(drive[...], lower, preferred_element_type=jnp.float32)
        right = (upper.astype(jnp.float32) + lap * pull).astype(jnp.bfloat16)
        xm[pl.ds(FRONT + start, size), :] = jnp.transpose(right[:LANES].astype(jnp.float32))
        xe[pl.ds(FRONT + start, size), :] = lax.dot_general(
            jnp.transpose(right[LANES:].astype(jnp.float32)).astype(jnp.bfloat16),
            spread,
            (((1,), (1,)), ((), ())),
            preferred_element_type=jnp.float32,
        )

    def regroup(s, carry):
        order = jnp.maximum(orders_ref[s], 0)
        base = FRONT + s * slot_width
        for p in range(2):
            for x, low, up in ((xm, lm, um), (xe, le, ue)):
                up[pl.ds(2 * s + p, half, stride=UP), :] = x[
                    pl.ds(base + 2 * (half + 1) + p, half, stride=2), :
                ]
                low[pl.ds(2 * s + p, half, stride=LOW), :] = x[
                    pl.ds(base - 2 * order + p, half, stride=2), :
                ]
                up[pl.ds(2 * (slot_count + s) + p, half, stride=UP), :] = x[
                    pl.ds(base + 2 * (half - order) + p, half, stride=2), :
                ]

                @pl.when(orders_ref[s] >= 0)
                def _(x=x, up=up, p=p):
                    third = UP * (half - 1 - order) + 4 * slot_count + p
                    up[pl.ds(third, 1), :] = x[
                        pl.ds(base + 2 * (truncation + 1 - order) + p, 1), :
                    ]

        return carry

    lax.fori_loop(0, slot_count, regroup, 0)

    row = lax.broadcasted_iota(jnp.int32, (16, LANES), 0)
    order_rows = jnp.full((16, LANES), BIG, jnp.int32)
    for s in range(slot_count):
        order_rows = jnp.where(row // 2 == s, jnp.maximum(orders_ref[s], 0), order_rows)
    mask = edge_masks(slot_count, levels - LANES, (ROWS, LANES), 0)
    bottom = lax.broadcasted_iota(jnp.int32, (8, LANES), 0) >= 6

    def assemble(d, j):
        n = near[d, j]
        start = UP * (half - 1 - n)
        low = LOW * n
        lines = um[pl.ds(start, ROWS), :]
        edge = ue[pl.ds(start, ROWS), :]
        own = order_rows <= n
        top = jnp.where(own, lm[pl.ds(low, 16), :], lines[:16])
        top_edge = jnp.where(own, le[pl.ds(low, 16), :], edge[:16])
        folded = parity_fold(
            [
                jnp.where(mask[:8], top_edge[:8], 0.0),
                jnp.where(mask[8:16], top_edge[8:], 0.0),
                jnp.where(mask[16:], edge[16:], 0.0),
            ],
            0,
        )
        block = jnp.concatenate([top, jnp.where(bottom, folded, lines[16:])], axis=0)
        stage[d * pair_count + j] = block.astype(jnp.bfloat16)

    fetch.wait()
    count = half // pair_count // PARTS
    sends = []
    for k in range(PARTS):

        def assemble_all(d, carry):
            for j in range(pair_count):
                assemble(d, j)
            return carry

        lax.fori_loop(k * count, (k + 1) * count, assemble_all, 0, unroll=4)
        some = pl.ds(k * count * pair_count, count * pair_count)
        sends.append(pltpu.make_async_copy(stage.at[some], out_ref.at[some], out_sems.at[k]))
        sends[-1].start()
    for send in sends:
        send.wait()


def solve_kernel(
    sizes, lows_ref, index_ref, blocks_ref, weights_ref, out_ref, weights, sems, stage, out_sems
):
    levels, slot_count, chunk = sizes
    devices, pair_count = blocks_ref.shape[0], blocks_ref.shape[1]
    shape = (chunk, ROWS, LANES)
    mask = edge_masks(slot_count, levels - LANES, shape, 1)
    row = lax.broadcasted_iota(jnp.int32, shape, 1)
    slot = lax.broadcasted_iota(jnp.int32, (16, LANES), 0) // 2
    brings = []
    for j in range(pair_count):
        brings.append(pltpu.make_async_copy(weights_ref.at[j], weights.at[j], sems.at[j]))
        brings[-1].start()

    def solve_some(first):
        orders = []
        for k in range(chunk):
            lines = jnp.full((16, LANES), BIG, jnp.int32)
            for s in range(slot_count):
                order = index_ref[(first + k) * WORDS + pair_count + s]
                lines = jnp.where(slot == s, order, lines)
            orders.append(lines)
        orders = jnp.stack(orders)
        here = pl.ds(first, chunk)
        for j in range(pair_count):
            body = blocks_ref[here, j].astype(jnp.float32)
            edge = jnp.where(row % 2 == 0, body[:, ROWS - 2 : ROWS - 1], body[:, ROWS - 1 :])
            edge = jnp.where(mask, edge, 0.0)
            lines = jnp.concatenate([body, edge], axis=-1)
            top = lines[:, :16].reshape(chunk * 16, 2 * LANES).astype(jnp.bfloat16)
            lines = lines.reshape(chunk * ROWS, 2 * LANES).astype(jnp.bfloat16)
            pl.when(first == 0)(brings[j].wait)
            upper = jnp.dot(lines, weights[j, 1], preferred_element_type=jnp.float32)
            upper = upper.reshape(chunk, ROWS, 2 * LANES)
            lower = jnp.dot(top, weights[j, 0], preferred_element_type=jnp.float32)
            lower = lower.reshape(chunk, 16, 2 * LANES)
            own = orders <= lows_ref[j]
            main = jnp.where(own, lower[..., :LANES], upper[:, :16, :LANES])
            edge = jnp.where(own, lower[..., LANES:], upper[:, :16, LANES:])
            edge = jnp.where(mask[:, :16], edge, 0.0)
            rest = jnp.where(mask[:, 16:], upper[:, 16:, LANES:], 0.0)
            folded = parity_fold([edge[:, :8], edge[:, 8:], rest], 1)
            rest = jnp.where(row[:, 16:] >= ROWS - 2, folded, upper[:, 16:, :LANES])
            stage[here, j] = jnp.concatenate([main, rest], axis=1).astype(jnp.bfloat16)

    count = devices // PARTS
    sends = []
    for k in range(PARTS):

        def solve_all(c, carry):
            solve_some(k * count + c * chunk)
            return carry

        lax.fori_loop(0, count // chunk, solve_all, 0)
        some = pl.ds(k * count, count)
        sends.append(pltpu.make_async_copy(stage.at[some], out_ref.at[some], out_sems.at[k]))
        sends[-1].start()
    for send in sends:
        send.wait()


def final_kernel(
    sizes,
    index_ref,
    orders_ref,
    blocks_ref,
    state_ref,
    weights_ref,
    out_ref,
    body,
    tail,
    state_sems,
    out_body,
    out_tail,
    out_sems,
    xm,
    xe,
    lm,
    le,
    um,
    ue,
):
    levels, slot_count, slot_width, truncation, pair_count = sizes
    half = (truncation + 1) // 2
    parts = column_parts(state_ref.shape[1])
    head = state_ref.shape[0] - body.shape[0]
    copies = state_copies(state_ref, head, body, tail, state_sems)
    for copy in copies:
        copy.start()

    mask = edge_masks(slot_count, levels - LANES, (ROWS, LANES), 0)
    even = lax.broadcasted_iota(jnp.int32, (ROWS, LANES), 0) % 2 == 0

    def unfold(d, carry):
        for j in range(pair_count):
            n = index_ref[d * WORDS + j]
            block = blocks_ref[d * pair_count + j].astype(jnp.float32)
            edge = jnp.where(even, block[ROWS - 2 : ROWS - 1], block[ROWS - 1 :])
            edge = jnp.where(mask, edge, 0.0)
            start = UP * (half - 1 - n)
            low = LOW * n
            um[pl.ds(start, ROWS), :] = block
            ue[pl.ds(start, ROWS), :] = edge
            lm[pl.ds(low, 16), :] = block[:16]
            le[pl.ds(low, 16), :] = edge[:16]
        return carry

    lax.fori_loop(0, half // pair_count, unfold, 0, unroll=4)

    def regroup(k, carry):
        s = slot_count - 1 - k
        order = jnp.maximum(orders_ref[s], 0)
        base = FRONT + s * slot_width
        for p in range(2):
            for x, low, up in ((xm, lm, um), (xe, le, ue)):
                x[pl.ds(base + 2 * (half + 1) + p, half, stride=2), :] = up[
                    pl.ds(2 * s + p, half, stride=UP), :
                ]
                x[pl.ds(base - 2 * order + p, half, stride=2), :] = low[
                    pl.ds(2 * s + p, half, stride=LOW), :
                ]
                x[pl.ds(base + 2 * (half - order) + p, half, stride=2), :] = up[
                    pl.ds(2 * (slot_count + s) + p, half, stride=UP), :
                ]
            third = UP * (half - 1 - order) + 4 * slot_count + p
            place = base + 2 * (truncation + 1 - order) + p
            xm[pl.ds(place, 1), :] = um[pl.ds(third, 1), :]
            xe[pl.ds(place, 1), :] = ue[pl.ds(third, 1), :]
        return carry

    lax.fori_loop(0, slot_count, regroup, 0)

    row = lax.broadcasted_iota(jnp.int32, (state_ref.shape[0] - head, 1), 0)
    sends = []
    for k, (start, size) in enumerate(parts):
        copies[k].wait()
        at_end = k == len(parts) - 1
        base = tail[...] if at_end else body[:, start : start + size]
        lines = [x[pl.ds(FRONT + start, size), :] for x in (xm, xe)]
        moved = lax.dot_general(
            weights_ref[...],
            jnp.concatenate(lines, axis=1).astype(jnp.bfloat16),
            (((1,), (1,)), ((), ())),
            preferred_element_type=jnp.float32,
        )
        columns = start + lax.broadcasted_iota(jnp.int32, (1, size), 1)
        order, _ = slot_lines(columns, orders_ref, slot_count, slot_width)
        live = order >= 0
        kept = jnp.where(row >= levels - head, base.astype(jnp.float32), 0.0)
        first = jnp.where(live, moved[:head], 0.0).astype(jnp.bfloat16)
        second = jnp.where(live, kept + moved[head:], 0.0).astype(jnp.bfloat16)
        if at_end:
            out_tail[:head, :] = first
            out_tail[head:, :] = second
            source = out_tail
        else:
            out_body[:head, start : start + size] = first
            out_body[head:, start : start + size] = second
            source = out_body.at[:, pl.ds(start, size)]
        target = out_ref.at[:, pl.ds(start, size)]
        sends.append(pltpu.make_async_copy(source, target, out_sems.at[k]))
        sends[-1].start()
    for send in sends:
        send.wait()


def level_of_lane(levels, slot_count):
    edge = levels - LANES
    table = np.zeros((2 * LANES, levels), np.float32)
    table[np.arange(LANES), np.arange(LANES)] = 1.0
    folded = np.arange(edge * (2 * slot_count + 1))
    table[LANES + folded, LANES + folded % edge] = 1.0
    return table


def shards(
    state,
    held_orders,
    pair_lows,
    inverses,
    height_operator,
    pressure_column,
    thermal_response_matrix,
    mass_row,
):
    levels = height_operator.shape[0]
    pair_count = pair_lows.shape[0]
    slot_count = held_orders.shape[0]
    devices = lax.axis_size(GRP_WAVE)
    half = pair_count * devices
    truncation = 2 * half - 1
    slot_width = 2 * (truncation + 2)
    width = slot_count * slot_width
    rows = state.shape[0]
    parts = column_parts(width)
    split = parts[-1][0]
    bf16, f32 = jnp.bfloat16, jnp.float32
    vmem = pl.BlockSpec(memory_space=pltpu.VMEM)
    smem = pl.BlockSpec(memory_space=pltpu.SMEM)
    hbm = pl.BlockSpec(memory_space=pl.ANY)

    def params(mib):
        return pltpu.CompilerParams(vmem_limit_bytes=mib * 1024 * 1024)

    scratch = [
        pltpu.VMEM((FRONT + width + 6, LANES), f32),
        pltpu.VMEM((FRONT + width + 6, LANES), f32),
        pltpu.VMEM((LOW * half, LANES), f32),
        pltpu.VMEM((LOW * half, LANES), f32),
        pltpu.VMEM((UP * half, LANES), f32),
        pltpu.VMEM((UP * half, LANES), f32),
    ]

    own = jnp.concatenate([pair_lows, held_orders])
    own = jnp.pad(own, (0, LANES - own.shape[0]))
    index = lax.all_to_all(
        jnp.broadcast_to(own[None, None], (devices, 1, LANES)), GRP_WAVE, 0, 0, tiled=True
    ).reshape(devices, LANES)

    table = level_of_lane(levels, slot_count)
    padded = -(-levels // 16) * 16
    table = jnp.asarray(table, bf16)

    message = pl.pallas_call(
        functools.partial(rhs_kernel, (levels, slot_count, slot_width, truncation, pair_count)),
        in_specs=[
            hbm,
            smem,
            hbm,
            hbm,
            vmem,
        ],
        out_specs=hbm,
        out_shape=jax.ShapeDtypeStruct((half, ROWS, LANES), bf16),
        scratch_shapes=[
            pltpu.SMEM((devices, LANES), jnp.int32),
            pltpu.SemaphoreType.DMA,
            pltpu.VMEM((levels, levels), bf16),
            pltpu.SemaphoreType.DMA,
            pltpu.VMEM((padded, rows - LANES), bf16),
            pltpu.VMEM((rows, split), bf16),
            pltpu.VMEM((rows, width - split), bf16),
            pltpu.SemaphoreType.DMA((len(parts),)),
            pltpu.VMEM((half, ROWS, LANES), bf16),
            pltpu.SemaphoreType.DMA((PARTS,)),
        ]
        + scratch,
        compiler_params=params(56),
        name="right_side",
    )(index, held_orders, state, height_operator, pressure_column)

    arrived = lax.all_to_all(
        message.reshape(devices, pair_count * ROWS, LANES), GRP_WAVE, 0, 0, tiled=True
    ).reshape(devices, pair_count, ROWS, LANES)

    weights = jnp.einsum("al,jtkl->jtak", table, inverses, preferred_element_type=f32)
    weights = jnp.einsum("jtak,bk->jtab", weights.astype(bf16), table, preferred_element_type=f32)
    weights = weights.astype(bf16)
    words = index[:, :WORDS].reshape(-1)
    chunk = 32
    solved = pl.pallas_call(
        functools.partial(solve_kernel, (levels, slot_count, chunk)),
        in_specs=[smem, smem, vmem, hbm],
        out_specs=hbm,
        out_shape=jax.ShapeDtypeStruct((devices, pair_count, ROWS, LANES), bf16),
        scratch_shapes=[
            pltpu.VMEM((pair_count, 2, 2 * LANES, 2 * LANES), bf16),
            pltpu.SemaphoreType.DMA((pair_count,)),
            pltpu.VMEM((devices, pair_count, ROWS, LANES), bf16),
            pltpu.SemaphoreType.DMA((PARTS,)),
        ],
        compiler_params=params(24),
        name="solve",
    )(pair_lows, words, arrived, weights)

    returned = lax.all_to_all(
        solved.reshape(devices, pair_count * ROWS, LANES), GRP_WAVE, 0, 0, tiled=True
    ).reshape(half, ROWS, LANES)

    head = levels // 8 * 8
    response = jnp.concatenate(
        [jnp.eye(levels, dtype=bf16), -thermal_response_matrix, -mass_row[None, :]], axis=0
    )
    response = jnp.dot(response, table.T, preferred_element_type=f32).astype(bf16)
    return pl.pallas_call(
        functools.partial(final_kernel, (levels, slot_count, slot_width, truncation, pair_count)),
        in_specs=[smem, smem, vmem, hbm, vmem],
        out_specs=hbm,
        out_shape=jax.ShapeDtypeStruct((rows, width), bf16),
        scratch_shapes=[
            pltpu.VMEM((rows - head, split), bf16),
            pltpu.VMEM((rows - head, width - split), bf16),
            pltpu.SemaphoreType.DMA((len(parts),)),
            pltpu.VMEM((rows, split), bf16),
            pltpu.VMEM((rows, width - split), bf16),
            pltpu.SemaphoreType.DMA((len(parts),)),
        ]
        + scratch,
        compiler_params=params(48),
        name="final",
    )(words, held_orders, returned, state, response)


def solution(mesh):
    torus = Mesh(
        mesh.devices.reshape(mesh.shape["grp"], 4, 4, 2), ("grp", "wave_0", "wave_1", "wave_2")
    )
    placed = (
        P(None, GRP_WAVE),
        P(GRP_WAVE),
        P(GRP_WAVE),
        P(GRP_WAVE, None, None, None),
        P(),
        P(),
        P(),
        P(),
    )
    return jax.shard_map(
        shards, mesh=torus, in_specs=placed, out_specs=P(None, GRP_WAVE), check_vma=False
    )
```

time: 120 us -> 118 us (0.983)
  Pallas kernels: 21.2 us -> 18.9 us
  transfers between devices with their start and end apart: 2 -> 2, of which waited for: 2 -> 2; matrix products, arithmetic and copies ran while one was open for 1% -> 2% of each run, Pallas kernels for 0% -> 0%
where the time goes in v5:
time: 118 us
  waiting for transfers between devices  63.9 us (54%)
  blocking collectives  21.3 us (18%)
  Pallas kernels  18.9 us (16%)
  starting transfers between devices  9.4 us (8%)
  matrix products  1.96 us (2%)
  local copies, waits for them, and re-layouts  1.32 us (1%)
    all_to_all x1, waiting for transfers between devices, shards(): lax.all_to_all(solved.reshape(devices, pair_count * ROWS, LANES), GRP_WAV...  32.8 us
    all_to_all x1, waiting for transfers between devices, shards(): lax.all_to_all(message.reshape(devices, pair_count * ROWS, LANES), GRP_WA...  31.2 us
    all_to_all x1, blocking collectives, shards(): lax.all_to_all(jnp.broadcast_to(own[None, None], (devices, 1, LANES)), GR...  21.3 us
    pallas_call x1, Pallas kernels, shards(): pl.pallas_call(functools.partial(rhs_kernel, (levels, slot_count, slot_wi...  8.16 us
    pallas_call x1, Pallas kernels, shards(): pl.pallas_call(functools.partial(final_kernel, (levels, slot_count, slot_...  6.22 us
    all_to_all x1, starting transfers between devices, shards(): lax.all_to_all(solved.reshape(devices, pair_count * ROWS, LANES), GRP_WAV...  4.89 us
    all_to_all x1, starting transfers between devices, shards(): lax.all_to_all(message.reshape(devices, pair_count * ROWS, LANES), GRP_WA...  4.51 us
    pallas_call x1, Pallas kernels, shards(): pl.pallas_call(functools.partial(solve_kernel, (levels, slot_count, chunk...  4.48 us
  transfers between devices with their start and end apart: 2, of which 2 were waited for; matrix products, arithmetic and copies ran while one was open for 2% of the time, Pallas kernels for 0%

profile of v5, /device:TPU:1, one launch (start us, length us, event | category | flops | bytes accessed | tf_op | source)
XLA Modules:
  0.0 117.8 jit_solution(11109585274456452784)
XLA Ops:
  0.0 0.0 copy-start
  0.0 0.8 pad_add_fusion
  0.8 21.3 %all_to_all.15 = s32[128,1,128]{2,1,0:T(1,128)} all-to-all(s32[128,1,128]{2,1,0:T(1,128)S(1)} %broadcast_in_dim.2), channel_id=1, replica_groups=mesh['grp'=4,'wave_0'=4,'wave_1'=4,'wave_2'=2] {'grp','wave_0','wave_1',..., dimensions={0} | all-to-all | bytes 131072 | tf_op jit(solution)/shard_map/all_to_all | solution.py:424
  22.1 8.2 %right_side.1 = bf16[384,24,128]{2,1,0:T(8,128)(2,1)} custom-call(s32[128,128]{1,0:T(8,128)} %bitcast.19, s32[5]{0:T(128)} %orders_ref.3, bf16[275,7690]{1,0:T(8,128)(2,1)} %state_ref.3, bf16[137,137]{1,0:T(8,128)(2,1)} %height_ref.1, bf16[137]{0:T(256)(128)(2,1)} %pressure_ref.1), custom_call_target="tpu_custom_call" | custom-call | tf_op jit(solution)/shard_map/right_side/pallas_call | solution.py:432
  30.3 0.0 copy-start.8
  30.3 0.0 copy-start.4
  30.3 0.0 copy-start.3
  30.3 4.5 %all-to-all-start.1 = ((bf16[128,72,128]{2,1,0:T(8,128)(2,1)}), bf16[128,72,128]{2,1,0:T(8,128)(2,1)S(1)}, u32[]{:S(2)}, u32[]{:S(2)}) async-start(bf16[128,72,128]{2,1,0:T(8,128)(2,1)} %bitcast.18), calls=%async_computation.1 | async-start | bytes 4718592 | tf_op jit(solution)/shard_map/all_to_all | solution.py:460
  34.9 0.0 copy-done
  34.9 0.0 copy-done.8
  34.9 1.8 %convolution_convert_fusion.weights_ref = bf16[3,2,256,256]{3,2,1,0:T(8,128)(2,1)} fusion(bf16[256,137,1,1]{0,1,3,2:T(8,128)(2,1)S(1)} %copy-done.8, bf16[3,2,137,137]{3,1,2,0:T(2,128)(2,1)S(1)} %copy-done), kind=kOutput, calls=%fused_computation | convolution fusion | flops 166003200 | bytes 1081804 | tf_op jit(solution)/shard_map/jtak,bk->jtab/dot_general | solution.py:465
  36.7 0.0 copy-done.4
  36.7 0.1 reshape.23.index_ref
  36.7 31.2 %all-to-all-done.1 = bf16[128,72,128]{2,1,0:T(8,128)(2,1)S(1)} async-done(((bf16[128,72,128]{2,1,0:T(8,128)(2,1)}), bf16[128,72,128]{2,1,0:T(8,128)(2,1)S(1)}, u32[]{:S(2)}, u32[]{:S(2)}) %all-to-all-start.1) | async-done | bytes 2359328 | tf_op jit(solution)/shard_map/all_to_all | solution.py:460
  67.9 0.0 copy-done.3
  67.9 0.0 copy-start.1
  67.9 1.1 copy-done.1
  69.1 4.5 %solve.1 = bf16[128,3,24,128]{3,2,1,0:T(8,128)(2,1)} custom-call(s32[3]{0:T(128)S(1)} %copy-done.3, s32[1024]{0:T(1024)S(1)} %reshape.23.index_ref, bf16[128,3,24,128]{3,2,1,0:T(8,128)(2,1)S(1)} %bitcast.16, bf16[3,2,256,256]{3,2,1,0:T(8,128)(2,1)S(1)} %copy-done.1), custom_call_target="tpu_custom_call" | custom-call | tf_op jit(solution)/shard_map/solve/pallas_call | solution.py:469
  73.5 0.0 copy-start.6
  73.6 0.0 copy-start.5
  73.6 0.0 copy-start.7
  73.6 0.0 copy-start.2
  73.6 4.9 %all-to-all-start.2 = ((bf16[128,72,128]{2,1,0:T(8,128)(2,1)}), bf16[128,72,128]{2,1,0:T(8,128)(2,1)S(1)}, u32[]{:S(2)}, u32[]{:S(2)}) async-start(bf16[128,72,128]{2,1,0:T(8,128)(2,1)} %bitcast.6), calls=%async_computation.2 | async-start | bytes 4718592 | tf_op jit(solution)/shard_map/all_to_all | solution.py:484
  78.5 0.0 copy-done.6
  78.5 0.0 copy-done.5
  78.6 0.0 copy-done.7
  78.6 0.2 convolution_convert_fusion.2.weights_ref
  78.8 32.8 %all-to-all-done.2 = bf16[128,72,128]{2,1,0:T(8,128)(2,1)S(1)} async-done(((bf16[128,72,128]{2,1,0:T(8,128)(2,1)}), bf16[128,72,128]{2,1,0:T(8,128)(2,1)S(1)}, u32[]{:S(2)}, u32[]{:S(2)}) %all-to-all-start.2) | async-done | bytes 2359328 | tf_op jit(solution)/shard_map/all_to_all | solution.py:484
  111.6 0.0 copy-done.2
  111.6 6.2 %final.1 = bf16[275,7690]{1,0:T(8,128)(2,1)} custom-call(s32[1024]{0:T(1024)S(1)} %reshape.23.index_ref, s32[5]{0:T(128)S(1)} %copy-done.2, bf16[384,24,128]{2,1,0:T(8,128)(2,1)S(1)} %bitcast.17, bf16[275,7690]{1,0:T(8,128)(2,1)} %state_ref.3, bf16[275,256]{1,0:T(8,128)(2,1)S(1)} %convolution_convert_fusion.2.weights_ref), custom_call_target="tpu_custom_call" | custom-call | tf_op jit(solution)/shard_map/final/pallas_call | solution.py:493
  (6 shorter events, 0.1 us)
Async XLA Ops:
  0.0 34.9 %copy-start = (bf16[3,2,137,137]{3,1,2,0:T(2,128)(2,1)S(1)}, bf16[3,2,137,137]{3,1,2,0:T(2,128)(2,1)}, u32[]{:S(2)}) copy-start(bf16[3,2,137,137]{3,1,2,0:T(2,128)(2,1)} %param.12) | copy-start | bytes 675688
  30.3 4.6 %copy-start.8 = (bf16[256,137,1,1]{0,1,3,2:T(8,128)(2,1)S(1)}, bf16[256,137,1,1]{0,1,3,2:T(8,128)(2,1)}, u32[]{:S(2)}) copy-start(bf16[256,137,1,1]{0,1,3,2:T(8,128)(2,1)} %constant.11) | copy-start | bytes 210436
  30.3 6.3 %copy-start.4 = (s32[128,1,128]{2,1,0:T(1,128)S(1)}, s32[128,1,128]{2,1,0:T(1,128)}, u32[]{:S(2)}) copy-start(s32[128,1,128]{2,1,0:T(1,128)} %all_to_all.15) | copy-start | bytes 196612
  30.3 37.6 %copy-start.3 = (s32[3]{0:T(128)S(1)}, s32[3]{0:T(128)}, u32[]{:S(2)}) copy-start(s32[3]{0:T(128)} %lows_ref.1) | copy-start | bytes 40
  30.3 37.6 %all-to-all-start.1 = ((bf16[128,72,128]{2,1,0:T(8,128)(2,1)}), bf16[128,72,128]{2,1,0:T(8,128)(2,1)S(1)}, u32[]{:S(2)}, u32[]{:S(2)}) async-start(bf16[128,72,128]{2,1,0:T(8,128)(2,1)} %bitcast.18), calls=%async_computation.1 | async-start | bytes 4718592 | tf_op jit(solution)/shard_map/all_to_all | solution.py:460
  67.9 1.1 copy-start.1
  73.5 4.9 %copy-start.6 = (bf16[137]{0:T(256)(128)(2,1)S(1)}, bf16[137]{0:T(256)(128)(2,1)}, u32[]{:S(2)}) copy-start(bf16[137]{0:T(256)(128)(2,1)} %param.16) | copy-start | bytes 826
  73.6 5.0 %copy-start.5 = (bf16[137,137]{1,0:T(8,128)(2,1)S(1)}, bf16[137,137]{1,0:T(8,128)(2,1)}, u32[]{:S(2)}) copy-start(bf16[137,137]{1,0:T(8,128)(2,1)} %param.15) | copy-start | bytes 112618
  73.6 5.0 %copy-start.7 = (bf16[256,137]{0,1:T(8,128)(2,1)S(1)}, bf16[256,137]{0,1:T(8,128)(2,1)}, u32[]{:S(2)}) copy-start(bf16[256,137]{0,1:T(8,128)(2,1)} %constant.4.clone) | copy-start | bytes 210436
  73.6 38.0 %copy-start.2 = (s32[5]{0:T(128)S(1)}, s32[5]{0:T(128)}, u32[]{:S(2)}) copy-start(s32[5]{0:T(128)} %orders_ref.3) | copy-start | bytes 64
  73.6 38.0 %all-to-all-start.2 = ((bf16[128,72,128]{2,1,0:T(8,128)(2,1)}), bf16[128,72,128]{2,1,0:T(8,128)(2,1)S(1)}, u32[]{:S(2)}, u32[]{:S(2)}) async-start(bf16[128,72,128]{2,1,0:T(8,128)(2,1)} %bitcast.6), calls=%async_computation.2 | async-start | bytes 4718592 | tf_op jit(solution)/shard_map/all_to_all | solution.py:484

commit v6 on v5

--- a/solution.py
+++ b/solution.py
@@ -25,7 +25,7 @@
 def edge_masks(slot_count, edge, shape, row_dim):
     rows = lax.broadcasted_iota(jnp.int32, shape, row_dim)
     lanes = lax.broadcasted_iota(jnp.int32, shape, len(shape) - 1)
-    group = rows // 2
+    group = rows >> 1
     return (lanes >= edge * group) & (lanes < edge * (group + 1)) & (rows < 4 * slot_count + 2)
 
 
@@ -206,65 +206,41 @@
         send.wait()
 
 
-def solve_kernel(
-    sizes, lows_ref, index_ref, blocks_ref, weights_ref, out_ref, weights, sems, stage, out_sems
-):
-    levels, slot_count, chunk = sizes
-    devices, pair_count = blocks_ref.shape[0], blocks_ref.shape[1]
-    shape = (chunk, ROWS, LANES)
-    mask = edge_masks(slot_count, levels - LANES, shape, 1)
-    row = lax.broadcasted_iota(jnp.int32, shape, 1)
-    slot = lax.broadcasted_iota(jnp.int32, (16, LANES), 0) // 2
-    brings = []
+def solve_kernel(sizes, lows_ref, index_ref, blocks_ref, weights_ref, out_ref):
+    levels, slot_count = sizes
+    count, pair_count = blocks_ref.shape[0], blocks_ref.shape[1]
+    shape = (count, ROWS, LANES)
+    mask = edge_masks(slot_count, levels - LANES, (ROWS, LANES), 0)[None]
+    even = (lax.broadcasted_iota(jnp.int32, (ROWS, LANES), 0) & 1 == 0)[None]
+    bottom = (lax.broadcasted_iota(jnp.int32, (8, LANES), 0) >= 6)[None]
+    slot = lax.broadcasted_iota(jnp.int32, (16, LANES), 0) >> 1
+    orders = []
+    for k in range(count):
+        lines = jnp.full((16, LANES), BIG, jnp.int32)
+        for s in range(slot_count):
+            order = index_ref[(pl.program_id(0) * count + k) * WORDS + pair_count + s]
+            lines = jnp.where(slot == s, order, lines)
+        orders.append(lines)
+    orders = jnp.stack(orders)
     for j in range(pair_count):
-        brings.append(pltpu.make_async_copy(weights_ref.at[j], weights.at[j], sems.at[j]))
-        brings[-1].start()
-
-    def solve_some(first):
-        orders = []
-        for k in range(chunk):
-            lines = jnp.full((16, LANES), BIG, jnp.int32)
-            for s in range(slot_count):
-                order = index_ref[(first + k) * WORDS + pair_count + s]
-                lines = jnp.where(slot == s, order, lines)
-            orders.append(lines)
-        orders = jnp.stack(orders)
-        here = pl.ds(first, chunk)
-        for j in range(pair_count):
-            body = blocks_ref[here, j].astype(jnp.float32)
-            edge = jnp.where(row % 2 == 0, body[:, ROWS - 2 : ROWS - 1], body[:, ROWS - 1 :])
-            edge = jnp.where(mask, edge, 0.0)
-            lines = jnp.concatenate([body, edge], axis=-1)
-            top = lines[:, :16].reshape(chunk * 16, 2 * LANES).astype(jnp.bfloat16)
-            lines = lines.reshape(chunk * ROWS, 2 * LANES).astype(jnp.bfloat16)
-            pl.when(first == 0)(brings[j].wait)
-            upper = jnp.dot(lines, weights[j, 1], preferred_element_type=jnp.float32)
-            upper = upper.reshape(chunk, ROWS, 2 * LANES)
-            lower = jnp.dot(top, weights[j, 0], preferred_element_type=jnp.float32)
-            lower = lower.reshape(chunk, 16, 2 * LANES)
-            own = orders <= lows_ref[j]
-            main = jnp.where(own, lower[..., :LANES], upper[:, :16, :LANES])
-            edge = jnp.where(own, lower[..., LANES:], upper[:, :16, LANES:])
-            edge = jnp.where(mask[:, :16], edge, 0.0)
-            rest = jnp.where(mask[:, 16:], upper[:, 16:, LANES:], 0.0)
-            folded = parity_fold([edge[:, :8], edge[:, 8:], rest], 1)
-            rest = jnp.where(row[:, 16:] >= ROWS - 2, folded, upper[:, 16:, :LANES])
-            stage[here, j] = jnp.concatenate([main, rest], axis=1).astype(jnp.bfloat16)
-
-    count = devices // PARTS
-    sends = []
-    for k in range(PARTS):
-
-        def solve_all(c, carry):
-            solve_some(k * count + c * chunk)
-            return carry
-
-        lax.fori_loop(0, count // chunk, solve_all, 0)
-        some = pl.ds(k * count, count)
-        sends.append(pltpu.make_async_copy(stage.at[some], out_ref.at[some], out_sems.at[k]))
-        sends[-1].start()
-    for send in sends:
-        send.wait()
+        body = blocks_ref[:, j].astype(jnp.float32)
+        edge = jnp.where(even, body[:, ROWS - 2 : ROWS - 1], body[:, ROWS - 1 :])
+        edge = jnp.where(mask, edge, 0.0)
+        lines = jnp.concatenate([body, edge], axis=-1)
+        top = lines[:, :16].reshape(count * 16, 2 * LANES).astype(jnp.bfloat16)
+        lines = lines.reshape(count * ROWS, 2 * LANES).astype(jnp.bfloat16)
+        upper = jnp.dot(lines, weights_ref[j, 1], preferred_element_type=jnp.float32)
+        upper = upper.reshape(count, ROWS, 2 * LANES)
+        lower = jnp.dot(top, weights_ref[j, 0], preferred_element_type=jnp.float32)
+        lower = lower.reshape(count, 16, 2 * LANES)
+        own = orders <= lows_ref[j]
+        main = jnp.where(own, lower[..., :LANES], upper[:, :16, :LANES])
+        edge = jnp.where(own, lower[..., LANES:], upper[:, :16, LANES:])
+        edge = jnp.where(mask[:, :16], edge, 0.0)
+        rest = jnp.where(mask[:, 16:], upper[:, 16:, LANES:], 0.0)
+        folded = parity_fold([edge[:, :8], edge[:, 8:], rest], 1)
+        rest = jnp.where(bottom, folded, upper[:, 16:, :LANES])
+        out_ref[:, j] = jnp.concatenate([main, rest], axis=1).astype(jnp.bfloat16)
 
 
 def final_kernel(
@@ -465,19 +441,19 @@
     weights = jnp.einsum("jtak,bk->jtab", weights.astype(bf16), table, preferred_element_type=f32)
     weights = weights.astype(bf16)
     words = index[:, :WORDS].reshape(-1)
-    chunk = 32
+    chunk = 64
     solved = pl.pallas_call(
-        functools.partial(solve_kernel, (levels, slot_count, chunk)),
-        in_specs=[smem, smem, vmem, hbm],
-        out_specs=hbm,
+        functools.partial(solve_kernel, (levels, slot_count)),
+        grid=(devices // chunk,),
+        in_specs=[
+            smem,
+            smem,
+            pl.BlockSpec((chunk, pair_count, ROWS, LANES), lambda i: (i, 0, 0, 0)),
+            vmem,
+        ],
+        out_specs=pl.BlockSpec((chunk, pair_count, ROWS, LANES), lambda i: (i, 0, 0, 0)),
         out_shape=jax.ShapeDtypeStruct((devices, pair_count, ROWS, LANES), bf16),
-        scratch_shapes=[
-            pltpu.VMEM((pair_count, 2, 2 * LANES, 2 * LANES), bf16),
-            pltpu.SemaphoreType.DMA((pair_count,)),
-            pltpu.VMEM((devices, pair_count, ROWS, LANES), bf16),
-            pltpu.SemaphoreType.DMA((PARTS,)),
-        ],
-        compiler_params=params(24),
+        compiler_params=params(52),
         name="solve",
     )(pair_lows, words, arrived, weights)
 

time: 118 us -> 118 us (level)
  transfers between devices with their start and end apart: 2 -> 2, of which waited for: 2 -> 2; matrix products, arithmetic and copies ran while one was open for 2% -> 1% of each run, Pallas kernels for 0% -> 0%
where the time goes in v6:
time: 118 us
  waiting for transfers between devices  64.5 us (55%)
  blocking collectives  21.3 us (18%)
  Pallas kernels  19.4 us (16%)
  starting transfers between devices  10.3 us (9%)
    all_to_all x1, waiting for transfers between devices, shards(): lax.all_to_all(solved.reshape(devices, pair_count * ROWS, LANES), GRP_WAV...  32.8 us
    all_to_all x1, waiting for transfers between devices, shards(): lax.all_to_all(message.reshape(devices, pair_count * ROWS, LANES), GRP_WA...  31.8 us
    all_to_all x1, blocking collectives, shards(): lax.all_to_all(jnp.broadcast_to(own[None, None], (devices, 1, LANES)), GR...  21.3 us
    pallas_call x1, Pallas kernels, shards(): pl.pallas_call(functools.partial(rhs_kernel, (levels, slot_count, slot_wi...  8.14 us
    pallas_call x1, Pallas kernels, shards(): pl.pallas_call(functools.partial(final_kernel, (levels, slot_count, slot_...  6.23 us
    all_to_all x1, starting transfers between devices, shards(): lax.all_to_all(message.reshape(devices, pair_count * ROWS, LANES), GRP_WA...  5.44 us
    pallas_call x1, Pallas kernels, shards(): pl.pallas_call(functools.partial(solve_kernel, (levels, slot_count)), gri...  5 us
    all_to_all x1, starting transfers between devices, shards(): lax.all_to_all(solved.reshape(devices, pair_count * ROWS, LANES), GRP_WAV...  4.88 us
  transfers between devices with their start and end apart: 2, of which 2 were waited for; matrix products, arithmetic and copies ran while one was open for 1% of the time, Pallas kernels for 0%

profile of v6, /device:TPU:1, one launch (start us, length us, event | category | flops | bytes accessed | tf_op | source)
XLA Modules:
  0.0 117.8 jit_solution(4122034063307587597)
XLA Ops:
  0.0 0.0 copy-start
  0.0 0.8 pad_add_fusion
  0.8 21.3 %all_to_all.15 = s32[128,1,128]{2,1,0:T(1,128)} all-to-all(s32[128,1,128]{2,1,0:T(1,128)S(1)} %broadcast_in_dim.2), channel_id=1, replica_groups=mesh['grp'=4,'wave_0'=4,'wave_1'=4,'wave_2'=2] {'grp','wave_0','wave_1',..., dimensions={0} | all-to-all | bytes 131072 | tf_op jit(solution)/shard_map/all_to_all | solution.py:400
  22.1 8.1 %right_side.1 = bf16[384,24,128]{2,1,0:T(8,128)(2,1)} custom-call(s32[128,128]{1,0:T(8,128)} %bitcast.19, s32[5]{0:T(128)} %orders_ref.3, bf16[275,7690]{1,0:T(8,128)(2,1)} %state_ref.3, bf16[137,137]{1,0:T(8,128)(2,1)} %height_ref.1, bf16[137]{0:T(256)(128)(2,1)} %pressure_ref.1), custom_call_target="tpu_custom_call" | custom-call | tf_op jit(solution)/shard_map/right_side/pallas_call | solution.py:408
  30.3 0.0 copy-start.7
  30.3 0.0 copy-start.3
  30.3 0.0 copy-start.2
  30.3 5.4 %all-to-all-start.1 = ((bf16[128,72,128]{2,1,0:T(8,128)(2,1)}), bf16[128,72,128]{2,1,0:T(8,128)(2,1)}, u32[]{:S(2)}, u32[]{:S(2)}) async-start(bf16[128,72,128]{2,1,0:T(8,128)(2,1)} %bitcast.18), calls=%async_computation.1 | async-start | bytes 4718592 | tf_op jit(solution)/shard_map/all_to_all | solution.py:436
  35.8 0.0 copy-done
  35.8 0.0 copy-done.7
  35.8 0.9 convolution_convert_fusion.weights_ref
  36.7 0.0 copy-done.3
  36.7 0.1 reshape.23.index_ref
  36.8 31.8 %all-to-all-done.1 = bf16[128,72,128]{2,1,0:T(8,128)(2,1)} async-done(((bf16[128,72,128]{2,1,0:T(8,128)(2,1)}), bf16[128,72,128]{2,1,0:T(8,128)(2,1)}, u32[]{:S(2)}, u32[]{:S(2)}) %all-to-all-start.1) | async-done | bytes 2359328 | tf_op jit(solution)/shard_map/all_to_all | solution.py:436
  68.5 0.0 copy-done.2
  68.6 5.0 %solve.1 = bf16[128,3,24,128]{3,2,1,0:T(8,128)(2,1)} custom-call(s32[3]{0:T(128)S(1)} %copy-done.2, s32[1024]{0:T(1024)S(1)} %reshape.23.index_ref, bf16[128,3,24,128]{3,2,1,0:T(8,128)(2,1)} %bitcast.2.blocks_ref, bf16[3,2,256,256]{3,2,1,0:T(8,128)(2,1)S(1)} %convolution_convert_fusion.weights_ref), custom_call_target="tpu_custom_call" | custom-call | tf_op jit(solution)/shard_map/solve/pallas_call | solution.py:445
  73.6 0.0 copy-start.5
  73.6 0.0 copy-start.4
  73.6 0.0 copy-start.6
  73.6 0.0 copy-start.1
  73.6 4.9 %all-to-all-start.2 = ((bf16[128,72,128]{2,1,0:T(8,128)(2,1)}), bf16[128,72,128]{2,1,0:T(8,128)(2,1)S(1)}, u32[]{:S(2)}, u32[]{:S(2)}) async-start(bf16[128,72,128]{2,1,0:T(8,128)(2,1)} %bitcast.17), calls=%async_computation.2 | async-start | bytes 4718592 | tf_op jit(solution)/shard_map/all_to_all | solution.py:460
  78.5 0.0 copy-done.5
  78.5 0.0 copy-done.4
  78.6 0.0 copy-done.6
  78.6 0.2 convolution_convert_fusion.2.weights_ref
  78.8 32.8 %all-to-all-done.2 = bf16[128,72,128]{2,1,0:T(8,128)(2,1)S(1)} async-done(((bf16[128,72,128]{2,1,0:T(8,128)(2,1)}), bf16[128,72,128]{2,1,0:T(8,128)(2,1)S(1)}, u32[]{:S(2)}, u32[]{:S(2)}) %all-to-all-start.2) | async-done | bytes 2359328 | tf_op jit(solution)/shard_map/all_to_all | solution.py:460
  111.5 0.0 copy-done.1
  111.5 6.2 %final.1 = bf16[275,7690]{1,0:T(8,128)(2,1)} custom-call(s32[1024]{0:T(1024)S(1)} %reshape.23.index_ref, s32[5]{0:T(128)S(1)} %copy-done.1, bf16[384,24,128]{2,1,0:T(8,128)(2,1)S(1)} %bitcast.16, bf16[275,7690]{1,0:T(8,128)(2,1)} %state_ref.3, bf16[275,256]{1,0:T(8,128)(2,1)S(1)} %convolution_convert_fusion.2.weights_ref), custom_call_target="tpu_custom_call" | custom-call | tf_op jit(solution)/shard_map/final/pallas_call | solution.py:469
  (6 shorter events, 0.1 us)
Async XLA Ops:
  0.0 35.8 %copy-start = (bf16[3,2,137,137]{3,1,2,0:T(2,128)(2,1)S(1)}, bf16[3,2,137,137]{3,1,2,0:T(2,128)(2,1)}, u32[]{:S(2)}) copy-start(bf16[3,2,137,137]{3,1,2,0:T(2,128)(2,1)} %param.12) | copy-start | bytes 675688
  30.3 5.5 %copy-start.7 = (bf16[256,137,1,1]{0,1,3,2:T(8,128)(2,1)S(1)}, bf16[256,137,1,1]{0,1,3,2:T(8,128)(2,1)}, u32[]{:S(2)}) copy-start(bf16[256,137,1,1]{0,1,3,2:T(8,128)(2,1)} %constant.11) | copy-start | bytes 210436
  30.3 6.4 %copy-start.3 = (s32[128,1,128]{2,1,0:T(1,128)S(1)}, s32[128,1,128]{2,1,0:T(1,128)}, u32[]{:S(2)}) copy-start(s32[128,1,128]{2,1,0:T(1,128)} %all_to_all.15) | copy-start | bytes 196612
  30.3 38.2 %copy-start.2 = (s32[3]{0:T(128)S(1)}, s32[3]{0:T(128)}, u32[]{:S(2)}) copy-start(s32[3]{0:T(128)} %lows_ref.1) | copy-start | bytes 40
  30.3 38.2 %all-to-all-start.1 = ((bf16[128,72,128]{2,1,0:T(8,128)(2,1)}), bf16[128,72,128]{2,1,0:T(8,128)(2,1)}, u32[]{:S(2)}, u32[]{:S(2)}) async-start(bf16[128,72,128]{2,1,0:T(8,128)(2,1)} %bitcast.18), calls=%async_computation.1 | async-start | bytes 4718592 | tf_op jit(solution)/shard_map/all_to_all | solution.py:436
  73.6 4.9 %copy-start.5 = (bf16[137]{0:T(256)(128)(2,1)S(1)}, bf16[137]{0:T(256)(128)(2,1)}, u32[]{:S(2)}) copy-start(bf16[137]{0:T(256)(128)(2,1)} %param.16) | copy-start | bytes 826
  73.6 4.9 %copy-start.4 = (bf16[137,137]{1,0:T(8,128)(2,1)S(1)}, bf16[137,137]{1,0:T(8,128)(2,1)}, u32[]{:S(2)}) copy-start(bf16[137,137]{1,0:T(8,128)(2,1)} %param.15) | copy-start | bytes 112618
  73.6 5.0 %copy-start.6 = (bf16[256,137]{0,1:T(8,128)(2,1)S(1)}, bf16[256,137]{0,1:T(8,128)(2,1)}, u32[]{:S(2)}) copy-start(bf16[256,137]{0,1:T(8,128)(2,1)} %constant.4.clone) | copy-start | bytes 210436
  73.6 38.0 %copy-start.1 = (s32[5]{0:T(128)S(1)}, s32[5]{0:T(128)}, u32[]{:S(2)}) copy-start(s32[5]{0:T(128)} %orders_ref.3) | copy-start | bytes 64
  73.6 37.9 %all-to-all-start.2 = ((bf16[128,72,128]{2,1,0:T(8,128)(2,1)}), bf16[128,72,128]{2,1,0:T(8,128)(2,1)S(1)}, u32[]{:S(2)}, u32[]{:S(2)}) async-start(bf16[128,72,128]{2,1,0:T(8,128)(2,1)} %bitcast.17), calls=%async_computation.2 | async-start | bytes 4718592 | tf_op jit(solution)/shard_map/all_to_all | solution.py:460

commit v7 on v5

--- a/solution.py
+++ b/solution.py
@@ -207,7 +207,7 @@
 
 
 def solve_kernel(
-    sizes, lows_ref, index_ref, blocks_ref, weights_ref, out_ref, weights, sems, stage, out_sems
+    sizes, lows_ref, index_ref, blocks_ref, weights_ref, out_ref, stage, out_sems
 ):
     levels, slot_count, chunk = sizes
     devices, pair_count = blocks_ref.shape[0], blocks_ref.shape[1]
@@ -215,10 +215,11 @@
     mask = edge_masks(slot_count, levels - LANES, shape, 1)
     row = lax.broadcasted_iota(jnp.int32, shape, 1)
     slot = lax.broadcasted_iota(jnp.int32, (16, LANES), 0) // 2
-    brings = []
-    for j in range(pair_count):
-        brings.append(pltpu.make_async_copy(weights_ref.at[j], weights.at[j], sems.at[j]))
-        brings[-1].start()
+    depth = weights_ref.shape[2]
+    empty = jnp.zeros((2 * LANES - depth, 2 * LANES), jnp.bfloat16)
+
+    def whole(j, t):
+        return jnp.concatenate([weights_ref[j, t], empty], axis=0)
 
     def solve_some(first):
         orders = []
@@ -237,10 +238,9 @@
             lines = jnp.concatenate([body, edge], axis=-1)
             top = lines[:, :16].reshape(chunk * 16, 2 * LANES).astype(jnp.bfloat16)
             lines = lines.reshape(chunk * ROWS, 2 * LANES).astype(jnp.bfloat16)
-            pl.when(first == 0)(brings[j].wait)
-            upper = jnp.dot(lines, weights[j, 1], preferred_element_type=jnp.float32)
+            upper = jnp.dot(lines, whole(j, 1), preferred_element_type=jnp.float32)
             upper = upper.reshape(chunk, ROWS, 2 * LANES)
-            lower = jnp.dot(top, weights[j, 0], preferred_element_type=jnp.float32)
+            lower = jnp.dot(top, whole(j, 0), preferred_element_type=jnp.float32)
             lower = lower.reshape(chunk, 16, 2 * LANES)
             own = orders <= lows_ref[j]
             main = jnp.where(own, lower[..., :LANES], upper[:, :16, :LANES])
@@ -461,19 +461,18 @@
         message.reshape(devices, pair_count * ROWS, LANES), GRP_WAVE, 0, 0, tiled=True
     ).reshape(devices, pair_count, ROWS, LANES)
 
-    weights = jnp.einsum("al,jtkl->jtak", table, inverses, preferred_element_type=f32)
+    depth = -(-(LANES + (levels - LANES) * (2 * slot_count + 1)) // 16) * 16
+    weights = jnp.einsum("al,jtkl->jtak", table[:depth], inverses, preferred_element_type=f32)
     weights = jnp.einsum("jtak,bk->jtab", weights.astype(bf16), table, preferred_element_type=f32)
     weights = weights.astype(bf16)
     words = index[:, :WORDS].reshape(-1)
     chunk = 32
     solved = pl.pallas_call(
         functools.partial(solve_kernel, (levels, slot_count, chunk)),
-        in_specs=[smem, smem, vmem, hbm],
+        in_specs=[smem, smem, vmem, vmem],
         out_specs=hbm,
         out_shape=jax.ShapeDtypeStruct((devices, pair_count, ROWS, LANES), bf16),
         scratch_shapes=[
-            pltpu.VMEM((pair_count, 2, 2 * LANES, 2 * LANES), bf16),
-            pltpu.SemaphoreType.DMA((pair_count,)),
             pltpu.VMEM((devices, pair_count, ROWS, LANES), bf16),
             pltpu.SemaphoreType.DMA((PARTS,)),
         ],

time: 118 us -> 116 us (0.983)
  transfers between devices with their start and end apart: 2 -> 2, of which waited for: 2 -> 2; matrix products, arithmetic and copies ran while one was open for 2% -> 3% of each run, Pallas kernels for 0% -> 0%
where the time goes in v7:
time: 116 us
  waiting for transfers between devices  63.1 us (54%)
  blocking collectives  21.1 us (18%)
  Pallas kernels  18.2 us (16%)
  starting transfers between devices  9.41 us (8%)
  matrix products  1.97 us (2%)
    all_to_all x1, waiting for transfers between devices, shards(): lax.all_to_all(solved.reshape(devices, pair_count * ROWS, LANES), GRP_WAV...  32.8 us
    all_to_all x1, waiting for transfers between devices, shards(): lax.all_to_all(message.reshape(devices, pair_count * ROWS, LANES), GRP_WA...  30.3 us
    all_to_all x1, blocking collectives, shards(): lax.all_to_all(jnp.broadcast_to(own[None, None], (devices, 1, LANES)), GR...  21.1 us
    pallas_call x1, Pallas kernels, shards(): pl.pallas_call(functools.partial(rhs_kernel, (levels, slot_count, slot_wi...  8.14 us
    pallas_call x1, Pallas kernels, shards(): pl.pallas_call(functools.partial(final_kernel, (levels, slot_count, slot_...  6.25 us
    all_to_all x1, starting transfers between devices, shards(): lax.all_to_all(solved.reshape(devices, pair_count * ROWS, LANES), GRP_WAV...  4.89 us
    all_to_all x1, starting transfers between devices, shards(): lax.all_to_all(message.reshape(devices, pair_count * ROWS, LANES), GRP_WA...  4.52 us
    pallas_call x1, Pallas kernels, shards(): pl.pallas_call(functools.partial(solve_kernel, (levels, slot_count, chunk...  3.84 us
  transfers between devices with their start and end apart: 2, of which 2 were waited for; matrix products, arithmetic and copies ran while one was open for 3% of the time, Pallas kernels for 0%

profile of v7, /device:TPU:1, one launch (start us, length us, event | category | flops | bytes accessed | tf_op | source)
XLA Modules:
  0.0 115.9 jit_solution(11281499676864246166)
XLA Ops:
  0.0 0.0 copy-start
  0.0 0.8 pad_add_fusion
  0.8 21.1 %all_to_all.15 = s32[128,1,128]{2,1,0:T(1,128)} all-to-all(s32[128,1,128]{2,1,0:T(1,128)S(1)} %broadcast_in_dim.2), channel_id=1, replica_groups=mesh['grp'=4,'wave_0'=4,'wave_1'=4,'wave_2'=2] {'grp','wave_0','wave_1',..., dimensions={0} | all-to-all | bytes 131072 | tf_op jit(solution)/shard_map/all_to_all | solution.py:424
  22.0 8.1 %right_side.1 = bf16[384,24,128]{2,1,0:T(8,128)(2,1)} custom-call(s32[128,128]{1,0:T(8,128)} %bitcast.22, s32[5]{0:T(128)} %orders_ref.3, bf16[275,7690]{1,0:T(8,128)(2,1)} %state_ref.3, bf16[137,137]{1,0:T(8,128)(2,1)} %height_ref.1, bf16[137]{0:T(256)(128)(2,1)} %pressure_ref.1), custom_call_target="tpu_custom_call" | custom-call | tf_op jit(solution)/shard_map/right_side/pallas_call | solution.py:432
  30.1 0.0 copy-start.2
  30.2 4.5 %all-to-all-start.1 = ((bf16[128,72,128]{2,1,0:T(8,128)(2,1)}), bf16[128,72,128]{2,1,0:T(8,128)(2,1)S(1)}, u32[]{:S(2)}, u32[]{:S(2)}) async-start(bf16[128,72,128]{2,1,0:T(8,128)(2,1)} %bitcast.21), calls=%async_computation.1 | async-start | bytes 4718592 | tf_op jit(solution)/shard_map/all_to_all | solution.py:460
  34.7 0.0 copy-done
  34.7 1.8 %convolution_convert_fusion.weights_ref = bf16[3,2,240,256]{3,2,1,0:T(8,128)(2,1)S(1)} fusion(bf16[256,137,1,1]{0,1,3,2:T(8,128)(2,1)} %constant.13, bf16[240,137,1,1]{0,1,3,2:T(8,128)(2,1)} %constant.12, bf16[3,2,137,137]{3,1,2,0:T(2,128)(2,1)S(1)} %copy-done), kind=kOutput, calls=%fused_computation | convolution fusion | flops 155628000 | bytes 1098412 | tf_op jit(solution)/shard_map/jtak,bk->jtab/dot_general | solution.py:466
  36.5 0.9 reshape.23.index_ref
  37.4 30.3 %all-to-all-done.1 = bf16[128,72,128]{2,1,0:T(8,128)(2,1)S(1)} async-done(((bf16[128,72,128]{2,1,0:T(8,128)(2,1)}), bf16[128,72,128]{2,1,0:T(8,128)(2,1)S(1)}, u32[]{:S(2)}, u32[]{:S(2)}) %all-to-all-start.1) | async-done | bytes 2359328 | tf_op jit(solution)/shard_map/all_to_all | solution.py:460
  67.8 0.0 copy-done.2
  67.8 3.8 %solve.1 = bf16[128,3,24,128]{3,2,1,0:T(8,128)(2,1)} custom-call(s32[3]{0:T(128)S(1)} %copy-done.2, s32[1024]{0:T(1024)S(1)} %reshape.23.index_ref, bf16[128,3,24,128]{3,2,1,0:T(8,128)(2,1)S(1)} %bitcast.19, bf16[3,2,240,256]{3,2,1,0:T(8,128)(2,1)S(1)} %convolution_convert_fusion.weights_ref), custom_call_target="tpu_custom_call" | custom-call | tf_op jit(solution)/shard_map/solve/pallas_call | solution.py:470
  71.6 0.0 copy-start.4
  71.6 0.0 copy-start.3
  71.6 0.0 copy-start.5
  71.6 0.0 copy-start.1
  71.7 4.9 %all-to-all-start.2 = ((bf16[128,72,128]{2,1,0:T(8,128)(2,1)}), bf16[128,72,128]{2,1,0:T(8,128)(2,1)S(1)}, u32[]{:S(2)}, u32[]{:S(2)}) async-start(bf16[128,72,128]{2,1,0:T(8,128)(2,1)} %bitcast.8), calls=%async_computation.2 | async-start | bytes 4718592 | tf_op jit(solution)/shard_map/all_to_all | solution.py:483
  76.5 0.0 copy-done.4
  76.6 0.0 copy-done.3
  76.6 0.0 copy-done.5
  76.6 0.2 convolution_convert_fusion.2.weights_ref
  76.8 32.8 %all-to-all-done.2 = bf16[128,72,128]{2,1,0:T(8,128)(2,1)S(1)} async-done(((bf16[128,72,128]{2,1,0:T(8,128)(2,1)}), bf16[128,72,128]{2,1,0:T(8,128)(2,1)S(1)}, u32[]{:S(2)}, u32[]{:S(2)}) %all-to-all-start.2) | async-done | bytes 2359328 | tf_op jit(solution)/shard_map/all_to_all | solution.py:483
  109.6 0.0 copy-done.1
  109.6 6.2 %final.1 = bf16[275,7690]{1,0:T(8,128)(2,1)} custom-call(s32[1024]{0:T(1024)S(1)} %reshape.23.index_ref, s32[5]{0:T(128)S(1)} %copy-done.1, bf16[384,24,128]{2,1,0:T(8,128)(2,1)S(1)} %bitcast.20, bf16[275,7690]{1,0:T(8,128)(2,1)} %state_ref.3, bf16[275,256]{1,0:T(8,128)(2,1)S(1)} %convolution_convert_fusion.2.weights_ref), custom_call_target="tpu_custom_call" | custom-call | tf_op jit(solution)/shard_map/final/pallas_call | solution.py:492
  (6 shorter events, 0.1 us)
Async XLA Ops:
  0.0 34.7 %copy-start = (bf16[3,2,137,137]{3,1,2,0:T(2,128)(2,1)S(1)}, bf16[3,2,137,137]{3,1,2,0:T(2,128)(2,1)}, u32[]{:S(2)}) copy-start(bf16[3,2,137,137]{3,1,2,0:T(2,128)(2,1)} %param.12) | copy-start | bytes 675688
  30.1 37.6 %copy-start.2 = (s32[3]{0:T(128)S(1)}, s32[3]{0:T(128)}, u32[]{:S(2)}) copy-start(s32[3]{0:T(128)} %lows_ref.1) | copy-start | bytes 40
  30.2 37.6 %all-to-all-start.1 = ((bf16[128,72,128]{2,1,0:T(8,128)(2,1)}), bf16[128,72,128]{2,1,0:T(8,128)(2,1)S(1)}, u32[]{:S(2)}, u32[]{:S(2)}) async-start(bf16[128,72,128]{2,1,0:T(8,128)(2,1)} %bitcast.21), calls=%async_computation.1 | async-start | bytes 4718592 | tf_op jit(solution)/shard_map/all_to_all | solution.py:460
  71.6 4.9 %copy-start.4 = (bf16[137]{0:T(256)(128)(2,1)S(1)}, bf16[137]{0:T(256)(128)(2,1)}, u32[]{:S(2)}) copy-start(bf16[137]{0:T(256)(128)(2,1)} %param.16) | copy-start | bytes 826
  71.6 5.0 %copy-start.3 = (bf16[137,137]{1,0:T(8,128)(2,1)S(1)}, bf16[137,137]{1,0:T(8,128)(2,1)}, u32[]{:S(2)}) copy-start(bf16[137,137]{1,0:T(8,128)(2,1)} %param.15) | copy-start | bytes 112618
  71.6 5.0 %copy-start.5 = (bf16[256,137]{0,1:T(8,128)(2,1)S(1)}, bf16[256,137]{0,1:T(8,128)(2,1)}, u32[]{:S(2)}) copy-start(bf16[256,137]{0,1:T(8,128)(2,1)} %constant.4.clone) | copy-start | bytes 210436
  71.6 38.0 %copy-start.1 = (s32[5]{0:T(128)S(1)}, s32[5]{0:T(128)}, u32[]{:S(2)}) copy-start(s32[5]{0:T(128)} %orders_ref.3) | copy-start | bytes 64
  71.7 38.0 %all-to-all-start.2 = ((bf16[128,72,128]{2,1,0:T(8,128)(2,1)}), bf16[128,72,128]{2,1,0:T(8,128)(2,1)S(1)}, u32[]{:S(2)}, u32[]{:S(2)}) async-start(bf16[128,72,128]{2,1,0:T(8,128)(2,1)} %bitcast.8), calls=%async_computation.2 | async-start | bytes 4718592 | tf_op jit(solution)/shard_map/all_to_all | solution.py:483

commit v8 on v7

--- a/solution.py
+++ b/solution.py
@@ -16,6 +16,7 @@
 FRONT = 768
 WORDS = 8
 TILE = 3840
+LAST_TILE = 3072
 PARTS = 4
 BIG = 1 << 20
 LOW = 17
@@ -47,14 +48,14 @@
     return order, place // 2
 
 
-def column_parts(width):
-    starts = list(range(0, width - TILE // 2, TILE))
+def column_parts(width, tile):
+    starts = list(range(0, width - tile // 2, tile))
     return [(a, b - a) for a, b in zip(starts, starts[1:] + [width])]
 
 
-def state_copies(state_ref, first, body, tail, sems):
+def state_copies(state_ref, first, body, tail, sems, tile):
     copies = []
-    parts = column_parts(state_ref.shape[1])
+    parts = column_parts(state_ref.shape[1], tile)
     for k, (start, size) in enumerate(parts):
         source = state_ref.at[pl.ds(first, body.shape[0]), pl.ds(start, size)]
         target = tail if k == len(parts) - 1 else body.at[:, pl.ds(start, size)]
@@ -89,10 +90,10 @@
 ):
     levels, slot_count, slot_width, truncation, pair_count = sizes
     half = (truncation + 1) // 2
-    parts = column_parts(state_ref.shape[1])
+    parts = column_parts(state_ref.shape[1], TILE)
     bring = pltpu.make_async_copy(height_ref, height, height_sem)
     bring.start()
-    copies = state_copies(state_ref, 0, body, tail, state_sems)
+    copies = state_copies(state_ref, 0, body, tail, state_sems, TILE)
     for copy in copies:
         copy.start()
     fetch = pltpu.make_async_copy(index_ref, near, index_sem)
@@ -290,9 +291,9 @@
 ):
     levels, slot_count, slot_width, truncation, pair_count = sizes
     half = (truncation + 1) // 2
-    parts = column_parts(state_ref.shape[1])
+    parts = column_parts(state_ref.shape[1], LAST_TILE)
     head = state_ref.shape[0] - body.shape[0]
-    copies = state_copies(state_ref, head, body, tail, state_sems)
+    copies = state_copies(state_ref, head, body, tail, state_sems, LAST_TILE)
     for copy in copies:
         copy.start()
 
@@ -400,8 +401,10 @@
     slot_width = 2 * (truncation + 2)
     width = slot_count * slot_width
     rows = state.shape[0]
-    parts = column_parts(width)
+    parts = column_parts(width, TILE)
     split = parts[-1][0]
+    last_parts = column_parts(width, LAST_TILE)
+    last_split = last_parts[-1][0]
     bf16, f32 = jnp.bfloat16, jnp.float32
     vmem = pl.BlockSpec(memory_space=pltpu.VMEM)
     smem = pl.BlockSpec(memory_space=pltpu.SMEM)
@@ -495,12 +498,12 @@
         out_specs=hbm,
         out_shape=jax.ShapeDtypeStruct((rows, width), bf16),
         scratch_shapes=[
-            pltpu.VMEM((rows - head, split), bf16),
-            pltpu.VMEM((rows - head, width - split), bf16),
-            pltpu.SemaphoreType.DMA((len(parts),)),
-            pltpu.VMEM((rows, split), bf16),
-            pltpu.VMEM((rows, width - split), bf16),
-            pltpu.SemaphoreType.DMA((len(parts),)),
+            pltpu.VMEM((rows - head, last_split), bf16),
+            pltpu.VMEM((rows - head, width - last_split), bf16),
+            pltpu.SemaphoreType.DMA((len(last_parts),)),
+            pltpu.VMEM((rows, last_split), bf16),
+            pltpu.VMEM((rows, width - last_split), bf16),
+            pltpu.SemaphoreType.DMA((len(last_parts),)),
         ]
         + scratch,
         compiler_params=params(48),

time: 116 us -> 116 us (level)
  no operation moved by 1% of the time
where the time goes in v8:
time: 116 us
  waiting for transfers between devices  63.1 us (54%)
  blocking collectives  21.1 us (18%)
  Pallas kernels  18 us (16%)
  starting transfers between devices  9.41 us (8%)
  matrix products  1.97 us (2%)
    all_to_all x1, waiting for transfers between devices, shards(): lax.all_to_all(solved.reshape(devices, pair_count * ROWS, LANES), GRP_WAV...  32.8 us
    all_to_all x1, waiting for transfers between devices, shards(): lax.all_to_all(message.reshape(devices, pair_count * ROWS, LANES), GRP_WA...  30.3 us
    all_to_all x1, blocking collectives, shards(): lax.all_to_all(jnp.broadcast_to(own[None, None], (devices, 1, LANES)), GR...  21.1 us
    pallas_call x1, Pallas kernels, shards(): pl.pallas_call(functools.partial(rhs_kernel, (levels, slot_count, slot_wi...  8.15 us
    pallas_call x1, Pallas kernels, shards(): pl.pallas_call(functools.partial(final_kernel, (levels, slot_count, slot_...  6.03 us
    all_to_all x1, starting transfers between devices, shards(): lax.all_to_all(solved.reshape(devices, pair_count * ROWS, LANES), GRP_WAV...  4.89 us
    all_to_all x1, starting transfers between devices, shards(): lax.all_to_all(message.reshape(devices, pair_count * ROWS, LANES), GRP_WA...  4.52 us
    pallas_call x1, Pallas kernels, shards(): pl.pallas_call(functools.partial(solve_kernel, (levels, slot_count, chunk...  3.84 us
  transfers between devices with their start and end apart: 2, of which 2 were waited for; matrix products, arithmetic and copies ran while one was open for 3% of the time, Pallas kernels for 0%

profile of v8, /device:TPU:1, one launch (start us, length us, event | category | flops | bytes accessed | tf_op | source)
XLA Modules:
  0.0 115.6 jit_solution(5191618473188621969)
XLA Ops:
  0.0 0.0 copy-start
  0.0 0.8 pad_add_fusion
  0.8 21.1 %all_to_all.15 = s32[128,1,128]{2,1,0:T(1,128)} all-to-all(s32[128,1,128]{2,1,0:T(1,128)S(1)} %broadcast_in_dim.2), channel_id=1, replica_groups=mesh['grp'=4,'wave_0'=4,'wave_1'=4,'wave_2'=2] {'grp','wave_0','wave_1',..., dimensions={0} | all-to-all | bytes 131072 | tf_op jit(solution)/shard_map/all_to_all | solution.py:427
  22.0 8.1 %right_side.1 = bf16[384,24,128]{2,1,0:T(8,128)(2,1)} custom-call(s32[128,128]{1,0:T(8,128)} %bitcast.22, s32[5]{0:T(128)} %orders_ref.3, bf16[275,7690]{1,0:T(8,128)(2,1)} %state_ref.3, bf16[137,137]{1,0:T(8,128)(2,1)} %height_ref.1, bf16[137]{0:T(256)(128)(2,1)} %pressure_ref.1), custom_call_target="tpu_custom_call" | custom-call | tf_op jit(solution)/shard_map/right_side/pallas_call | solution.py:435
  30.2 0.0 copy-start.2
  30.2 4.5 %all-to-all-start.1 = ((bf16[128,72,128]{2,1,0:T(8,128)(2,1)}), bf16[128,72,128]{2,1,0:T(8,128)(2,1)S(1)}, u32[]{:S(2)}, u32[]{:S(2)}) async-start(bf16[128,72,128]{2,1,0:T(8,128)(2,1)} %bitcast.21), calls=%async_computation.1 | async-start | bytes 4718592 | tf_op jit(solution)/shard_map/all_to_all | solution.py:463
  34.7 0.0 copy-done
  34.7 1.8 %convolution_convert_fusion.weights_ref = bf16[3,2,240,256]{3,2,1,0:T(8,128)(2,1)S(1)} fusion(bf16[256,137,1,1]{0,1,3,2:T(8,128)(2,1)} %constant.13, bf16[240,137,1,1]{0,1,3,2:T(8,128)(2,1)} %constant.12, bf16[3,2,137,137]{3,1,2,0:T(2,128)(2,1)S(1)} %copy-done), kind=kOutput, calls=%fused_computation | convolution fusion | flops 155628000 | bytes 1098412 | tf_op jit(solution)/shard_map/jtak,bk->jtab/dot_general | solution.py:469
  36.5 0.9 reshape.23.index_ref
  37.4 30.3 %all-to-all-done.1 = bf16[128,72,128]{2,1,0:T(8,128)(2,1)S(1)} async-done(((bf16[128,72,128]{2,1,0:T(8,128)(2,1)}), bf16[128,72,128]{2,1,0:T(8,128)(2,1)S(1)}, u32[]{:S(2)}, u32[]{:S(2)}) %all-to-all-start.1) | async-done | bytes 2359328 | tf_op jit(solution)/shard_map/all_to_all | solution.py:463
  67.8 0.0 copy-done.2
  67.8 3.8 %solve.1 = bf16[128,3,24,128]{3,2,1,0:T(8,128)(2,1)} custom-call(s32[3]{0:T(128)S(1)} %copy-done.2, s32[1024]{0:T(1024)S(1)} %reshape.23.index_ref, bf16[128,3,24,128]{3,2,1,0:T(8,128)(2,1)S(1)} %bitcast.19, bf16[3,2,240,256]{3,2,1,0:T(8,128)(2,1)S(1)} %convolution_convert_fusion.weights_ref), custom_call_target="tpu_custom_call" | custom-call | tf_op jit(solution)/shard_map/solve/pallas_call | solution.py:473
  71.6 0.0 copy-start.4
  71.6 0.0 copy-start.3
  71.6 0.0 copy-start.5
  71.6 0.0 copy-start.1
  71.7 4.9 %all-to-all-start.2 = ((bf16[128,72,128]{2,1,0:T(8,128)(2,1)}), bf16[128,72,128]{2,1,0:T(8,128)(2,1)S(1)}, u32[]{:S(2)}, u32[]{:S(2)}) async-start(bf16[128,72,128]{2,1,0:T(8,128)(2,1)} %bitcast.8), calls=%async_computation.2 | async-start | bytes 4718592 | tf_op jit(solution)/shard_map/all_to_all | solution.py:486
  76.6 0.0 copy-done.4
  76.6 0.0 copy-done.3
  76.6 0.0 copy-done.5
  76.7 0.2 convolution_convert_fusion.2.weights_ref
  76.8 32.8 %all-to-all-done.2 = bf16[128,72,128]{2,1,0:T(8,128)(2,1)S(1)} async-done(((bf16[128,72,128]{2,1,0:T(8,128)(2,1)}), bf16[128,72,128]{2,1,0:T(8,128)(2,1)S(1)}, u32[]{:S(2)}, u32[]{:S(2)}) %all-to-all-start.2) | async-done | bytes 2359328 | tf_op jit(solution)/shard_map/all_to_all | solution.py:486
  109.6 0.0 copy-done.1
  109.6 6.0 %final.1 = bf16[275,7690]{1,0:T(8,128)(2,1)} custom-call(s32[1024]{0:T(1024)S(1)} %reshape.23.index_ref, s32[5]{0:T(128)S(1)} %copy-done.1, bf16[384,24,128]{2,1,0:T(8,128)(2,1)S(1)} %bitcast.20, bf16[275,7690]{1,0:T(8,128)(2,1)} %state_ref.3, bf16[275,256]{1,0:T(8,128)(2,1)S(1)} %convolution_convert_fusion.2.weights_ref), custom_call_target="tpu_custom_call" | custom-call | tf_op jit(solution)/shard_map/final/pallas_call | solution.py:495
  (6 shorter events, 0.1 us)
Async XLA Ops:
  0.0 34.7 %copy-start = (bf16[3,2,137,137]{3,1,2,0:T(2,128)(2,1)S(1)}, bf16[3,2,137,137]{3,1,2,0:T(2,128)(2,1)}, u32[]{:S(2)}) copy-start(bf16[3,2,137,137]{3,1,2,0:T(2,128)(2,1)} %param.12) | copy-start | bytes 675688
  30.2 37.6 %copy-start.2 = (s32[3]{0:T(128)S(1)}, s32[3]{0:T(128)}, u32[]{:S(2)}) copy-start(s32[3]{0:T(128)} %lows_ref.1) | copy-start | bytes 40
  30.2 37.6 %all-to-all-start.1 = ((bf16[128,72,128]{2,1,0:T(8,128)(2,1)}), bf16[128,72,128]{2,1,0:T(8,128)(2,1)S(1)}, u32[]{:S(2)}, u32[]{:S(2)}) async-start(bf16[128,72,128]{2,1,0:T(8,128)(2,1)} %bitcast.21), calls=%async_computation.1 | async-start | bytes 4718592 | tf_op jit(solution)/shard_map/all_to_all | solution.py:463
  71.6 4.9 %copy-start.4 = (bf16[137]{0:T(256)(128)(2,1)S(1)}, bf16[137]{0:T(256)(128)(2,1)}, u32[]{:S(2)}) copy-start(bf16[137]{0:T(256)(128)(2,1)} %param.16) | copy-start | bytes 826
  71.6 5.0 %copy-start.3 = (bf16[137,137]{1,0:T(8,128)(2,1)S(1)}, bf16[137,137]{1,0:T(8,128)(2,1)}, u32[]{:S(2)}) copy-start(bf16[137,137]{1,0:T(8,128)(2,1)} %param.15) | copy-start | bytes 112618
  71.6 5.0 %copy-start.5 = (bf16[256,137]{0,1:T(8,128)(2,1)S(1)}, bf16[256,137]{0,1:T(8,128)(2,1)}, u32[]{:S(2)}) copy-start(bf16[256,137]{0,1:T(8,128)(2,1)} %constant.4.clone) | copy-start | bytes 210436
  71.6 38.0 %copy-start.1 = (s32[5]{0:T(128)S(1)}, s32[5]{0:T(128)}, u32[]{:S(2)}) copy-start(s32[5]{0:T(128)} %orders_ref.3) | copy-start | bytes 64
  71.7 38.0 %all-to-all-start.2 = ((bf16[128,72,128]{2,1,0:T(8,128)(2,1)}), bf16[128,72,128]{2,1,0:T(8,128)(2,1)S(1)}, u32[]{:S(2)}, u32[]{:S(2)}) async-start(bf16[128,72,128]{2,1,0:T(8,128)(2,1)} %bitcast.8), calls=%async_computation.2 | async-start | bytes 4718592 | tf_op jit(solution)/shard_map/all_to_all | solution.py:486
